TPU v7x, 128 devices: a whole 4x4x4 slice. The times are simulated.
128 devices in a mesh: zero: 32 (over y, x, core), width: 4 (over z).
Axes of the slice: x: 4, y: 4, z: 4, core: 2. Of those that a mesh axis runs over, the one named last changes fastest.
Arguments:
- train_query: bfloat16 [3584, 4096], P('zero', 'width'), may hold values from -0.09375 to 0.09375
- low_query: bfloat16 [3584, 32], P('zero'), may hold values from -0.09375 to 0.09375
- high_query: bfloat16 [32, 4096], P(None, 'width'), may hold values from -1 to 1
- train_key: bfloat16 [3584, 2048], P('zero', 'width'), may hold values from -0.09375 to 0.09375
- low_key: bfloat16 [3584, 32], P('zero'), may hold values from -0.09375 to 0.09375
- high_key: bfloat16 [32, 2048], P(None, 'width'), may hold values from -1 to 1
- train_value: bfloat16 [3584, 2048], P('zero', 'width'), may hold values from -0.09375 to 0.09375
- low_value: bfloat16 [3584, 32], P('zero'), may hold values from -0.09375 to 0.09375
- high_value: bfloat16 [32, 2048], P(None, 'width'), may hold values from -1 to 1
- train_mixed: bfloat16 [4096, 3584], P('width', 'zero'), may hold values from -0.09375 to 0.09375
- low_mixed: bfloat16 [4096, 32], P('width'), may hold values from -0.09375 to 0.09375
- high_mixed: bfloat16 [32, 3584], P(None, 'zero'), may hold values from -1 to 1
- norm_train: float32 [3584], P(('zero', 'width')), may hold values from 0.25 to 1.75
- norm_step: float32 [3584], P(('zero', 'width')), may hold values from -0.3 to 0.3
Outputs:
- ready_query: bfloat16 [4096, 3584], P('width')
- ready_key: bfloat16 [2048, 3584], P('width')
- ready_value: bfloat16 [2048, 3584], P('width')
- ready_mixed: bfloat16 [3584, 4096], P(None, 'width')
- serve_norm: bfloat16 [3584], replicated
All inputs are finite; a program needn't handle non-finite values.
Results may differ from a plain program's by a relative error of at most 0.001.
Values may be sent and summed in bfloat16 or wider, within the bound.
No kernel may reach another device: no remote copies, remote signals or barrier semaphores. Data moves between devices by JAX's collectives and lax.ppermute only.
A program may use at most 128 MiB of HBM per device.

v0:
```python
import jax
import jax.numpy as jnp
from jax import lax
from jax.experimental import pallas as pl
from jax.experimental.pallas import tpu as pltpu
from jax.sharding import Mesh
from jax.sharding import PartitionSpec as P

ZERO = ("zero_0", "zero_1", "zero_2")
ZERO_WIDTH = ("zero_0", "zero_1", "zero_2", "width")


mix_rate = 0.5

ROWS = 112
HALF = 1536
CHUNK = 384
CHUNKS = 4
GROUP = 8 * ROWS
STRIP = 2 * ROWS
NORM = 28

ROUTE0 = (("query", 0, 1024), ("key", 0, 512))
ROUTE1 = (("value", 0, 512), ("mixed", 0, 1024))


def parts_of(route, chunk):
    low, high, at, found = chunk * CHUNK, (chunk + 1) * CHUNK, 0, []
    for name, _, width in route:
        first, last = max(low, at), min(high, at + width)
        if first < last:
            found.append((name, first - at, first - low, last - first))
        at += width
    return found


def pairs(move):
    return [
        ((y * 4 + x) * 2 + c, ((v % 4) * 4 + u % 4) * 2 + d)
        for y in range(4)
        for x in range(4)
        for c in range(2)
        for v, u, d in (move(y, x, c),)
    ]


def first_axis(step):
    return pairs(lambda y, x, c: (y, x + step, c) if c == 0 else (y + step, x, c))


def first_axis_across(step):
    return pairs(lambda y, x, c: (y, x + step, 0) if c == 1 else (y + step, x, 1))


def second_axis(step):
    return pairs(lambda y, x, c: (y + step, x, c) if c == 0 else (y, x + step, c))


PARTNER = pairs(lambda y, x, c: (y, x, 1 - c))


def send(array, to):
    return lax.ppermute(array, ZERO, to)


def place():
    return tuple(lax.axis_index(a) for a in ZERO)


def held(arrays):
    return [pltpu.with_memory_space_constraint(a, pltpu.VMEM) for a in arrays]


def vmem(n):
    return [pl.BlockSpec(memory_space=pltpu.VMEM)] * n


def anywhere(n):
    return [pl.BlockSpec(memory_space=pl.ANY)] * n


MERGED = (
    (ROWS, 1024), (32, ROWS), (32, 1024),
    (ROWS, 512), (32, ROWS), (32, 512),
    (ROWS, 512), (32, ROWS), (32, 512),
    (ROWS, 1024), (32, ROWS), (32, 1024),
    (1, NORM), (1, NORM),
)


def merge_kernel(*refs):
    ins, (keep, give), here, line, sems = refs[:14], refs[14:16], refs[16:30], refs[30], refs[31]
    _, _, c = place()
    copies = [pltpu.make_async_copy(a, b, sems.at[i]) for i, (a, b) in enumerate(zip(ins, here))]
    for copy in copies:
        copy.start()
    line[...] = jnp.zeros(line.shape, jnp.float32)
    for copy in copies:
        copy.wait()
    tq, lq, hq, tk, lk, hk, tv, lv, hv, tm, lm, hm, gain, step = here

    def latest(train, low, high):
        product = lax.dot_general(
            low[...], high[...], (((0,), (0,)), ((), ())), preferred_element_type=jnp.float32
        )
        return (train[...].astype(jnp.float32) + mix_rate * product).astype(jnp.bfloat16)

    line[0:1, 0:NORM] = gain[...] + step[...]
    rows = slice(0, ROWS)
    for to in (keep, give):
        to[ROWS : ROWS + 8, 0:128] = line[...].astype(jnp.bfloat16)

    def fill(first, second):
        first[rows, 0:1024] = latest(tq, lq, hq)
        first[rows, 1024:1536] = latest(tk, lk, hk)
        second[rows, 0:512] = latest(tv, lv, hv)
        second[rows, 512:1536] = latest(tm, lm, hm)

    @pl.when(c == 0)
    def _():
        fill(keep, give)

    @pl.when(c == 1)
    def _():
        fill(give, keep)


def merge(*args):
    piece = pltpu.VMEM((ROWS + 8, HALF), jnp.bfloat16)
    return pl.pallas_call(
        merge_kernel,
        out_shape=(piece, piece),
        in_specs=anywhere(len(args)),
        out_specs=tuple(vmem(2)),
        scratch_shapes=[pltpu.VMEM(shape, a.dtype) for shape, a in zip(MERGED, args)]
        + [pltpu.VMEM((8, 128), jnp.float32), pltpu.SemaphoreType.DMA((14,))],
        compiler_params=pltpu.CompilerParams(vmem_limit_bytes=8 * 2**20),
        name="merge",
    )(*[pltpu.with_memory_space_constraint(a, pltpu.HBM) for a in args])


OFFSETS = ((0, 0), (0, 1), (-1, 0), (1, 0), (-1, 1), (1, 1), (2, 0), (2, 1))


def stack_kernel(*refs):
    pieces, chunks, lines = refs[:8], refs[8:12], refs[12]
    y, x, c = place()
    a = jnp.where(c == 0, x, y)
    for piece, (step, other) in zip(pieces, OFFSETS):
        core = c if other == 0 else 1 - c
        at = ((a + step + 4) % 4) * 2 + core
        for j in range(CHUNKS):
            chunks[j][pl.ds(pl.multiple_of(at * ROWS, 16), ROWS), :] = piece[
                0:ROWS, j * CHUNK : (j + 1) * CHUNK
            ]
        lines[pl.ds(at, 1), :] = piece[ROWS : ROWS + 8, 0:128].astype(jnp.float32)[0:1]
    chunks[0][GROUP : GROUP + 8, 0:128] = lines[...].astype(jnp.bfloat16)


def stack(pieces):
    return pl.pallas_call(
        stack_kernel,
        out_shape=tuple(
            pltpu.VMEM((GROUP + (8 if j == 0 else 0), CHUNK), jnp.bfloat16)
            for j in range(CHUNKS)
        ),
        in_specs=vmem(8),
        out_specs=tuple(vmem(CHUNKS)),
        scratch_shapes=[pltpu.VMEM((8, 128), jnp.float32)],
        compiler_params=pltpu.CompilerParams(vmem_limit_bytes=4 * 2**20),
        name="stack",
    )(*held(pieces))


NAMES = ("query", "key", "mixed")
SHAPES = {"query": (1024, 3584), "key": (512, 3584), "mixed": (3584, 1024)}


def lay_kernel(work, n_in, *refs):
    units, refs = refs[: 2 * len(work)], refs[2 * len(work) + n_in :]
    outs, (turned, sems) = dict(zip(NAMES, refs[:3])), refs[3:]
    y, x, c = place()

    def lay(route0, route1):
        started = []

        def start(source, target):
            copy = pltpu.make_async_copy(source, target, sems.at[len(started)])
            copy.start()
            started.append(copy)

        for (step, chunk), unit in zip(work, route1):
            g = (x + step + 4) % 4
            for name, first, at, width in parts_of(ROUTE1, chunk):
                if name == "mixed":
                    for s in range(4):
                        row = pl.multiple_of(s * GROUP + g * STRIP, 16)
                        start(
                            unit.at[pl.ds(s * STRIP, STRIP), pl.ds(at, width)],
                            outs[name].at[pl.ds(row, STRIP), pl.ds(first, width)],
                        )
        for i, ((step, chunk), unit) in enumerate(zip(work, route0)):
            g = (y + step + 4) % 4
            turned[i] = unit[0:GROUP, :].T
            for name, first, at, width in parts_of(ROUTE0, chunk):
                column = pl.multiple_of(g * GROUP, 128)
                start(
                    turned.at[i, pl.ds(at, width), :],
                    outs[name].at[pl.ds(first, width), pl.ds(column, GROUP)],
                )
        for copy in started:
            copy.wait()

    half = len(work)

    @pl.when(c == 0)
    def _():
        lay(units[:half], units[half:])

    @pl.when(c == 1)
    def _():
        lay(units[half:], units[:half])


LAID = (
    ((0, 0), (0, 1), (0, 2), (0, 3)),
    ((-1, 0), (1, 0), (-1, 1), (1, 1)),
    ((2, 0), (2, 1)),
    ((-1, 2), (1, 2), (-1, 3), (1, 3)),
    ((2, 2), (2, 3)),
)


def lay(work, own, partner, before):
    n = len(work)
    n_in = 0 if before is None else 3
    shapes = tuple(jax.ShapeDtypeStruct(SHAPES[name], jnp.bfloat16) for name in NAMES)
    return pl.pallas_call(
        lambda *refs: lay_kernel(work, n_in, *refs),
        out_shape=shapes,
        in_specs=vmem(2 * n) + anywhere(n_in),
        out_specs=tuple(anywhere(3)),
        scratch_shapes=[
            pltpu.VMEM((n, CHUNK, GROUP), jnp.bfloat16),
            pltpu.SemaphoreType.DMA((6 * n,)),
        ],
        input_output_aliases={2 * n + i: i for i in range(n_in)},
        compiler_params=pltpu.CompilerParams(vmem_limit_bytes=12 * 2**20),
    )(*held(own), *held(partner), *(before or ()))


STEPS = (0, -1, 1, 2)


def value_kernel(*refs):
    units, out, whole, turned, sems = refs[:16], refs[16], refs[17], refs[18], refs[19]
    _, x, c = place()

    def gather(mine):
        for k, step in enumerate(STEPS):
            g = (x + step + 4) % 4
            for chunk in range(2):
                for name, first, at, width in parts_of(ROUTE1, chunk):
                    if name == "value":
                        for s in range(4):
                            row = pl.multiple_of(s * GROUP + g * STRIP, 16)
                            whole[pl.ds(row, STRIP), first : first + width] = mine[2 * k + chunk][
                                s * STRIP : (s + 1) * STRIP, at : at + width
                            ]

    @pl.when(c == 0)
    def _():
        gather(units[8:])

    @pl.when(c == 1)
    def _():
        gather(units[:8])

    copies = []
    for s in range(4):
        turned[s] = whole[s * GROUP : (s + 1) * GROUP, :].T
        copy = pltpu.make_async_copy(turned.at[s], out.at[:, pl.ds(s * GROUP, GROUP)], sems.at[s])
        copy.start()
        copies.append(copy)
    for copy in copies:
        copy.wait()


def value_of(own, partner):
    return pl.pallas_call(
        value_kernel,
        out_shape=jax.ShapeDtypeStruct((512, 3584), jnp.bfloat16),
        in_specs=vmem(16),
        out_specs=pl.BlockSpec(memory_space=pl.ANY),
        scratch_shapes=[
            pltpu.VMEM((3584, 512), jnp.bfloat16),
            pltpu.VMEM((4, 512, GROUP), jnp.bfloat16),
            pltpu.SemaphoreType.DMA((4,)),
        ],
        compiler_params=pltpu.CompilerParams(vmem_limit_bytes=16 * 2**20),
        name="value",
    )(*held(own), *held(partner))


def lines_kernel(*refs):
    units, out, rows = refs[:4], refs[4], refs[5]
    y, x, c = place()
    b = jnp.where(c == 0, y, x)
    for unit, step in zip(units, STEPS):
        g = (b + step + 4) % 4
        found = unit[GROUP : GROUP + 8, 0:128].astype(jnp.float32)
        for p in range(8):
            at = jnp.where(c == 0, g * 8 + p, (p // 2) * 8 + g * 2 + p % 2)
            rows[pl.ds(at, 1), :] = found[p : p + 1]
    out[...] = rows[...].astype(jnp.bfloat16)


def lines_of(units):
    return pl.pallas_call(
        lines_kernel,
        out_shape=jax.ShapeDtypeStruct((32, 128), jnp.bfloat16),
        in_specs=vmem(4),
        out_specs=pl.BlockSpec(memory_space=pltpu.VMEM),
        scratch_shapes=[pltpu.VMEM((32, 128), jnp.float32)],
        compiler_params=pltpu.CompilerParams(vmem_limit_bytes=4 * 2**20),
        name="lines",
    )(*held(units))


def norm_kernel(here, last, beyond, following, out, rows):
    z = lax.axis_index("width")
    at = lax.broadcasted_iota(jnp.int32, (128, 32), 0)
    piece = lax.broadcasted_iota(jnp.int32, (128, 32), 1)
    found = jnp.zeros((128, 128), jnp.float32)
    for step, ref in enumerate((here, last, beyond, following)):
        pick = (at == piece * 4 + (z - step + 4) % 4).astype(jnp.float32).astype(jnp.bfloat16)
        found += jnp.dot(pick, ref[...], preferred_element_type=jnp.float32)
    start = lax.broadcasted_iota(jnp.int32, (128, 128), 0) * NORM
    lane = lax.broadcasted_iota(jnp.int32, (128, 128), 1)
    column = (lane - start) & 127
    row = jnp.where(column < NORM, (start + column) >> 7, 128)
    turned = jnp.zeros((128, 128), jnp.float32)
    for k in range(NORM):
        turned = jnp.where(column == k, found[:, k : k + 1], turned)
    rows[...] = jnp.zeros(rows.shape, jnp.float32)
    for r in range(28):
        rows[r : r + 1, :] = jnp.sum(jnp.where(row == r, turned, 0.0), axis=0, keepdims=True)
    out[...] = rows[0:28, :].astype(jnp.bfloat16)


def norm_of(lines):
    return pl.pallas_call(
        norm_kernel,
        out_shape=jax.ShapeDtypeStruct((28, 128), jnp.bfloat16),
        in_specs=vmem(4),
        out_specs=pl.BlockSpec(memory_space=pltpu.VMEM),
        scratch_shapes=[pltpu.VMEM((32, 128), jnp.float32)],
        compiler_params=pltpu.CompilerParams(vmem_limit_bytes=4 * 2**20),
        name="norm",
    )(*held(lines))


def body(
    train_query,
    low_query,
    high_query,
    train_key,
    low_key,
    high_key,
    train_value,
    low_value,
    high_value,
    train_mixed,
    low_mixed,
    high_mixed,
    norm_train,
    norm_step,
):
    keep, give = merge(
        train_query,
        low_query.T,
        high_query,
        train_key,
        low_key.T,
        high_key,
        train_value,
        low_value.T,
        high_value,
        train_mixed.T,
        high_mixed,
        low_mixed.T,
        norm_train.reshape(1, NORM),
        norm_step.reshape(1, NORM),
    )
    beside = send(give, PARTNER)
    keep_up = send(keep, first_axis(1))
    give_down = send(give, first_axis_across(-1))
    keep_down = send(keep, first_axis(-1))
    give_up = send(give, first_axis_across(1))
    far_keep = send(keep_up, first_axis(1))
    far_give = send(give_down, first_axis(-1))
    group = stack((keep, beside, keep_up, keep_down, give_up, give_down, far_keep, far_give))
    mine = {
        0: group,
        -1: [send(g, second_axis(1)) for g in group],
        1: [send(g, second_axis(-1)) for g in group],
    }
    mine[2] = [
        send(mine[-1 if j % 2 == 0 else 1][j], second_axis(1 if j % 2 == 0 else -1))
        for j in range(CHUNKS)
    ]
    theirs = {s: [send(u, PARTNER) for u in mine[s]] for s in STEPS}

    outs = None
    for work in LAID:
        own, partner = [mine[s][j] for s, j in work], [theirs[s][j] for s, j in work]
        outs = lay(work, own, partner, outs)
    ready_query, ready_key, ready_mixed = outs
    ready_value = value_of(
        [mine[s][j] for s in STEPS for j in range(2)],
        [theirs[s][j] for s in STEPS for j in range(2)],
    )

    lines = lines_of([mine[s][0] for s in STEPS])
    around = [lines]
    for k in range(1, 4):
        to = [(i, (i + k) % 4) for i in range(4)]
        around.append(lax.ppermute(lines, "width", to))
    serve_norm = norm_of(around).reshape(-1)
    return (ready_query, ready_key, ready_value, ready_mixed, serve_norm)


def solution(mesh):
    torus = Mesh(
        mesh.devices.reshape(4, 4, 2, mesh.shape["width"]), ("zero_0", "zero_1", "zero_2", "width")
    )
    return jax.shard_map(
        body,
        mesh=torus,
        in_specs=(
            P(ZERO, "width"),
            P(ZERO, None),
            P(None, "width"),
            P(ZERO, "width"),
            P(ZERO, None),
            P(None, "width"),
            P(ZERO, "width"),
            P(ZERO, None),
            P(None, "width"),
            P("width", ZERO),
            P("width", None),
            P(None, ZERO),
            P(ZERO_WIDTH),
            P(ZERO_WIDTH),
        ),
        out_specs=(P("width", None), P("width", None), P("width", None), P(None, "width"), P()),
        check_vma=False,
    )
```

profile of v0, /device:TPU:1, one launch (start us, length us, event | category | flops | bytes accessed | tf_op | source)
XLA Modules:
  0.0 107.8 jit_solution(14439352729918828983)
XLA Ops:
  2.4 2.2 %collective-permute-start.1 = (bf16[120,1536]{1,0:T(8,128)(2,1)S(1)}, bf16[120,1536]{1,0:T(8,128)(2,1)S(1)}, u32[]{:S(2)}, u32[]{:S(2)}) collective-permute-start(bf16[120,1536]{1,0:T(8,128)(2,1)S(1)} %get-tuple-element.26.refs_0_), channel_id=1, source_target_pairs={{0,8},{4,36},{8,16},{12,44},{16,24},{20,52},{24,0},{28,60},{32,40}... | collective-permute-start | bytes 1105928 | tf_op jit(solution)/shard_map/ppermute | solution.py:63
  4.6 2.1 %collective-permute-start.4 = (bf16[120,1536]{1,0:T(8,128)(2,1)S(1)}, bf16[120,1536]{1,0:T(8,128)(2,1)S(1)}, u32[]{:S(2)}, u32[]{:S(2)}) collective-permute-start(bf16[120,1536]{1,0:T(8,128)(2,1)S(1)} %get-tuple-element.27), channel_id=1, source_target_pairs={{0,100},{4,24},{8,108},{12,0},{16,116},{20,8},{24,124},{28,16},{32... | collective-permute-start | bytes 1105928 | tf_op jit(solution)/shard_map/ppermute | solution.py:63
  6.7 2.8 %collective-permute-start.2 = (bf16[120,1536]{1,0:T(8,128)(2,1)S(1)}, bf16[120,1536]{1,0:T(8,128)(2,1)S(1)}, u32[]{:S(2)}, u32[]{:S(2)}) collective-permute-start(bf16[120,1536]{1,0:T(8,128)(2,1)S(1)} %get-tuple-element.26.refs_0_), channel_id=1, source_target_pairs={{0,24},{4,100},{8,0},{12,108},{16,8},{20,116},{24,16},{28,124},{32... | collective-permute-start | bytes 1105928 | tf_op jit(solution)/shard_map/ppermute | solution.py:63
  11.3 3.6 %collective-permute-done.4.refs_5_ = bf16[120,1536]{1,0:T(8,128)(2,1)S(1)} collective-permute-done((bf16[120,1536]{1,0:T(8,128)(2,1)S(1)}, bf16[120,1536]{1,0:T(8,128)(2,1)S(1)}, u32[]{:S(2)}, u32[]{:S(2)}) %collective-permute-start.4) | collective-permute-done | bytes 368672 | tf_op jit(solution)/shard_map/ppermute | solution.py:63
  16.1 4.7 %collective-permute-done.3.refs_4_ = bf16[120,1536]{1,0:T(8,128)(2,1)S(1)} collective-permute-done((bf16[120,1536]{1,0:T(8,128)(2,1)S(1)}, bf16[120,1536]{1,0:T(8,128)(2,1)S(1)}, u32[]{:S(2)}, u32[]{:S(2)}) %collective-permute-start.3) | collective-permute-done | bytes 368672 | tf_op jit(solution)/shard_map/ppermute | solution.py:63
  22.0 2.7 %collective-permute-start.21 = (bf16[896,384]{1,0:T(8,128)(2,1)S(1)}, bf16[896,384]{1,0:T(8,128)(2,1)S(1)}, u32[]{:S(2)}, u32[]{:S(2)}) collective-permute-start(bf16[896,384]{1,0:T(8,128)(2,1)S(1)} %get-tuple-element.31.refs_1_), channel_id=1, source_target_pairs={{0,96},{4,28},{8,104},{12,4},{16,112},{20,12},{24,120},{28,20},{32... | collective-permute-start | bytes 2064392 | tf_op jit(solution)/shard_map/ppermute | solution.py:63
  26.0 6.6 %collective-permute-done.21.refs_3_.refs_5_ = bf16[896,384]{1,0:T(8,128)(2,1)S(1)} collective-permute-done((bf16[896,384]{1,0:T(8,128)(2,1)S(1)}, bf16[896,384]{1,0:T(8,128)(2,1)S(1)}, u32[]{:S(2)}, u32[]{:S(2)}) %collective-permute-start.21) | collective-permute-done | bytes 688160 | tf_op jit(solution)/shard_map/ppermute | solution.py:63
  33.8 2.2 %collective-permute-done.26.refs_2_.refs_3_ = bf16[896,384]{1,0:T(8,128)(2,1)S(1)} collective-permute-done((bf16[896,384]{1,0:T(8,128)(2,1)S(1)}, bf16[896,384]{1,0:T(8,128)(2,1)S(1)}, u32[]{:S(2)}, u32[]{:S(2)}) %collective-permute-start.26) | collective-permute-done | bytes 688160 | tf_op jit(solution)/shard_map/ppermute | solution.py:63
  37.5 2.6 %collective-permute-start.25 = (bf16[904,384]{1,0:T(8,128)(2,1)S(1)}, bf16[904,384]{1,0:T(8,128)(2,1)S(1)}, u32[]{:S(2)}, u32[]{:S(2)}) collective-permute-start(bf16[904,384]{1,0:T(8,128)(2,1)S(1)} %get-tuple-element.30.refs_0_), channel_id=1, source_target_pairs={{0,96},{4,28},{8,104},{12,4},{16,112},{20,12},{24,120},{28,20},{32... | collective-permute-start | bytes 2082824 | tf_op jit(solution)/shard_map/ppermute | solution.py:63
  40.1 4.5 %collective-permute-done.7.refs_0_ = bf16[896,384]{1,0:T(8,128)(2,1)S(1)} collective-permute-done((bf16[896,384]{1,0:T(8,128)(2,1)S(1)}, bf16[896,384]{1,0:T(8,128)(2,1)S(1)}, u32[]{:S(2)}, u32[]{:S(2)}) %collective-permute-start.7) | collective-permute-done | bytes 688160 | tf_op jit(solution)/shard_map/ppermute | solution.py:63
  44.6 1.9 %collective-permute-start.31 = (bf16[904,384]{1,0:T(8,128)(2,1)S(1)}, bf16[904,384]{1,0:T(8,128)(2,1)S(1)}, u32[]{:S(2)}, u32[]{:S(2)}) collective-permute-start(bf16[904,384]{1,0:T(8,128)(2,1)S(1)} %get-tuple-element.30.refs_0_), channel_id=1, source_target_pairs={{0,4},{4,0},{8,12},{12,8},{16,20},{20,16},{24,28},{28,24},{32,36},... | collective-permute-start | bytes 2082824 | tf_op jit(solution)/shard_map/ppermute | solution.py:63
  48.3 5.1 %collective-permute-done.13.refs_1_ = bf16[896,384]{1,0:T(8,128)(2,1)S(1)} collective-permute-done((bf16[896,384]{1,0:T(8,128)(2,1)S(1)}, bf16[896,384]{1,0:T(8,128)(2,1)S(1)}, u32[]{:S(2)}, u32[]{:S(2)}) %collective-permute-start.13) | collective-permute-done | bytes 688160 | tf_op jit(solution)/shard_map/ppermute | solution.py:63
  54.7 4.8 %collective-permute-done.14.refs_2_ = bf16[896,384]{1,0:T(8,128)(2,1)S(1)} collective-permute-done((bf16[896,384]{1,0:T(8,128)(2,1)S(1)}, bf16[896,384]{1,0:T(8,128)(2,1)S(1)}, u32[]{:S(2)}, u32[]{:S(2)}) %collective-permute-start.14) | collective-permute-done | bytes 688160 | tf_op jit(solution)/shard_map/ppermute | solution.py:63
  59.4 1.9 %collective-permute-start.30 = (bf16[896,384]{1,0:T(8,128)(2,1)S(1)}, bf16[896,384]{1,0:T(8,128)(2,1)S(1)}, u32[]{:S(2)}, u32[]{:S(2)}) collective-permute-start(bf16[896,384]{1,0:T(8,128)(2,1)S(1)} %collective-permute-done.21.refs_3_.refs_5_), channel_id=1, source_target_pairs={{0,4},{4,0},{8,12},{12,8},{16,20},{20,16},{24,28},{28,24},{32,36},... | collective-permute-start | bytes 2064392 | tf_op jit(solution)/shard_map/ppermute | solution.py:63
  63.4 4.9 %collective-permute-done.22.refs_1_.refs_7_ = bf16[896,384]{1,0:T(8,128)(2,1)S(1)} collective-permute-done((bf16[896,384]{1,0:T(8,128)(2,1)S(1)}, bf16[896,384]{1,0:T(8,128)(2,1)S(1)}, u32[]{:S(2)}, u32[]{:S(2)}) %collective-permute-start.22) | collective-permute-done | bytes 688160 | tf_op jit(solution)/shard_map/ppermute | solution.py:63
  68.3 2.5 %collective-permute-start.27 = (bf16[904,384]{1,0:T(8,128)(2,1)S(1)}, bf16[904,384]{1,0:T(8,128)(2,1)S(1)}, u32[]{:S(2)}, u32[]{:S(2)}) collective-permute-start(bf16[904,384]{1,0:T(8,128)(2,1)S(1)} %collective-permute-done.19.refs_0_.refs_2_.refs_1_), channel_id=1, source_target_pairs={{0,4},{4,0},{8,12},{12,8},{16,20},{20,16},{24,28},{28,24},{32,36},... | collective-permute-start | bytes 2082824 | tf_op jit(solution)/shard_map/ppermute | solution.py:63
  70.9 3.4 %collective-permute-start.10 = (bf16[896,384]{1,0:T(8,128)(2,1)S(1)}, bf16[896,384]{1,0:T(8,128)(2,1)S(1)}, u32[]{:S(2)}, u32[]{:S(2)}) collective-permute-start(bf16[896,384]{1,0:T(8,128)(2,1)S(1)} %collective-permute-done.9.refs_3_), channel_id=1, source_target_pairs={{0,96},{4,28},{8,104},{12,4},{16,112},{20,12},{24,120},{28,20},{32... | collective-permute-start | bytes 2064392 | tf_op jit(solution)/shard_map/ppermute | solution.py:63
  75.6 5.3 %collective-permute-done.8.refs_0_ = bf16[896,384]{1,0:T(8,128)(2,1)S(1)} collective-permute-done((bf16[896,384]{1,0:T(8,128)(2,1)S(1)}, bf16[896,384]{1,0:T(8,128)(2,1)S(1)}, u32[]{:S(2)}, u32[]{:S(2)}) %collective-permute-start.8) | collective-permute-done | bytes 688160 | tf_op jit(solution)/shard_map/ppermute | solution.py:63
  80.9 2.1 %collective-permute-start.24 = (bf16[896,384]{1,0:T(8,128)(2,1)S(1)}, bf16[896,384]{1,0:T(8,128)(2,1)S(1)}, u32[]{:S(2)}, u32[]{:S(2)}) collective-permute-start(bf16[896,384]{1,0:T(8,128)(2,1)S(1)} %collective-permute-done.22.refs_1_.refs_7_), channel_id=1, source_target_pairs={{0,4},{4,0},{8,12},{12,8},{16,20},{20,16},{24,28},{28,24},{32,36},... | collective-permute-start | bytes 2064392 | tf_op jit(solution)/shard_map/ppermute | solution.py:63
  84.7 3.3 %collective-permute-start.36 = (bf16[32,128]{1,0:T(8,128)(2,1)S(1)}, bf16[32,128]{1,0:T(8,128)(2,1)S(1)}, u32[]{:S(2)}, u32[]{:S(2)}) collective-permute-start(bf16[32,128]{1,0:T(8,128)(2,1)S(1)} %lines.1.here), channel_id=1, source_target_pairs={{0,2},{1,3},{2,0},{3,1},{4,6},{5,7},{6,4},{7,5},{8,10},{9,11},{10,... | collective-permute-start | bytes 24584 | tf_op jit(solution)/shard_map/ppermute | solution.py:428
  92.8 2.4 %shard_map.173 = (bf16[1024,3584]{1,0:T(8,128)(2,1)}, bf16[512,3584]{1,0:T(8,128)(2,1)}, bf16[3584,1024]{1,0:T(8,128)(2,1)}) custom-call(bf16[904,384]{1,0:T(8,128)(2,1)S(1)} %get-tuple-element.30.refs_0_, bf16[896,384]{1,0:T(8,128)(2,1)S(1)} %get-tuple-element.31.refs_1_, bf16[896,384]{1,0:T(8,128)(2,1)S(1)} %get-tuple-element.28.refs_2_, ...), custom_call_target="tpu_custom_call" | custom-call | tf_op jit(solution)/shard_map/pallas_call | solution.py:238
  95.2 2.1 %shard_map.174 = (bf16[1024,3584]{1,0:T(8,128)(2,1)}, bf16[512,3584]{1,0:T(8,128)(2,1)}, bf16[3584,1024]{1,0:T(8,128)(2,1)}) custom-call(bf16[904,384]{1,0:T(8,128)(2,1)S(1)} %collective-permute-done.19.refs_0_.refs_2_.refs_1_, ...), custom_call_target="tpu_custom_call", output_to_operand_aliasing={{0}: (8, {}), {1}: (9, {}), {2}: (10, {})} | custom-call | tf_op jit(solution)/shard_map/pallas_call | solution.py:238
  98.9 2.6 %value.1 = bf16[512,3584]{1,0:T(8,128)(2,1)} custom-call(bf16[904,384]{1,0:T(8,128)(2,1)S(1)} %get-tuple-element.30.refs_0_, bf16[896,384]{1,0:T(8,128)(2,1)S(1)} %get-tuple-element.31.refs_1_, bf16[904,384]{1,0:T(8,128)(2,1)S(1)} %collective-permute-done.19.refs_0_.refs_2_.refs_1_, bf16[896,384]{1,0:T(8,128)(2,1)S(1)} %collective-permute-done.26.refs_2_.refs_3_, ...), custom_call_target="tpu_custom_call" | custom-call | tf_op jit(solution)/shard_map/value/pallas_call | solution.py:290
  103.0 2.7 %shard_map.176 = (bf16[1024,3584]{1,0:T(8,128)(2,1)}, bf16[512,3584]{1,0:T(8,128)(2,1)}, bf16[3584,1024]{1,0:T(8,128)(2,1)}) custom-call(bf16[896,384]{1,0:T(8,128)(2,1)S(1)} %collective-permute-done.7.refs_0_, bf16[896,384]{1,0:T(8,128)(2,1)S(1)} %collective-permute-done.13.refs_1_, ...), custom_call_target="tpu_custom_call", output_to_operand_aliasing={{0}: (8, {}), {1}: (9, {}), {2}: (10, {})} | custom-call | tf_op jit(solution)/shard_map/pallas_call | solution.py:238
  (62 shorter events, 27.7 us)
Async XLA Ops:
  9.6 11.3 %collective-permute-start.3 = (bf16[120,1536]{1,0:T(8,128)(2,1)S(1)}, bf16[120,1536]{1,0:T(8,128)(2,1)S(1)}, u32[]{:S(2)}, u32[]{:S(2)}) collective-permute-start(bf16[120,1536]{1,0:T(8,128)(2,1)S(1)} %get-tuple-element.27), channel_id=1, source_target_pairs={{0,36},{4,8},{8,44},{12,16},{16,52},{20,24},{24,60},{28,0},{32,68}... | collective-permute-start | bytes 1105928 | tf_op jit(solution)/shard_map/ppermute | solution.py:63
  24.7 11.3 %collective-permute-start.26 = (bf16[896,384]{1,0:T(8,128)(2,1)S(1)}, bf16[896,384]{1,0:T(8,128)(2,1)S(1)}, u32[]{:S(2)}, u32[]{:S(2)}) collective-permute-start(bf16[896,384]{1,0:T(8,128)(2,1)S(1)} %get-tuple-element.31.refs_1_), channel_id=1, source_target_pairs={{0,32},{4,12},{8,40},{12,20},{16,48},{20,28},{24,56},{28,4},{32,64... | collective-permute-start | bytes 2064392 | tf_op jit(solution)/shard_map/ppermute | solution.py:63
  24.7 11.3 %collective-permute-start.32 = (bf16[896,384]{1,0:T(8,128)(2,1)S(1)}, bf16[896,384]{1,0:T(8,128)(2,1)S(1)}, u32[]{:S(2)}, u32[]{:S(2)}) collective-permute-start(bf16[896,384]{1,0:T(8,128)(2,1)S(1)} %get-tuple-element.31.refs_1_), channel_id=1, source_target_pairs={{0,4},{4,0},{8,12},{12,8},{16,20},{20,16},{24,28},{28,24},{32,36},... | collective-permute-start | bytes 2064392 | tf_op jit(solution)/shard_map/ppermute | solution.py:63
  25.5 12.0 %collective-permute-start.33 = (bf16[896,384]{1,0:T(8,128)(2,1)S(1)}, bf16[896,384]{1,0:T(8,128)(2,1)S(1)}, u32[]{:S(2)}, u32[]{:S(2)}) collective-permute-start(bf16[896,384]{1,0:T(8,128)(2,1)S(1)} %get-tuple-element.28.refs_2_), channel_id=1, source_target_pairs={{0,4},{4,0},{8,12},{12,8},{16,20},{20,16},{24,28},{28,24},{32,36},... | collective-permute-start | bytes 2064392 | tf_op jit(solution)/shard_map/ppermute | solution.py:63
  25.5 12.0 %collective-permute-start.34 = (bf16[896,384]{1,0:T(8,128)(2,1)S(1)}, bf16[896,384]{1,0:T(8,128)(2,1)S(1)}, u32[]{:S(2)}, u32[]{:S(2)}) collective-permute-start(bf16[896,384]{1,0:T(8,128)(2,1)S(1)} %get-tuple-element.29.refs_3_), channel_id=1, source_target_pairs={{0,4},{4,0},{8,12},{12,8},{16,20},{20,16},{24,28},{28,24},{32,36},... | collective-permute-start | bytes 2064392 | tf_op jit(solution)/shard_map/ppermute | solution.py:63
  32.6 12.0 %collective-permute-start.7 = (bf16[896,384]{1,0:T(8,128)(2,1)S(1)}, bf16[896,384]{1,0:T(8,128)(2,1)S(1)}, u32[]{:S(2)}, u32[]{:S(2)}) collective-permute-start(bf16[896,384]{1,0:T(8,128)(2,1)S(1)} %get-tuple-element.28.refs_2_), channel_id=1, source_target_pairs={{0,32},{4,12},{8,40},{12,20},{16,48},{20,28},{24,56},{28,4},{32,64... | collective-permute-start | bytes 2064392 | tf_op jit(solution)/shard_map/ppermute | solution.py:63
  36.0 17.4 %collective-permute-start.13 = (bf16[896,384]{1,0:T(8,128)(2,1)S(1)}, bf16[896,384]{1,0:T(8,128)(2,1)S(1)}, u32[]{:S(2)}, u32[]{:S(2)}) collective-permute-start(bf16[896,384]{1,0:T(8,128)(2,1)S(1)} %get-tuple-element.28.refs_2_), channel_id=1, source_target_pairs={{0,96},{4,28},{8,104},{12,4},{16,112},{20,12},{24,120},{28,20},{32... | collective-permute-start | bytes 2064392 | tf_op jit(solution)/shard_map/ppermute | solution.py:63
  37.5 23.9 %collective-permute-start.19 = (bf16[904,384]{1,0:T(8,128)(2,1)S(1)}, bf16[904,384]{1,0:T(8,128)(2,1)S(1)}, u32[]{:S(2)}, u32[]{:S(2)}) collective-permute-start(bf16[904,384]{1,0:T(8,128)(2,1)S(1)} %get-tuple-element.30.refs_0_), channel_id=1, source_target_pairs={{0,32},{4,12},{8,40},{12,20},{16,48},{20,28},{24,56},{28,4},{32,64... | collective-permute-start | bytes 2082824 | tf_op jit(solution)/shard_map/ppermute | solution.py:63
  37.5 23.8 %collective-permute-start.25 = (bf16[904,384]{1,0:T(8,128)(2,1)S(1)}, bf16[904,384]{1,0:T(8,128)(2,1)S(1)}, u32[]{:S(2)}, u32[]{:S(2)}) collective-permute-start(bf16[904,384]{1,0:T(8,128)(2,1)S(1)} %get-tuple-element.30.refs_0_), channel_id=1, source_target_pairs={{0,96},{4,28},{8,104},{12,4},{16,112},{20,12},{24,120},{28,20},{32... | collective-permute-start | bytes 2082824 | tf_op jit(solution)/shard_map/ppermute | solution.py:63
  44.6 18.6 %collective-permute-start.31 = (bf16[904,384]{1,0:T(8,128)(2,1)S(1)}, bf16[904,384]{1,0:T(8,128)(2,1)S(1)}, u32[]{:S(2)}, u32[]{:S(2)}) collective-permute-start(bf16[904,384]{1,0:T(8,128)(2,1)S(1)} %get-tuple-element.30.refs_0_), channel_id=1, source_target_pairs={{0,4},{4,0},{8,12},{12,8},{16,20},{20,16},{24,28},{28,24},{32,36},... | collective-permute-start | bytes 2082824 | tf_op jit(solution)/shard_map/ppermute | solution.py:63
  46.5 12.9 %collective-permute-start.14 = (bf16[896,384]{1,0:T(8,128)(2,1)S(1)}, bf16[896,384]{1,0:T(8,128)(2,1)S(1)}, u32[]{:S(2)}, u32[]{:S(2)}) collective-permute-start(bf16[896,384]{1,0:T(8,128)(2,1)S(1)} %get-tuple-element.29.refs_3_), channel_id=1, source_target_pairs={{0,32},{4,12},{8,40},{12,20},{16,48},{20,28},{24,56},{28,4},{32,64... | collective-permute-start | bytes 2064392 | tf_op jit(solution)/shard_map/ppermute | solution.py:63
  53.4 14.8 %collective-permute-start.22 = (bf16[896,384]{1,0:T(8,128)(2,1)S(1)}, bf16[896,384]{1,0:T(8,128)(2,1)S(1)}, u32[]{:S(2)}, u32[]{:S(2)}) collective-permute-start(bf16[896,384]{1,0:T(8,128)(2,1)S(1)} %collective-permute-done.21.refs_3_.refs_5_), channel_id=1, source_target_pairs={{0,96},{4,28},{8,104},{12,4},{16,112},{20,12},{24,120},{28,20},{32... | collective-permute-start | bytes 2064392 | tf_op jit(solution)/shard_map/ppermute | solution.py:63
  61.4 12.9 %collective-permute-start.20 = (bf16[904,384]{1,0:T(8,128)(2,1)S(1)}, bf16[904,384]{1,0:T(8,128)(2,1)S(1)}, u32[]{:S(2)}, u32[]{:S(2)}) collective-permute-start(bf16[904,384]{1,0:T(8,128)(2,1)S(1)} %collective-permute-done.19.refs_0_.refs_2_.refs_1_), channel_id=1, source_target_pairs={{0,32},{4,12},{8,40},{12,20},{16,48},{20,28},{24,56},{28,4},{32,64... | collective-permute-start | bytes 2082824 | tf_op jit(solution)/shard_map/ppermute | solution.py:63
  68.2 12.7 %collective-permute-start.8 = (bf16[896,384]{1,0:T(8,128)(2,1)S(1)}, bf16[896,384]{1,0:T(8,128)(2,1)S(1)}, u32[]{:S(2)}, u32[]{:S(2)}) collective-permute-start(bf16[896,384]{1,0:T(8,128)(2,1)S(1)} %collective-permute-done.7.refs_0_), channel_id=1, source_target_pairs={{0,32},{4,12},{8,40},{12,20},{16,48},{20,28},{24,56},{28,4},{32,64... | collective-permute-start | bytes 2064392 | tf_op jit(solution)/shard_map/ppermute | solution.py:63
  68.3 16.5 %collective-permute-start.27 = (bf16[904,384]{1,0:T(8,128)(2,1)S(1)}, bf16[904,384]{1,0:T(8,128)(2,1)S(1)}, u32[]{:S(2)}, u32[]{:S(2)}) collective-permute-start(bf16[904,384]{1,0:T(8,128)(2,1)S(1)} %collective-permute-done.19.refs_0_.refs_2_.refs_1_), channel_id=1, source_target_pairs={{0,4},{4,0},{8,12},{12,8},{16,20},{20,16},{24,28},{28,24},{32,36},... | collective-permute-start | bytes 2082824 | tf_op jit(solution)/shard_map/ppermute | solution.py:63
  70.8 17.3 %collective-permute-start.28 = (bf16[904,384]{1,0:T(8,128)(2,1)S(1)}, bf16[904,384]{1,0:T(8,128)(2,1)S(1)}, u32[]{:S(2)}, u32[]{:S(2)}) collective-permute-start(bf16[904,384]{1,0:T(8,128)(2,1)S(1)} %collective-permute-done.25.refs_1_.refs_4_.refs_2_), channel_id=1, source_target_pairs={{0,4},{4,0},{8,12},{12,8},{16,20},{20,16},{24,28},{28,24},{32,36},... | collective-permute-start | bytes 2082824 | tf_op jit(solution)/shard_map/ppermute | solution.py:63
  70.9 12.1 %collective-permute-start.10 = (bf16[896,384]{1,0:T(8,128)(2,1)S(1)}, bf16[896,384]{1,0:T(8,128)(2,1)S(1)}, u32[]{:S(2)}, u32[]{:S(2)}) collective-permute-start(bf16[896,384]{1,0:T(8,128)(2,1)S(1)} %collective-permute-done.9.refs_3_), channel_id=1, source_target_pairs={{0,96},{4,28},{8,104},{12,4},{16,112},{20,12},{24,120},{28,20},{32... | collective-permute-start | bytes 2064392 | tf_op jit(solution)/shard_map/ppermute | solution.py:63
  74.3 18.0 %collective-permute-start.23 = (bf16[904,384]{1,0:T(8,128)(2,1)S(1)}, bf16[904,384]{1,0:T(8,128)(2,1)S(1)}, u32[]{:S(2)}, u32[]{:S(2)}) collective-permute-start(bf16[904,384]{1,0:T(8,128)(2,1)S(1)} %collective-permute-done.20.refs_0_.refs_6_.refs_3_), channel_id=1, source_target_pairs={{0,4},{4,0},{8,12},{12,8},{16,20},{20,16},{24,28},{28,24},{32,36},... | collective-permute-start | bytes 2082824 | tf_op jit(solution)/shard_map/ppermute | solution.py:63
  80.9 11.4 %collective-permute-start.24 = (bf16[896,384]{1,0:T(8,128)(2,1)S(1)}, bf16[896,384]{1,0:T(8,128)(2,1)S(1)}, u32[]{:S(2)}, u32[]{:S(2)}) collective-permute-start(bf16[896,384]{1,0:T(8,128)(2,1)S(1)} %collective-permute-done.22.refs_1_.refs_7_), channel_id=1, source_target_pairs={{0,4},{4,0},{8,12},{12,8},{16,20},{20,16},{24,28},{28,24},{32,36},... | collective-permute-start | bytes 2064392 | tf_op jit(solution)/shard_map/ppermute | solution.py:63
  88.8 14.3 %collective-permute-start.18 = (bf16[896,384]{1,0:T(8,128)(2,1)S(1)}, bf16[896,384]{1,0:T(8,128)(2,1)S(1)}, u32[]{:S(2)}, u32[]{:S(2)}) collective-permute-start(bf16[896,384]{1,0:T(8,128)(2,1)S(1)} %collective-permute-done.9.refs_3_), channel_id=1, source_target_pairs={{0,4},{4,0},{8,12},{12,8},{16,20},{20,16},{24,28},{28,24},{32,36},... | collective-permute-start | bytes 2064392 | tf_op jit(solution)/shard_map/ppermute | solution.py:63
  89.6 13.4 %collective-permute-start.16 = (bf16[896,384]{1,0:T(8,128)(2,1)S(1)}, bf16[896,384]{1,0:T(8,128)(2,1)S(1)}, u32[]{:S(2)}, u32[]{:S(2)}) collective-permute-start(bf16[896,384]{1,0:T(8,128)(2,1)S(1)} %collective-permute-done.13.refs_1_), channel_id=1, source_target_pairs={{0,4},{4,0},{8,12},{12,8},{16,20},{20,16},{24,28},{28,24},{32,36},... | collective-permute-start | bytes 2064392 | tf_op jit(solution)/shard_map/ppermute | solution.py:63
  90.5 12.5 %collective-permute-start.17 = (bf16[896,384]{1,0:T(8,128)(2,1)S(1)}, bf16[896,384]{1,0:T(8,128)(2,1)S(1)}, u32[]{:S(2)}, u32[]{:S(2)}) collective-permute-start(bf16[896,384]{1,0:T(8,128)(2,1)S(1)} %collective-permute-done.14.refs_2_), channel_id=1, source_target_pairs={{0,4},{4,0},{8,12},{12,8},{16,20},{20,16},{24,28},{28,24},{32,36},... | collective-permute-start | bytes 2064392 | tf_op jit(solution)/shard_map/ppermute | solution.py:63
  92.3 13.5 %collective-permute-start.11 = (bf16[896,384]{1,0:T(8,128)(2,1)S(1)}, bf16[896,384]{1,0:T(8,128)(2,1)S(1)}, u32[]{:S(2)}, u32[]{:S(2)}) collective-permute-start(bf16[896,384]{1,0:T(8,128)(2,1)S(1)} %collective-permute-done.8.refs_0_), channel_id=1, source_target_pairs={{0,4},{4,0},{8,12},{12,8},{16,20},{20,16},{24,28},{28,24},{32,36},... | collective-permute-start | bytes 2064392 | tf_op jit(solution)/shard_map/ppermute | solution.py:63
  92.3 13.5 %collective-permute-start.12 = (bf16[896,384]{1,0:T(8,128)(2,1)S(1)}, bf16[896,384]{1,0:T(8,128)(2,1)S(1)}, u32[]{:S(2)}, u32[]{:S(2)}) collective-permute-start(bf16[896,384]{1,0:T(8,128)(2,1)S(1)} %collective-permute-done.10.refs_1_), channel_id=1, source_target_pairs={{0,4},{4,0},{8,12},{12,8},{16,20},{20,16},{24,28},{28,24},{32,36},... | collective-permute-start | bytes 2064392 | tf_op jit(solution)/shard_map/ppermute | solution.py:63
  (14 other events, 114.9 us)
where the time goes:
time: 109 us; the launch traced here: 108 us
  starting transfers between devices  45.2 us (41%)
  waiting for transfers between devices  44.8 us (41%)
  Pallas kernels  16.8 us (15%)
    ppermute x35, waiting for transfers between devices, send(): return lax.ppermute(array, ZERO, to)  44.5 us
    ppermute x35, starting transfers between devices, send(): return lax.ppermute(array, ZERO, to)  39.5 us
    pallas_call x5, Pallas kernels, lay(): pl.pallas_call(lambda *refs: lay_kernel(work, n_in, *refs), out_shape=sha...  10.6 us
    ppermute x3, starting transfers between devices, body(): around.append(lax.ppermute(lines, 'width', to))  5.74 us
    pallas_call x1, Pallas kernels, value_of(): pl.pallas_call(value_kernel, out_shape=jax.ShapeDtypeStruct((512, 3584),...  2.55 us
  transfers between devices with their start and end apart: 38, of which 13 were waited for; matrix products, arithmetic and copies ran while one was open for 0% of the time, Pallas kernels for 12%

commit v1 on v0

v1 whole, which is shorter than its diff:
```python
import jax
import jax.numpy as jnp
from jax import lax
from jax.experimental import pallas as pl
from jax.experimental.pallas import tpu as pltpu
from jax.sharding import Mesh
from jax.sharding import PartitionSpec as P

ZERO = ("zero_0", "zero_1", "zero_2")
ZERO_WIDTH = ("zero_0", "zero_1", "zero_2", "width")


mix_rate = 0.5

ROWS = 112
HALF = 1536
WIDTHS = (512, 768, 256)
FIRSTS = (0, 512, 1280)
CHUNKS = 3
GROUP = 8 * ROWS
STRIP = 2 * ROWS
REST = 3 * STRIP
NORM = 28

ROUTE0 = (
    (("query", 0, 0, 512),),
    (("query", 512, 0, 512), ("key", 0, 512, 256)),
    (("key", 256, 0, 256),),
)
ROUTE1 = ((("value", 0, 0, 512),), (("mixed", 0, 0, 768),), (("mixed", 768, 0, 256),))


def columns(j):
    return slice(FIRSTS[j], FIRSTS[j] + WIDTHS[j])


def pairs(move):
    return [
        ((y * 4 + x) * 2 + c, ((v % 4) * 4 + u % 4) * 2 + d)
        for y in range(4)
        for x in range(4)
        for c in range(2)
        for v, u, d in (move(y, x, c),)
    ]


def first_axis(step):
    return pairs(lambda y, x, c: (y, x + step, c) if c == 0 else (y + step, x, c))


def first_axis_across(step):
    return pairs(lambda y, x, c: (y, x + step, 0) if c == 1 else (y + step, x, 1))


def second_axis(step):
    return pairs(lambda y, x, c: (y + step, x, c) if c == 0 else (y, x + step, c))


PARTNER = pairs(lambda y, x, c: (y, x, 1 - c))


def send(array, to):
    return lax.ppermute(array, ZERO, to)


def place():
    return tuple(lax.axis_index(a) for a in ZERO)


def held(arrays):
    return [pltpu.with_memory_space_constraint(a, pltpu.VMEM) for a in arrays]


def vmem(n):
    return [pl.BlockSpec(memory_space=pltpu.VMEM)] * n


def anywhere(n):
    return [pl.BlockSpec(memory_space=pl.ANY)] * n


MERGED = (
    (ROWS, 1024), (32, ROWS), (32, 1024),
    (ROWS, 512), (32, ROWS), (32, 512),
    (ROWS, 512), (32, ROWS), (32, 512),
    (ROWS, 1024), (32, ROWS), (32, 1024),
    (1, NORM), (1, NORM),
)


def merge_kernel(*refs):
    ins, (keep, give, norm), here, (line, sems) = refs[:14], refs[14:17], refs[17:31], refs[31:]
    y, x, c = place()
    copies = [pltpu.make_async_copy(a, b, sems.at[i]) for i, (a, b) in enumerate(zip(ins, here))]
    for copy in copies:
        copy.start()
    line[...] = jnp.zeros(line.shape, jnp.float32)
    for copy in copies:
        copy.wait()
    tq, lq, hq, tk, lk, hk, tv, lv, hv, tm, lm, hm, gain, step = here

    def latest(train, low, high):
        product = lax.dot_general(
            low[...], high[...], (((0,), (0,)), ((), ())), preferred_element_type=jnp.float32
        )
        return (train[...].astype(jnp.float32) + mix_rate * product).astype(jnp.bfloat16)

    first = ((((y * 4 + x) * 2 + c) * 4) + lax.axis_index("width")) * NORM
    row, at = first // 128, first % 128
    lane = lax.broadcasted_iota(jnp.int32, (1, 128), 1)
    line[0:1, 0:NORM] = gain[...] + step[...]
    turned = pltpu.roll(line[0:1, :], at, 1)
    line[0:1, :] = jnp.zeros((1, 128), jnp.float32)
    line[pl.ds(row, 1), :] = jnp.where(lane >= at, turned, 0.0)
    line[pl.ds(row + 1, 1), :] = jnp.where(lane < at, turned, line[pl.ds(row + 1, 1), :])
    norm[...] = line[...].astype(jnp.bfloat16)

    rows = slice(0, ROWS)

    def fill(first, second):
        first[rows, 0:1024] = latest(tq, lq, hq)
        first[rows, 1024:1536] = latest(tk, lk, hk)
        second[rows, 0:512] = latest(tv, lv, hv)
        second[rows, 512:1536] = latest(tm, lm, hm)

    @pl.when(c == 0)
    def _():
        fill(keep, give)

    @pl.when(c == 1)
    def _():
        fill(give, keep)


def merge(*args):
    piece = pltpu.VMEM((ROWS, HALF), jnp.bfloat16)
    return pl.pallas_call(
        merge_kernel,
        out_shape=(piece, piece, pltpu.VMEM((32, 128), jnp.bfloat16)),
        in_specs=anywhere(len(args)),
        out_specs=tuple(vmem(3)),
        scratch_shapes=[pltpu.VMEM(shape, a.dtype) for shape, a in zip(MERGED, args)]
        + [pltpu.VMEM((32, 128), jnp.float32), pltpu.SemaphoreType.DMA((14,))],
        compiler_params=pltpu.CompilerParams(vmem_limit_bytes=8 * 2**20),
        name="merge",
    )(*[pltpu.with_memory_space_constraint(a, pltpu.HBM) for a in args])


def pair_kernel(keep, beside, out):
    _, _, c = place()
    for piece, core in ((keep, c), (beside, 1 - c)):
        out[pl.ds(pl.multiple_of(core * ROWS, 16), ROWS), :] = piece[...]


def pair_of(keep, beside):
    return pl.pallas_call(
        pair_kernel,
        out_shape=pltpu.VMEM((STRIP, HALF), jnp.bfloat16),
        in_specs=vmem(2),
        out_specs=pl.BlockSpec(memory_space=pltpu.VMEM),
        compiler_params=pltpu.CompilerParams(vmem_limit_bytes=2 * 2**20),
        name="pair",
    )(*held((keep, beside)))


OFFSETS = ((3, 0), (1, 0), (3, 1), (1, 1), (2, 0), (2, 1))


def stack_kernel(*refs):
    pieces, chunks = refs[:6], refs[6:]
    _, _, c = place()
    for piece, (step, other) in zip(pieces, OFFSETS):
        core = c if other == 0 else 1 - c
        at = pl.multiple_of(((step - 1) * 2 + core) * ROWS, 16)
        for j in range(CHUNKS):
            chunks[j][pl.ds(at, ROWS), :] = piece[:, columns(j)]


def stack(pieces):
    return pl.pallas_call(
        stack_kernel,
        out_shape=tuple(pltpu.VMEM((REST, width), jnp.bfloat16) for width in WIDTHS),
        in_specs=vmem(6),
        out_specs=tuple(vmem(CHUNKS)),
        compiler_params=pltpu.CompilerParams(vmem_limit_bytes=4 * 2**20),
        name="stack",
    )(*held(pieces))


NAMES = ("query", "key", "mixed")
SHAPES = {"query": (1024, 3584), "key": (512, 3584), "mixed": (3584, 1024)}


def lay_kernel(work, n_in, *refs):
    units, refs = refs[: 4 * len(work)], refs[4 * len(work) + n_in :]
    outs, scratch, sems = dict(zip(NAMES, refs[:3])), refs[3:-1], refs[-1]
    y, x, c = place()

    def lay(route0, route1):
        started = []

        def start(source, target):
            copy = pltpu.make_async_copy(source, target, sems.at[len(started)])
            copy.start()
            started.append(copy)

        for (step, j), (pair, rest) in zip(work, route1):
            for name, first, at, width in ROUTE1[j]:
                if name != "mixed":
                    continue
                g = (x + step + 4) % 4
                for k in range(4):
                    row = pl.multiple_of(((y + k) % 4) * GROUP + g * STRIP, 16)
                    source = (
                        pair.at[:, pl.ds(FIRSTS[j] + at, width)]
                        if k == 0
                        else rest.at[pl.ds((k - 1) * STRIP, STRIP), pl.ds(at, width)]
                    )
                    start(source, outs[name].at[pl.ds(row, STRIP), pl.ds(first, width)])
        for i, ((step, j), (pair, rest)) in enumerate(zip(work, route0)):
            whole, turned = scratch[2 * i], scratch[2 * i + 1]
            for k in range(4):
                row = pl.multiple_of(((x + k) % 4) * STRIP, 16)
                whole[pl.ds(row, STRIP), :] = (
                    pair[:, columns(j)] if k == 0 else rest[(k - 1) * STRIP : k * STRIP, :]
                )
            column = pl.multiple_of(((y + step + 4) % 4) * GROUP, 128)
            for name, first, at, width in ROUTE0[j]:
                turned[at : at + width, :] = whole[:, at : at + width].T
                start(
                    turned.at[pl.ds(at, width), :],
                    outs[name].at[pl.ds(first, width), pl.ds(column, GROUP)],
                )
        for copy in started:
            copy.wait()

    n = len(work)
    own, partner = list(zip(units[:n], units[n : 2 * n])), list(zip(units[2 * n : 3 * n], units[3 * n :]))

    @pl.when(c == 0)
    def _():
        lay(own, partner)

    @pl.when(c == 1)
    def _():
        lay(partner, own)


LAID = (
    ((0, 0), (0, 1), (0, 2)),
    ((-1, 0), (1, 1)),
    ((1, 0), (2, 0)),
    ((-1, 1), (2, 1), (1, 2)),
    ((-1, 2), (2, 2)),
)


def lay(work, mine, theirs, before):
    n = len(work)
    n_in = 0 if before is None else 3
    shapes = tuple(jax.ShapeDtypeStruct(SHAPES[name], jnp.bfloat16) for name in NAMES)
    units = [u[s][at(j)] for u in (mine, theirs) for at in (lambda j: 3, lambda j: j) for s, j in work]
    return pl.pallas_call(
        lambda *refs: lay_kernel(work, n_in, *refs),
        out_shape=shapes,
        in_specs=vmem(4 * n) + anywhere(n_in),
        out_specs=tuple(anywhere(3)),
        scratch_shapes=[
            pltpu.VMEM(shape, jnp.bfloat16)
            for _, j in work
            for shape in ((GROUP, WIDTHS[j]), (WIDTHS[j], GROUP))
        ]
        + [pltpu.SemaphoreType.DMA((6 * n,))],
        input_output_aliases={4 * n + i: i for i in range(n_in)},
        compiler_params=pltpu.CompilerParams(vmem_limit_bytes=10 * 2**20),
    )(*held(units), *(before or ()))


STEPS = (0, -1, 1, 2)


def value_kernel(*refs):
    units, out, whole, turned, sems = refs[:16], refs[16], refs[17], refs[18], refs[19]
    y, x, c = place()

    def gather(pairs, rests):
        for step, pair, rest in zip(STEPS, pairs, rests):
            g = (x + step + 4) % 4
            for k in range(4):
                row = pl.multiple_of(((y + k) % 4) * GROUP + g * STRIP, 16)
                whole[pl.ds(row, STRIP), :] = (
                    pair[:, columns(0)] if k == 0 else rest[(k - 1) * STRIP : k * STRIP, :]
                )

    @pl.when(c == 0)
    def _():
        gather(units[8:12], units[12:])

    @pl.when(c == 1)
    def _():
        gather(units[:4], units[4:8])

    copies = []
    for s in range(4):
        turned[s] = whole[s * GROUP : (s + 1) * GROUP, :].T
        copy = pltpu.make_async_copy(turned.at[s], out.at[:, pl.ds(s * GROUP, GROUP)], sems.at[s])
        copy.start()
        copies.append(copy)
    for copy in copies:
        copy.wait()


def value_of(units):
    return pl.pallas_call(
        value_kernel,
        out_shape=jax.ShapeDtypeStruct((512, 3584), jnp.bfloat16),
        in_specs=vmem(16),
        out_specs=pl.BlockSpec(memory_space=pl.ANY),
        scratch_shapes=[
            pltpu.VMEM((3584, 512), jnp.bfloat16),
            pltpu.VMEM((4, 512, GROUP), jnp.bfloat16),
            pltpu.SemaphoreType.DMA((4,)),
        ],
        compiler_params=pltpu.CompilerParams(vmem_limit_bytes=10 * 2**20),
        name="value",
    )(*held(units))


def join_kernel(here, there, out):
    rows = out.shape[0]
    mine = here[0:rows, :].astype(jnp.float32)
    out[...] = jnp.where(mine != 0, mine, there[0:rows, :].astype(jnp.float32)).astype(out.dtype)


def join(here, there, out):
    return pl.pallas_call(
        join_kernel,
        out_shape=out,
        in_specs=vmem(2),
        out_specs=pl.BlockSpec(memory_space=pltpu.VMEM),
        compiler_params=pltpu.CompilerParams(vmem_limit_bytes=2 * 2**20),
    )(*held((here, there)))


NEAR, ACROSS = (1, 0, 3, 2), (3, 2, 1, 0)


def along_first(partners):
    return pairs(lambda y, x, c: (y, partners[x], c) if c == 0 else (partners[y], x, c))


def meet(norm):
    route = (along_first(NEAR), along_first(ACROSS), PARTNER)
    moves = [("width", list(enumerate(NEAR))), ("width", list(enumerate(ACROSS)))]
    moves += [(ZERO, move) for move in route + route]
    for k, (axis, move) in enumerate(moves):
        there = lax.ppermute(norm, axis, move)
        last = k + 1 == len(moves)
        out = jax.ShapeDtypeStruct((28, 128), norm.dtype) if last else pltpu.VMEM((32, 128), norm.dtype)
        norm = join(norm, there, out)
    return norm.reshape(-1)


def body(
    train_query,
    low_query,
    high_query,
    train_key,
    low_key,
    high_key,
    train_value,
    low_value,
    high_value,
    train_mixed,
    low_mixed,
    high_mixed,
    norm_train,
    norm_step,
):
    keep, give, norm = merge(
        train_query,
        low_query.T,
        high_query,
        train_key,
        low_key.T,
        high_key,
        train_value,
        low_value.T,
        high_value,
        train_mixed.T,
        high_mixed,
        low_mixed.T,
        norm_train.reshape(1, NORM),
        norm_step.reshape(1, NORM),
    )
    beside = send(give, PARTNER)
    keep_up = send(keep, first_axis(1))
    give_down = send(give, first_axis_across(-1))
    keep_down = send(keep, first_axis(-1))
    give_up = send(give, first_axis_across(1))
    far_keep = send(keep_up, first_axis(1))
    far_give = send(give_down, first_axis(-1))
    pair = pair_of(keep, beside)
    rest = stack((keep_up, keep_down, give_up, give_down, far_keep, far_give))
    units = (*rest, pair)
    mine = {
        0: units,
        -1: [send(u, second_axis(1)) for u in units],
        1: [send(u, second_axis(-1)) for u in units],
    }
    mine[2] = [
        send(mine[-1][j], second_axis(1))
        if j in (0, 3)
        else send(mine[1][j], second_axis(-1))
        for j in range(4)
    ]
    theirs = {s: [send(u, PARTNER) for u in mine[s]] for s in STEPS}

    outs = None
    for work in LAID:
        outs = lay(work, mine, theirs, outs)
    ready_query, ready_key, ready_mixed = outs
    ready_value = value_of([u[s][j] for u in (mine, theirs) for j in (3, 0) for s in STEPS])

    serve_norm = meet(norm)
    return (ready_query, ready_key, ready_value, ready_mixed, serve_norm)


def solution(mesh):
    torus = Mesh(
        mesh.devices.reshape(4, 4, 2, mesh.shape["width"]), ("zero_0", "zero_1", "zero_2", "width")
    )
    return jax.shard_map(
        body,
        mesh=torus,
        in_specs=(
            P(ZERO, "width"),
            P(ZERO, None),
            P(None, "width"),
            P(ZERO, "width"),
            P(ZERO, None),
            P(None, "width"),
            P(ZERO, "width"),
            P(ZERO, None),
            P(None, "width"),
            P("width", ZERO),
            P("width", None),
            P(None, ZERO),
            P(ZERO_WIDTH),
            P(ZERO_WIDTH),
        ),
        out_specs=(P("width", None), P("width", None), P("width", None), P(None, "width"), P()),
        check_vma=False,
    )
```

time: 109 us -> 126 us (1.16)
  starting transfers between devices: 45.2 us -> 58.7 us
  waiting for transfers between devices: 44.8 us -> 49.6 us
    ppermute x3 -> x8, starting transfers between devices: 5.74 us -> 20.6 us  [meet(): there = lax.ppermute(norm, axis, move)]
    ppermute x3 -> x8, waiting for transfers between devices: 0.23 us -> 8.24 us  [meet(): there = lax.ppermute(norm, axis, move)]
    ppermute x35, waiting for transfers between devices: 44.5 us -> 41.3 us  [send(): return lax.ppermute(array, ZERO, to)]
    ppermute x35, starting transfers between devices: 39.5 us -> 38 us  [send(): return lax.ppermute(array, ZERO, to)]
    pallas_call x4 -> x11, Pallas kernels: 3.68 us -> 2.71 us  [the longest x1 1.86 us: merge(): pl.pallas_call(merge_kernel, out_shape=(piece, piece, pltpu.VMEM((32, 128...]
  transfers between devices with their start and end apart: 38 -> 43, of which waited for: 13 -> 19; matrix products, arithmetic and copies ran while one was open for 0% -> 0% of each run, Pallas kernels for 12% -> 10%
where the time goes in v1:
time: 126 us; the launch traced here: 125 us
  starting transfers between devices  58.7 us (47%)
  waiting for transfers between devices  49.6 us (39%)
  Pallas kernels  16.2 us (13%)
    ppermute x35, waiting for transfers between devices, send(): return lax.ppermute(array, ZERO, to)  41.3 us
    ppermute x35, starting transfers between devices, send(): return lax.ppermute(array, ZERO, to)  38 us
    ppermute x8, starting transfers between devices, meet(): there = lax.ppermute(norm, axis, move)  20.6 us
    pallas_call x5, Pallas kernels, lay(): pl.pallas_call(lambda *refs: lay_kernel(work, n_in, *refs), out_shape=sha...  11.1 us
    ppermute x8, waiting for transfers between devices, meet(): there = lax.ppermute(norm, axis, move)  8.24 us
  transfers between devices with their start and end apart: 43, of which 19 were waited for; matrix products, arithmetic and copies ran while one was open for 0% of the time, Pallas kernels for 10%

profile of v1, /device:TPU:1, one launch (start us, length us, event | category | flops | bytes accessed | tf_op | source)
XLA Modules:
  0.0 125.4 jit_solution(2748665372898982680)
XLA Ops:
  6.7 2.8 %collective-permute-start.4 = (bf16[112,1536]{1,0:T(8,128)(2,1)S(1)}, bf16[112,1536]{1,0:T(8,128)(2,1)S(1)}, u32[]{:S(2)}, u32[]{:S(2)}) collective-permute-start(bf16[112,1536]{1,0:T(8,128)(2,1)S(1)} %get-tuple-element.26.keep), channel_id=1, source_target_pairs={{0,24},{4,100},{8,0},{12,108},{16,8},{20,116},{24,16},{28,124},{32... | collective-permute-start | bytes 1032200 | tf_op jit(solution)/shard_map/ppermute | solution.py:63
  11.1 3.3 %collective-permute-done.6.refs_3_ = bf16[112,1536]{1,0:T(8,128)(2,1)S(1)} collective-permute-done((bf16[112,1536]{1,0:T(8,128)(2,1)S(1)}, bf16[112,1536]{1,0:T(8,128)(2,1)S(1)}, u32[]{:S(2)}, u32[]{:S(2)}) %collective-permute-start.6) | collective-permute-done | bytes 344096 | tf_op jit(solution)/shard_map/ppermute | solution.py:63
  17.6 2.9 %collective-permute-done.5.refs_2_ = bf16[112,1536]{1,0:T(8,128)(2,1)S(1)} collective-permute-done((bf16[112,1536]{1,0:T(8,128)(2,1)S(1)}, bf16[112,1536]{1,0:T(8,128)(2,1)S(1)}, u32[]{:S(2)}, u32[]{:S(2)}) %collective-permute-start.5) | collective-permute-done | bytes 344096 | tf_op jit(solution)/shard_map/ppermute | solution.py:63
  25.2 3.6 %collective-permute-start.36 = (bf16[32,128]{1,0:T(8,128)(2,1)S(1)}, bf16[32,128]{1,0:T(8,128)(2,1)S(1)}, u32[]{:S(2)}, u32[]{:S(2)}) collective-permute-start(bf16[32,128]{1,0:T(8,128)(2,1)S(1)} %shard_map.178.here), channel_id=1, source_target_pairs={{0,3},{1,2},{2,1},{3,0},{4,7},{5,6},{6,5},{7,4},{8,11},{9,10},{10,... | collective-permute-start | bytes 24584 | tf_op jit(solution)/shard_map/ppermute | solution.py:357
  32.9 3.0 %collective-permute-start.38 = (bf16[32,128]{1,0:T(8,128)(2,1)S(1)}, bf16[32,128]{1,0:T(8,128)(2,1)S(1)}, u32[]{:S(2)}, u32[]{:S(2)}) collective-permute-start(bf16[32,128]{1,0:T(8,128)(2,1)S(1)} %shard_map.180.here), channel_id=1, source_target_pairs={{0,24},{4,100},{8,16},{12,108},{16,8},{20,116},{24,0},{28,124},{32... | collective-permute-start | bytes 24584 | tf_op jit(solution)/shard_map/ppermute | solution.py:357
  36.9 3.7 %collective-permute-start.39 = (bf16[32,128]{1,0:T(8,128)(2,1)S(1)}, bf16[32,128]{1,0:T(8,128)(2,1)S(1)}, u32[]{:S(2)}, u32[]{:S(2)}) collective-permute-start(bf16[32,128]{1,0:T(8,128)(2,1)S(1)} %shard_map.181.here), channel_id=1, source_target_pairs={{0,4},{4,0},{8,12},{12,8},{16,20},{20,16},{24,28},{28,24},{32,36},... | collective-permute-start | bytes 24584 | tf_op jit(solution)/shard_map/ppermute | solution.py:357
  41.4 2.5 %collective-permute-start.40 = (bf16[32,128]{1,0:T(8,128)(2,1)S(1)}, bf16[32,128]{1,0:T(8,128)(2,1)S(1)}, u32[]{:S(2)}, u32[]{:S(2)}) collective-permute-start(bf16[32,128]{1,0:T(8,128)(2,1)S(1)} %shard_map.182.here), channel_id=1, source_target_pairs={{0,8},{4,36},{8,0},{12,44},{16,24},{20,52},{24,16},{28,60},{32,40}... | collective-permute-start | bytes 24584 | tf_op jit(solution)/shard_map/ppermute | solution.py:357
  45.0 2.8 %collective-permute-start.41 = (bf16[32,128]{1,0:T(8,128)(2,1)S(1)}, bf16[32,128]{1,0:T(8,128)(2,1)S(1)}, u32[]{:S(2)}, u32[]{:S(2)}) collective-permute-start(bf16[32,128]{1,0:T(8,128)(2,1)S(1)} %shard_map.183.here), channel_id=1, source_target_pairs={{0,24},{4,100},{8,16},{12,108},{16,8},{20,116},{24,0},{28,124},{32... | collective-permute-start | bytes 24584 | tf_op jit(solution)/shard_map/ppermute | solution.py:357
  53.6 2.7 %collective-permute-start.24 = (bf16[672,512]{1,0:T(8,128)(2,1)S(1)}, bf16[672,512]{1,0:T(8,128)(2,1)S(1)}, u32[]{:S(2)}, u32[]{:S(2)}) collective-permute-start(bf16[672,512]{1,0:T(8,128)(2,1)S(1)} %get-tuple-element.30.refs_3_.refs_4_), channel_id=1, source_target_pairs={{0,96},{4,28},{8,104},{12,4},{16,112},{20,12},{24,120},{28,20},{32... | collective-permute-start | bytes 2064392 | tf_op jit(solution)/shard_map/ppermute | solution.py:63
  57.8 3.0 %collective-permute-start.18 = (bf16[672,768]{1,0:T(8,128)(2,1)S(1)}, bf16[672,768]{1,0:T(8,128)(2,1)S(1)}, u32[]{:S(2)}, u32[]{:S(2)}) collective-permute-start(bf16[672,768]{1,0:T(8,128)(2,1)S(1)} %get-tuple-element.29.refs_4_), channel_id=1, source_target_pairs={{0,96},{4,28},{8,104},{12,4},{16,112},{20,12},{24,120},{28,20},{32... | collective-permute-start | bytes 3096584 | tf_op jit(solution)/shard_map/ppermute | solution.py:63
  61.1 3.2 %collective-permute-start.33 = (bf16[672,768]{1,0:T(8,128)(2,1)S(1)}, bf16[672,768]{1,0:T(8,128)(2,1)S(1)}, u32[]{:S(2)}, u32[]{:S(2)}) collective-permute-start(bf16[672,768]{1,0:T(8,128)(2,1)S(1)} %get-tuple-element.29.refs_4_), channel_id=1, source_target_pairs={{0,4},{4,0},{8,12},{12,8},{16,20},{20,16},{24,28},{28,24},{32,36},... | collective-permute-start | bytes 3096584 | tf_op jit(solution)/shard_map/ppermute | solution.py:63
  64.3 4.2 %collective-permute-done.25.refs_2_.refs_5_ = bf16[672,512]{1,0:T(8,128)(2,1)S(1)} collective-permute-done((bf16[672,512]{1,0:T(8,128)(2,1)S(1)}, bf16[672,512]{1,0:T(8,128)(2,1)S(1)}, u32[]{:S(2)}, u32[]{:S(2)}) %collective-permute-start.25) | collective-permute-done | bytes 688160 | tf_op jit(solution)/shard_map/ppermute | solution.py:63
  68.5 3.2 %collective-permute-start.12 = (bf16[224,1536]{1,0:T(8,128)(2,1)S(1)}, bf16[224,1536]{1,0:T(8,128)(2,1)S(1)}, u32[]{:S(2)}, u32[]{:S(2)}) collective-permute-start(bf16[224,1536]{1,0:T(8,128)(2,1)S(1)} %collective-permute-done.1.refs_0_.refs_1_), channel_id=1, source_target_pairs={{0,4},{4,0},{8,12},{12,8},{16,20},{20,16},{24,28},{28,24},{32,36},... | collective-permute-start | bytes 2064392 | tf_op jit(solution)/shard_map/ppermute | solution.py:63
  71.7 8.3 %collective-permute-done.11.refs_3_ = bf16[672,256]{1,0:T(8,128)(2,1)S(1)} collective-permute-done((bf16[672,256]{1,0:T(8,128)(2,1)S(1)}, bf16[672,256]{1,0:T(8,128)(2,1)S(1)}, u32[]{:S(2)}, u32[]{:S(2)}) %collective-permute-start.11) | collective-permute-done | bytes 344096 | tf_op jit(solution)/shard_map/ppermute | solution.py:63
  80.0 2.8 %collective-permute-start.20 = (bf16[224,1536]{1,0:T(8,128)(2,1)S(1)}, bf16[224,1536]{1,0:T(8,128)(2,1)S(1)}, u32[]{:S(2)}, u32[]{:S(2)}) collective-permute-start(bf16[224,1536]{1,0:T(8,128)(2,1)S(1)} %collective-permute-done.16.refs_1_.refs_0_.refs_2_), channel_id=1, source_target_pairs={{0,4},{4,0},{8,12},{12,8},{16,20},{20,16},{24,28},{28,24},{32,36},... | collective-permute-start | bytes 2064392 | tf_op jit(solution)/shard_map/ppermute | solution.py:63
  87.0 9.2 %collective-permute-done.2.refs_1_.refs_3_ = bf16[224,1536]{1,0:T(8,128)(2,1)S(1)} collective-permute-done((bf16[224,1536]{1,0:T(8,128)(2,1)S(1)}, bf16[224,1536]{1,0:T(8,128)(2,1)S(1)}, u32[]{:S(2)}, u32[]{:S(2)}) %collective-permute-start.2) | collective-permute-done | bytes 688160 | tf_op jit(solution)/shard_map/ppermute | solution.py:63
  96.2 2.4 %collective-permute-start.30 = (bf16[672,768]{1,0:T(8,128)(2,1)S(1)}, bf16[672,768]{1,0:T(8,128)(2,1)S(1)}, u32[]{:S(2)}, u32[]{:S(2)}) collective-permute-start(bf16[672,768]{1,0:T(8,128)(2,1)S(1)} %collective-permute-done.18.refs_3_), channel_id=1, source_target_pairs={{0,4},{4,0},{8,12},{12,8},{16,20},{20,16},{24,28},{28,24},{32,36},... | collective-permute-start | bytes 3096584 | tf_op jit(solution)/shard_map/ppermute | solution.py:63
  98.6 5.0 %collective-permute-done.26.refs_3_.refs_7_ = bf16[672,512]{1,0:T(8,128)(2,1)S(1)} collective-permute-done((bf16[672,512]{1,0:T(8,128)(2,1)S(1)}, bf16[672,512]{1,0:T(8,128)(2,1)S(1)}, u32[]{:S(2)}, u32[]{:S(2)}) %collective-permute-start.26) | collective-permute-done | bytes 688160 | tf_op jit(solution)/shard_map/ppermute | solution.py:63
  103.6 2.4 %collective-permute-start.21 = (bf16[672,768]{1,0:T(8,128)(2,1)S(1)}, bf16[672,768]{1,0:T(8,128)(2,1)S(1)}, u32[]{:S(2)}, u32[]{:S(2)}) collective-permute-start(bf16[672,768]{1,0:T(8,128)(2,1)S(1)} %collective-permute-done.17.refs_3_), channel_id=1, source_target_pairs={{0,4},{4,0},{8,12},{12,8},{16,20},{20,16},{24,28},{28,24},{32,36},... | collective-permute-start | bytes 3096584 | tf_op jit(solution)/shard_map/ppermute | solution.py:63
  107.0 3.7 %collective-permute-done.28.refs_7_.refs_15_ = bf16[672,512]{1,0:T(8,128)(2,1)S(1)} collective-permute-done((bf16[672,512]{1,0:T(8,128)(2,1)S(1)}, bf16[672,512]{1,0:T(8,128)(2,1)S(1)}, u32[]{:S(2)}, u32[]{:S(2)}) %collective-permute-start.28) | collective-permute-done | bytes 688160 | tf_op jit(solution)/shard_map/ppermute | solution.py:63
  111.6 2.6 %shard_map.173 = (bf16[1024,3584]{1,0:T(8,128)(2,1)}, bf16[512,3584]{1,0:T(8,128)(2,1)}, bf16[3584,1024]{1,0:T(8,128)(2,1)}) custom-call(bf16[224,1536]{1,0:T(8,128)(2,1)S(1)} %pair.1.refs_0_.refs_1_.refs_2_, bf16[224,1536]{1,0:T(8,128)(2,1)S(1)} %pair.1.refs_0_.refs_1_.refs_2_, bf16[224,1536]{1,0:T(8,128)(2,1)S(1)} %pair.1.refs_0_.refs_1_.refs_2_, ...), custom_call_target="tpu_custom_call" | custom-call | tf_op jit(solution)/shard_map/pallas_call | solution.py:263
  114.3 2.4 %value.1 = bf16[512,3584]{1,0:T(8,128)(2,1)} custom-call(bf16[224,1536]{1,0:T(8,128)(2,1)S(1)} %pair.1.refs_0_.refs_1_.refs_2_, bf16[224,1536]{1,0:T(8,128)(2,1)S(1)} %collective-permute-done.1.refs_0_.refs_1_, bf16[224,1536]{1,0:T(8,128)(2,1)S(1)} %collective-permute-done.16.refs_1_.refs_0_.refs_2_, ...), custom_call_target="tpu_custom_call" | custom-call | tf_op jit(solution)/shard_map/value/pallas_call | solution.py:314
  116.7 2.3 %shard_map.174 = (bf16[1024,3584]{1,0:T(8,128)(2,1)}, bf16[512,3584]{1,0:T(8,128)(2,1)}, bf16[3584,1024]{1,0:T(8,128)(2,1)}) custom-call(bf16[224,1536]{1,0:T(8,128)(2,1)S(1)} %collective-permute-done.1.refs_0_.refs_1_, ...), custom_call_target="tpu_custom_call", output_to_operand_aliasing={{0}: (8, {}), {1}: (9, {}), {2}: (10, {})} | custom-call | tf_op jit(solution)/shard_map/pallas_call | solution.py:263
  120.8 3.0 %shard_map.176 = (bf16[1024,3584]{1,0:T(8,128)(2,1)}, bf16[512,3584]{1,0:T(8,128)(2,1)}, bf16[3584,1024]{1,0:T(8,128)(2,1)}) custom-call(bf16[224,1536]{1,0:T(8,128)(2,1)S(1)} %collective-permute-done.1.refs_0_.refs_1_, bf16[224,1536]{1,0:T(8,128)(2,1)S(1)} %collective-permute-done.2.refs_1_.refs_3_, ...), custom_call_target="tpu_custom_call", output_to_operand_aliasing={{0}: (12, {}), {1}: (13, {}), {2}: (14, {})} | custom-call | tf_op jit(solution)/shard_map/pallas_call | solution.py:263
  (79 shorter events, 39.6 us)
Async XLA Ops:
  9.6 11.0 %collective-permute-start.5 = (bf16[112,1536]{1,0:T(8,128)(2,1)S(1)}, bf16[112,1536]{1,0:T(8,128)(2,1)S(1)}, u32[]{:S(2)}, u32[]{:S(2)}) collective-permute-start(bf16[112,1536]{1,0:T(8,128)(2,1)S(1)} %get-tuple-element.27), channel_id=1, source_target_pairs={{0,36},{4,8},{8,44},{12,16},{16,52},{20,24},{24,60},{28,0},{32,68}... | collective-permute-start | bytes 1032200 | tf_op jit(solution)/shard_map/ppermute | solution.py:63
  11.1 10.9 %collective-permute-start.7 = (bf16[112,1536]{1,0:T(8,128)(2,1)S(1)}, bf16[112,1536]{1,0:T(8,128)(2,1)S(1)}, u32[]{:S(2)}, u32[]{:S(2)}) collective-permute-start(bf16[112,1536]{1,0:T(8,128)(2,1)S(1)} %collective-permute-done.3.refs_0_), channel_id=1, source_target_pairs={{0,8},{4,36},{8,16},{12,44},{16,24},{20,52},{24,0},{28,60},{32,40}... | collective-permute-start | bytes 1032200 | tf_op jit(solution)/shard_map/ppermute | solution.py:63
  15.3 38.2 %collective-permute-start.31 = (bf16[224,1536]{1,0:T(8,128)(2,1)S(1)}, bf16[224,1536]{1,0:T(8,128)(2,1)S(1)}, u32[]{:S(2)}, u32[]{:S(2)}) collective-permute-start(bf16[224,1536]{1,0:T(8,128)(2,1)S(1)} %pair.1.refs_0_.refs_1_.refs_2_), channel_id=1, source_target_pairs={{0,4},{4,0},{8,12},{12,8},{16,20},{20,16},{24,28},{28,24},{32,36},... | collective-permute-start | bytes 2064392 | tf_op jit(solution)/shard_map/ppermute | solution.py:63
  16.4 37.2 %collective-permute-start.1 = (bf16[224,1536]{1,0:T(8,128)(2,1)S(1)}, bf16[224,1536]{1,0:T(8,128)(2,1)S(1)}, u32[]{:S(2)}, u32[]{:S(2)}) collective-permute-start(bf16[224,1536]{1,0:T(8,128)(2,1)S(1)} %pair.1.refs_0_.refs_1_.refs_2_), channel_id=1, source_target_pairs={{0,32},{4,12},{8,40},{12,20},{16,48},{20,28},{24,56},{28,4},{32,64... | collective-permute-start | bytes 2064392 | tf_op jit(solution)/shard_map/ppermute | solution.py:63
  20.6 33.1 %collective-permute-start.16 = (bf16[224,1536]{1,0:T(8,128)(2,1)S(1)}, bf16[224,1536]{1,0:T(8,128)(2,1)S(1)}, u32[]{:S(2)}, u32[]{:S(2)}) collective-permute-start(bf16[224,1536]{1,0:T(8,128)(2,1)S(1)} %pair.1.refs_0_.refs_1_.refs_2_), channel_id=1, source_target_pairs={{0,96},{4,28},{8,104},{12,4},{16,112},{20,12},{24,120},{28,20},{32... | collective-permute-start | bytes 2064392 | tf_op jit(solution)/shard_map/ppermute | solution.py:63
  22.1 29.4 %collective-permute-start.34 = (bf16[672,256]{1,0:T(8,128)(2,1)S(1)}, bf16[672,256]{1,0:T(8,128)(2,1)S(1)}, u32[]{:S(2)}, u32[]{:S(2)}) collective-permute-start(bf16[672,256]{1,0:T(8,128)(2,1)S(1)} %get-tuple-element.28.refs_5_), channel_id=1, source_target_pairs={{0,4},{4,0},{8,12},{12,8},{16,20},{20,16},{24,28},{28,24},{32,36},... | collective-permute-start | bytes 1032200 | tf_op jit(solution)/shard_map/ppermute | solution.py:63
  51.1 13.2 %collective-permute-start.32 = (bf16[672,512]{1,0:T(8,128)(2,1)S(1)}, bf16[672,512]{1,0:T(8,128)(2,1)S(1)}, u32[]{:S(2)}, u32[]{:S(2)}) collective-permute-start(bf16[672,512]{1,0:T(8,128)(2,1)S(1)} %get-tuple-element.30.refs_3_.refs_4_), channel_id=1, source_target_pairs={{0,4},{4,0},{8,12},{12,8},{16,20},{20,16},{24,28},{28,24},{32,36},... | collective-permute-start | bytes 2064392 | tf_op jit(solution)/shard_map/ppermute | solution.py:63
  53.5 15.0 %collective-permute-start.25 = (bf16[672,512]{1,0:T(8,128)(2,1)S(1)}, bf16[672,512]{1,0:T(8,128)(2,1)S(1)}, u32[]{:S(2)}, u32[]{:S(2)}) collective-permute-start(bf16[672,512]{1,0:T(8,128)(2,1)S(1)} %get-tuple-element.30.refs_3_.refs_4_), channel_id=1, source_target_pairs={{0,32},{4,12},{8,40},{12,20},{16,48},{20,28},{24,56},{28,4},{32,64... | collective-permute-start | bytes 2064392 | tf_op jit(solution)/shard_map/ppermute | solution.py:63
  53.6 14.9 %collective-permute-start.24 = (bf16[672,512]{1,0:T(8,128)(2,1)S(1)}, bf16[672,512]{1,0:T(8,128)(2,1)S(1)}, u32[]{:S(2)}, u32[]{:S(2)}) collective-permute-start(bf16[672,512]{1,0:T(8,128)(2,1)S(1)} %get-tuple-element.30.refs_3_.refs_4_), channel_id=1, source_target_pairs={{0,96},{4,28},{8,104},{12,4},{16,112},{20,12},{24,120},{28,20},{32... | collective-permute-start | bytes 2064392 | tf_op jit(solution)/shard_map/ppermute | solution.py:63
  57.8 24.9 %collective-permute-start.18 = (bf16[672,768]{1,0:T(8,128)(2,1)S(1)}, bf16[672,768]{1,0:T(8,128)(2,1)S(1)}, u32[]{:S(2)}, u32[]{:S(2)}) collective-permute-start(bf16[672,768]{1,0:T(8,128)(2,1)S(1)} %get-tuple-element.29.refs_4_), channel_id=1, source_target_pairs={{0,96},{4,28},{8,104},{12,4},{16,112},{20,12},{24,120},{28,20},{32... | collective-permute-start | bytes 3096584 | tf_op jit(solution)/shard_map/ppermute | solution.py:63
  61.1 23.8 %collective-permute-start.33 = (bf16[672,768]{1,0:T(8,128)(2,1)S(1)}, bf16[672,768]{1,0:T(8,128)(2,1)S(1)}, u32[]{:S(2)}, u32[]{:S(2)}) collective-permute-start(bf16[672,768]{1,0:T(8,128)(2,1)S(1)} %get-tuple-element.29.refs_4_), channel_id=1, source_target_pairs={{0,4},{4,0},{8,12},{12,8},{16,20},{20,16},{24,28},{28,24},{32,36},... | collective-permute-start | bytes 3096584 | tf_op jit(solution)/shard_map/ppermute | solution.py:63
  64.3 20.6 %collective-permute-start.17 = (bf16[672,768]{1,0:T(8,128)(2,1)S(1)}, bf16[672,768]{1,0:T(8,128)(2,1)S(1)}, u32[]{:S(2)}, u32[]{:S(2)}) collective-permute-start(bf16[672,768]{1,0:T(8,128)(2,1)S(1)} %get-tuple-element.29.refs_4_), channel_id=1, source_target_pairs={{0,32},{4,12},{8,40},{12,20},{16,48},{20,28},{24,56},{28,4},{32,64... | collective-permute-start | bytes 3096584 | tf_op jit(solution)/shard_map/ppermute | solution.py:63
  68.5 11.5 %collective-permute-start.11 = (bf16[672,256]{1,0:T(8,128)(2,1)S(1)}, bf16[672,256]{1,0:T(8,128)(2,1)S(1)}, u32[]{:S(2)}, u32[]{:S(2)}) collective-permute-start(bf16[672,256]{1,0:T(8,128)(2,1)S(1)} %collective-permute-done.10.refs_5_), channel_id=1, source_target_pairs={{0,96},{4,28},{8,104},{12,4},{16,112},{20,12},{24,120},{28,20},{32... | collective-permute-start | bytes 1032200 | tf_op jit(solution)/shard_map/ppermute | solution.py:63
  68.5 18.0 %collective-permute-start.12 = (bf16[224,1536]{1,0:T(8,128)(2,1)S(1)}, bf16[224,1536]{1,0:T(8,128)(2,1)S(1)}, u32[]{:S(2)}, u32[]{:S(2)}) collective-permute-start(bf16[224,1536]{1,0:T(8,128)(2,1)S(1)} %collective-permute-done.1.refs_0_.refs_1_), channel_id=1, source_target_pairs={{0,4},{4,0},{8,12},{12,8},{16,20},{20,16},{24,28},{28,24},{32,36},... | collective-permute-start | bytes 2064392 | tf_op jit(solution)/shard_map/ppermute | solution.py:63
  82.7 23.2 %collective-permute-start.19 = (bf16[672,768]{1,0:T(8,128)(2,1)S(1)}, bf16[672,768]{1,0:T(8,128)(2,1)S(1)}, u32[]{:S(2)}, u32[]{:S(2)}) collective-permute-start(bf16[672,768]{1,0:T(8,128)(2,1)S(1)} %collective-permute-done.18.refs_3_), channel_id=1, source_target_pairs={{0,96},{4,28},{8,104},{12,4},{16,112},{20,12},{24,120},{28,20},{32... | collective-permute-start | bytes 3096584 | tf_op jit(solution)/shard_map/ppermute | solution.py:63
  84.9 11.3 %collective-permute-start.2 = (bf16[224,1536]{1,0:T(8,128)(2,1)S(1)}, bf16[224,1536]{1,0:T(8,128)(2,1)S(1)}, u32[]{:S(2)}, u32[]{:S(2)}) collective-permute-start(bf16[224,1536]{1,0:T(8,128)(2,1)S(1)} %collective-permute-done.1.refs_0_.refs_1_), channel_id=1, source_target_pairs={{0,32},{4,12},{8,40},{12,20},{16,48},{20,28},{24,56},{28,4},{32,64... | collective-permute-start | bytes 2064392 | tf_op jit(solution)/shard_map/ppermute | solution.py:63
  84.9 13.6 %collective-permute-start.29 = (bf16[672,512]{1,0:T(8,128)(2,1)S(1)}, bf16[672,512]{1,0:T(8,128)(2,1)S(1)}, u32[]{:S(2)}, u32[]{:S(2)}) collective-permute-start(bf16[672,512]{1,0:T(8,128)(2,1)S(1)} %collective-permute-done.25.refs_2_.refs_5_), channel_id=1, source_target_pairs={{0,4},{4,0},{8,12},{12,8},{16,20},{20,16},{24,28},{28,24},{32,36},... | collective-permute-start | bytes 2064392 | tf_op jit(solution)/shard_map/ppermute | solution.py:63
  86.5 17.1 %collective-permute-start.26 = (bf16[672,512]{1,0:T(8,128)(2,1)S(1)}, bf16[672,512]{1,0:T(8,128)(2,1)S(1)}, u32[]{:S(2)}, u32[]{:S(2)}) collective-permute-start(bf16[672,512]{1,0:T(8,128)(2,1)S(1)} %collective-permute-done.25.refs_2_.refs_5_), channel_id=1, source_target_pairs={{0,32},{4,12},{8,40},{12,20},{16,48},{20,28},{24,56},{28,4},{32,64... | collective-permute-start | bytes 2064392 | tf_op jit(solution)/shard_map/ppermute | solution.py:63
  86.5 19.4 %collective-permute-start.27 = (bf16[672,512]{1,0:T(8,128)(2,1)S(1)}, bf16[672,512]{1,0:T(8,128)(2,1)S(1)}, u32[]{:S(2)}, u32[]{:S(2)}) collective-permute-start(bf16[672,512]{1,0:T(8,128)(2,1)S(1)} %collective-permute-done.24.refs_2_.refs_6_), channel_id=1, source_target_pairs={{0,4},{4,0},{8,12},{12,8},{16,20},{20,16},{24,28},{28,24},{32,36},... | collective-permute-start | bytes 2064392 | tf_op jit(solution)/shard_map/ppermute | solution.py:63
  103.6 17.2 %collective-permute-start.21 = (bf16[672,768]{1,0:T(8,128)(2,1)S(1)}, bf16[672,768]{1,0:T(8,128)(2,1)S(1)}, u32[]{:S(2)}, u32[]{:S(2)}) collective-permute-start(bf16[672,768]{1,0:T(8,128)(2,1)S(1)} %collective-permute-done.17.refs_3_), channel_id=1, source_target_pairs={{0,4},{4,0},{8,12},{12,8},{16,20},{20,16},{24,28},{28,24},{32,36},... | collective-permute-start | bytes 3096584 | tf_op jit(solution)/shard_map/ppermute | solution.py:63
  106.0 14.8 %collective-permute-start.22 = (bf16[672,768]{1,0:T(8,128)(2,1)S(1)}, bf16[672,768]{1,0:T(8,128)(2,1)S(1)}, u32[]{:S(2)}, u32[]{:S(2)}) collective-permute-start(bf16[672,768]{1,0:T(8,128)(2,1)S(1)} %collective-permute-done.19.refs_4_), channel_id=1, source_target_pairs={{0,4},{4,0},{8,12},{12,8},{16,20},{20,16},{24,28},{28,24},{32,36},... | collective-permute-start | bytes 3096584 | tf_op jit(solution)/shard_map/ppermute | solution.py:63
  106.5 14.3 %collective-permute-start.23 = (bf16[672,256]{1,0:T(8,128)(2,1)S(1)}, bf16[672,256]{1,0:T(8,128)(2,1)S(1)}, u32[]{:S(2)}, u32[]{:S(2)}) collective-permute-start(bf16[672,256]{1,0:T(8,128)(2,1)S(1)} %collective-permute-done.10.refs_5_), channel_id=1, source_target_pairs={{0,4},{4,0},{8,12},{12,8},{16,20},{20,16},{24,28},{28,24},{32,36},... | collective-permute-start | bytes 1032200 | tf_op jit(solution)/shard_map/ppermute | solution.py:63
  106.6 17.2 %collective-permute-start.14 = (bf16[672,256]{1,0:T(8,128)(2,1)S(1)}, bf16[672,256]{1,0:T(8,128)(2,1)S(1)}, u32[]{:S(2)}, u32[]{:S(2)}) collective-permute-start(bf16[672,256]{1,0:T(8,128)(2,1)S(1)} %collective-permute-done.9.refs_2_), channel_id=1, source_target_pairs={{0,4},{4,0},{8,12},{12,8},{16,20},{20,16},{24,28},{28,24},{32,36},... | collective-permute-start | bytes 1032200 | tf_op jit(solution)/shard_map/ppermute | solution.py:63
  110.7 13.1 %collective-permute-start.15 = (bf16[672,256]{1,0:T(8,128)(2,1)S(1)}, bf16[672,256]{1,0:T(8,128)(2,1)S(1)}, u32[]{:S(2)}, u32[]{:S(2)}) collective-permute-start(bf16[672,256]{1,0:T(8,128)(2,1)S(1)} %collective-permute-done.11.refs_3_), channel_id=1, source_target_pairs={{0,4},{4,0},{8,12},{12,8},{16,20},{20,16},{24,28},{28,24},{32,36},... | collective-permute-start | bytes 1032200 | tf_op jit(solution)/shard_map/ppermute | solution.py:63
  (19 other events, 116.3 us)

commit v2 on v1

v2 whole, which is shorter than its diff:
```python
import jax
import jax.numpy as jnp
from jax import lax
from jax.experimental import pallas as pl
from jax.experimental.pallas import tpu as pltpu
from jax.sharding import Mesh
from jax.sharding import PartitionSpec as P

ZERO = ("zero_0", "zero_1", "zero_2")
ZERO_WIDTH = ("zero_0", "zero_1", "zero_2", "width")


mix_rate = 0.5

ROWS = 112
HALF = 1536
CHUNK = 512
GROUP = 8 * ROWS
STRIP = 2 * ROWS
REST = 3 * STRIP
NORM = 28
TILE = (8, 512)

ROUTE0 = (("query", 0), ("query", 512), ("key", 0))
ROUTE1 = (("value", 0), ("mixed", 0), ("mixed", 512))

UNITS_OF = ((3, 0, 2), (3, 1), (3, 2))


def spot(j, k):
    if k == 0:
        return 3, 0, j * CHUNK
    if j == 0:
        return (2, REST, 0) if k == 2 else (0, (k - 1) // 2 * STRIP, 0)
    return j, (k - 1) * STRIP, 0


def pairs(move):
    return [
        ((y * 4 + x) * 2 + c, ((v % 4) * 4 + u % 4) * 2 + d)
        for y in range(4)
        for x in range(4)
        for c in range(2)
        for v, u, d in (move(y, x, c),)
    ]


def first_axis(step):
    return pairs(lambda y, x, c: (y, x + step, c) if c == 0 else (y + step, x, c))


def first_axis_across(step):
    return pairs(lambda y, x, c: (y, x + step, 0) if c == 1 else (y + step, x, 1))


def second_axis(step):
    return pairs(lambda y, x, c: (y + step, x, c) if c == 0 else (y, x + step, c))


PARTNER = pairs(lambda y, x, c: (y, x, 1 - c))


def send(array, to):
    return lax.ppermute(array, ZERO, to)


def place():
    return tuple(lax.axis_index(a) for a in ZERO)


def held(arrays):
    return [pltpu.with_memory_space_constraint(a, pltpu.VMEM) for a in arrays]


def vmem(n):
    return [pl.BlockSpec(memory_space=pltpu.VMEM)] * n


def anywhere(n):
    return [pl.BlockSpec(memory_space=pl.ANY)] * n


MERGED = (
    (ROWS, 1024), (32, ROWS), (32, 1024),
    (ROWS, 512), (32, ROWS), (32, 512),
    (ROWS, 512), (32, ROWS), (32, 512),
    (ROWS, 1024), (32, ROWS), (32, 1024),
    (1, NORM), (1, NORM),
)


def merge_kernel(*refs):
    ins, (keep, give), here, (line, sems) = refs[:14], refs[14:16], refs[16:30], refs[30:]
    y, x, c = place()
    copies = [pltpu.make_async_copy(a, b, sems.at[i]) for i, (a, b) in enumerate(zip(ins, here))]
    for copy in copies:
        copy.start()
    line[...] = jnp.zeros(line.shape, jnp.float32)
    for copy in copies:
        copy.wait()
    tq, lq, hq, tk, lk, hk, tv, lv, hv, tm, lm, hm, gain, step = here

    def latest(train, low, high):
        product = lax.dot_general(
            low[...], high[...], (((0,), (0,)), ((), ())), preferred_element_type=jnp.float32
        )
        return (train[...].astype(jnp.float32) + mix_rate * product).astype(jnp.bfloat16)

    first = ((((y * 4 + x) * 2 + c) * 4) + lax.axis_index("width")) * NORM
    row, at = first // 512, first % 512
    lane = lax.broadcasted_iota(jnp.int32, (1, 512), 1)
    line[0:1, 0:NORM] = gain[...] + step[...]
    turned = pltpu.roll(line[0:1, :], at, 1)
    line[0:1, :] = jnp.zeros((1, 512), jnp.float32)
    line[pl.ds(row, 1), :] = jnp.where(lane >= at, turned, 0.0)
    line[pl.ds(row + 1, 1), :] = jnp.where(lane < at, turned, line[pl.ds(row + 1, 1), :])
    for to in (keep, give):
        to[ROWS : ROWS + 8, 0:512] = line[...].astype(jnp.bfloat16)

    rows = slice(0, ROWS)

    def fill(first, second):
        first[rows, 0:1024] = latest(tq, lq, hq)
        first[rows, 1024:1536] = latest(tk, lk, hk)
        second[rows, 0:512] = latest(tv, lv, hv)
        second[rows, 512:1536] = latest(tm, lm, hm)

    @pl.when(c == 0)
    def _():
        fill(keep, give)

    @pl.when(c == 1)
    def _():
        fill(give, keep)


def merge(*args):
    piece = pltpu.VMEM((ROWS + 8, HALF), jnp.bfloat16)
    return pl.pallas_call(
        merge_kernel,
        out_shape=(piece, piece),
        in_specs=anywhere(len(args)),
        out_specs=tuple(vmem(2)),
        scratch_shapes=[pltpu.VMEM(shape, a.dtype) for shape, a in zip(MERGED, args)]
        + [pltpu.VMEM(TILE, jnp.float32), pltpu.SemaphoreType.DMA((14,))],
        compiler_params=pltpu.CompilerParams(vmem_limit_bytes=8 * 2**20),
        name="merge",
    )(*[pltpu.with_memory_space_constraint(a, pltpu.HBM) for a in args])


def pair_kernel(keep, beside, out):
    _, _, c = place()
    for piece, core in ((keep, c), (beside, 1 - c)):
        out[pl.ds(pl.multiple_of(core * ROWS, 16), ROWS), :] = piece[0:ROWS, :]


def pair_of(keep, beside):
    return pl.pallas_call(
        pair_kernel,
        out_shape=pltpu.VMEM((STRIP, HALF), jnp.bfloat16),
        in_specs=vmem(2),
        out_specs=pl.BlockSpec(memory_space=pltpu.VMEM),
        compiler_params=pltpu.CompilerParams(vmem_limit_bytes=2 * 2**20),
        name="pair",
    )(*held((keep, beside)))


OFFSETS = ((3, 0), (1, 0), (3, 1), (1, 1), (2, 0), (2, 1))


def place_pieces(pieces, units, spots):
    _, _, c = place()
    for piece, (k, other) in zip(pieces, OFFSETS):
        core = c if other == 0 else 1 - c
        for j in range(3):
            if (j, k) in spots:
                unit, row, _ = spot(j, k)
                at = pl.multiple_of(row + core * ROWS, 16)
                units[unit][pl.ds(at, ROWS), :] = piece[0:ROWS, j * CHUNK : (j + 1) * CHUNK]


def near_kernel(*refs):
    place_pieces(refs[:4], {0: refs[4]}, ((0, 1), (0, 3)))


def known(*tiles):
    found = tiles[0].astype(jnp.float32)
    for tile in tiles[1:]:
        found = jnp.where(found != 0, found, tile.astype(jnp.float32))
    return found


def rest_kernel(*refs):
    pieces, one, two, tile = refs[:8], refs[8], refs[9], refs[10]
    spots = [(j, k) for j in (1, 2) for k in (1, 2, 3)] + [(0, 2)]
    place_pieces(pieces[:6], {1: one, 2: two}, spots)
    tile[...] = known(*[p[ROWS : ROWS + 8, 0:512] for p in pieces]).astype(tile.dtype)


def stack(kernel, pieces, shapes):
    return pl.pallas_call(
        kernel,
        out_shape=tuple(pltpu.VMEM(shape, jnp.bfloat16) for shape in shapes),
        in_specs=vmem(len(pieces)),
        out_specs=tuple(vmem(len(shapes))),
        compiler_params=pltpu.CompilerParams(vmem_limit_bytes=4 * 2**20),
    )(*held(pieces))


NAMES = ("query", "key", "mixed")
SHAPES = {"query": (1024, 3584), "key": (512, 3584), "mixed": (3584, 1024)}


def lay_kernel(work, keys, n_in, *refs):
    n = len(keys)
    own, partner, refs = dict(zip(keys, refs)), dict(zip(keys, refs[n:])), refs[2 * n + n_in :]
    outs, (whole, turned, sems) = dict(zip(NAMES, refs[:3])), refs[3:]
    y, x, c = place()

    def lay(route0, route1):
        started = []

        def start(source, target):
            copy = pltpu.make_async_copy(source, target, sems.at[len(started)])
            copy.start()
            started.append(copy)

        for step, j in work:
            name, first = ROUTE1[j]
            if name == "mixed":
                g = (x + step + 4) % 4
                for k in range(4):
                    row = pl.multiple_of(((y + k) % 4) * GROUP + g * STRIP, 16)
                    unit, at, column = spot(j, k)
                    start(
                        route1[step, unit].at[pl.ds(at, STRIP), pl.ds(column, CHUNK)],
                        outs[name].at[pl.ds(row, STRIP), pl.ds(first, CHUNK)],
                    )
        for i, (step, j) in enumerate(work):
            name, first = ROUTE0[j]
            for k in range(4):
                row = pl.multiple_of(((x + k) % 4) * STRIP, 16)
                unit, at, column = spot(j, k)
                whole[i, pl.ds(row, STRIP), :] = route0[step, unit][
                    at : at + STRIP, column : column + CHUNK
                ]
            turned[i] = whole[i].T
            column = pl.multiple_of(((y + step + 4) % 4) * GROUP, 128)
            start(turned.at[i], outs[name].at[pl.ds(first, CHUNK), pl.ds(column, GROUP)])
        for copy in started:
            copy.wait()

    @pl.when(c == 0)
    def _():
        lay(own, partner)

    @pl.when(c == 1)
    def _():
        lay(partner, own)


LAID = (
    ((0, 0), (0, 1), (0, 2)),
    ((-1, 0), (-1, 2), (1, 1)),
    ((1, 0), (1, 2)),
    ((2, 0), (2, 2)),
    ((-1, 1), (2, 1)),
)


def lay(work, mine, theirs, before):
    n = len(work)
    n_in = 0 if before is None else 3
    shapes = tuple(jax.ShapeDtypeStruct(SHAPES[name], jnp.bfloat16) for name in NAMES)
    keys = tuple(dict.fromkeys((s, u) for s, j in work for u in UNITS_OF[j]))
    units = [side[s][u] for side in (mine, theirs) for s, u in keys]
    return pl.pallas_call(
        lambda *refs: lay_kernel(work, keys, n_in, *refs),
        out_shape=shapes,
        in_specs=vmem(len(units)) + anywhere(n_in),
        out_specs=tuple(anywhere(3)),
        scratch_shapes=[
            pltpu.VMEM((n, GROUP, CHUNK), jnp.bfloat16),
            pltpu.VMEM((n, CHUNK, GROUP), jnp.bfloat16),
            pltpu.SemaphoreType.DMA((5 * n,)),
        ],
        input_output_aliases={len(units) + i: i for i in range(n_in)},
        compiler_params=pltpu.CompilerParams(vmem_limit_bytes=10 * 2**20),
    )(*held(units), *(before or ()))


STEPS = (0, -1, 1, 2)
VALUE_KEYS = tuple((s, u) for s in STEPS for u in UNITS_OF[0])


def value_kernel(*refs):
    n = len(VALUE_KEYS)
    own, partner, refs = dict(zip(VALUE_KEYS, refs)), dict(zip(VALUE_KEYS, refs[n:])), refs[2 * n :]
    out, whole, turned, sems = refs
    y, x, c = place()

    def gather(route1):
        for step in STEPS:
            g = (x + step + 4) % 4
            for k in range(4):
                row = pl.multiple_of(((y + k) % 4) * GROUP + g * STRIP, 16)
                unit, at, column = spot(0, k)
                whole[pl.ds(row, STRIP), :] = route1[step, unit][
                    at : at + STRIP, column : column + CHUNK
                ]

    @pl.when(c == 0)
    def _():
        gather(partner)

    @pl.when(c == 1)
    def _():
        gather(own)

    copies = []
    for s in range(4):
        turned[s] = whole[s * GROUP : (s + 1) * GROUP, :].T
        copy = pltpu.make_async_copy(turned.at[s], out.at[:, pl.ds(s * GROUP, GROUP)], sems.at[s])
        copy.start()
        copies.append(copy)
    for copy in copies:
        copy.wait()


def value_of(units):
    return pl.pallas_call(
        value_kernel,
        out_shape=jax.ShapeDtypeStruct((512, 3584), jnp.bfloat16),
        in_specs=vmem(2 * len(VALUE_KEYS)),
        out_specs=pl.BlockSpec(memory_space=pl.ANY),
        scratch_shapes=[
            pltpu.VMEM((3584, 512), jnp.bfloat16),
            pltpu.VMEM((4, 512, GROUP), jnp.bfloat16),
            pltpu.SemaphoreType.DMA((4,)),
        ],
        compiler_params=pltpu.CompilerParams(vmem_limit_bytes=10 * 2**20),
        name="value",
    )(*held(units))


def join_kernel(here, there, out):
    out[...] = known(here[...], there[...]).astype(jnp.bfloat16)


def norm_kernel(here, there, out, rows):
    found = known(here[...], there[...])
    for r in range(28):
        rows[r : r + 1, :] = found[r // 4 : r // 4 + 1, r % 4 * 128 : (r % 4 + 1) * 128]
    out[...] = rows[0:28, :].astype(jnp.bfloat16)


NEAR, ACROSS = (1, 0, 3, 2), (3, 2, 1, 0)


def along_first(partners):
    return pairs(lambda y, x, c: (y, partners[x], c) if c == 0 else (partners[y], x, c))


def norm_of(tile):
    moves = (
        (ZERO, PARTNER), (ZERO, along_first(NEAR)), (ZERO, along_first(ACROSS)),
        ("width", list(enumerate(NEAR))), ("width", list(enumerate(ACROSS))),
    )
    for k, (axis, move) in enumerate(moves):
        there = lax.ppermute(tile, axis, move)
        if k < 4:
            (tile,) = stack(join_kernel, (tile, there), (TILE,))
    return pl.pallas_call(
        norm_kernel,
        out_shape=jax.ShapeDtypeStruct((28, 128), jnp.bfloat16),
        in_specs=vmem(2),
        out_specs=pl.BlockSpec(memory_space=pltpu.VMEM),
        scratch_shapes=[pltpu.VMEM((32, 128), jnp.float32)],
        compiler_params=pltpu.CompilerParams(vmem_limit_bytes=2 * 2**20),
        name="norm",
    )(*held((tile, there))).reshape(-1)


def body(
    train_query,
    low_query,
    high_query,
    train_key,
    low_key,
    high_key,
    train_value,
    low_value,
    high_value,
    train_mixed,
    low_mixed,
    high_mixed,
    norm_train,
    norm_step,
):
    keep, give = merge(
        train_query,
        low_query.T,
        high_query,
        train_key,
        low_key.T,
        high_key,
        train_value,
        low_value.T,
        high_value,
        train_mixed.T,
        high_mixed,
        low_mixed.T,
        norm_train.reshape(1, NORM),
        norm_step.reshape(1, NORM),
    )
    beside = send(give, PARTNER)
    keep_up = send(keep, first_axis(1))
    give_down = send(give, first_axis_across(-1))
    keep_down = send(keep, first_axis(-1))
    give_up = send(give, first_axis_across(1))
    far_keep = send(keep_up, first_axis(1))
    far_give = send(give_down, first_axis(-1))
    pieces = (keep_up, keep_down, give_up, give_down, far_keep, far_give)
    (near,) = stack(near_kernel, pieces[:4], ((2 * STRIP, CHUNK),))
    shapes = ((REST, CHUNK), (REST + STRIP, CHUNK), TILE)
    *rest, tile = stack(rest_kernel, (*pieces, keep, beside), shapes)
    units = (near, *rest, pair_of(keep, beside))
    mine = {
        0: units,
        -1: [send(u, second_axis(1)) for u in units],
        1: [send(u, second_axis(-1)) for u in units],
    }
    mine[2] = [
        send(mine[-1][j], second_axis(1))
        if j in (0, 2)
        else send(mine[1][j], second_axis(-1))
        for j in range(4)
    ]
    theirs = {s: [send(u, PARTNER) for u in mine[s]] for s in STEPS}

    outs = None
    for work in LAID:
        outs = lay(work, mine, theirs, outs)
    ready_query, ready_key, ready_mixed = outs
    ready_value = value_of([side[s][u] for side in (mine, theirs) for s, u in VALUE_KEYS])

    serve_norm = norm_of(tile)
    return (ready_query, ready_key, ready_value, ready_mixed, serve_norm)


def solution(mesh):
    torus = Mesh(
        mesh.devices.reshape(4, 4, 2, mesh.shape["width"]), ("zero_0", "zero_1", "zero_2", "width")
    )
    return jax.shard_map(
        body,
        mesh=torus,
        in_specs=(
            P(ZERO, "width"),
            P(ZERO, None),
            P(None, "width"),
            P(ZERO, "width"),
            P(ZERO, None),
            P(None, "width"),
            P(ZERO, "width"),
            P(ZERO, None),
            P(None, "width"),
            P("width", ZERO),
            P("width", None),
            P(None, ZERO),
            P(ZERO_WIDTH),
            P(ZERO_WIDTH),
        ),
        out_specs=(P("width", None), P("width", None), P("width", None), P(None, "width"), P()),
        check_vma=False,
    )
```

time: 126 us -> 123 us (0.976)
  waiting for transfers between devices: 49.6 us -> 34.7 us
  starting transfers between devices: 58.7 us -> 70.6 us
    ppermute x35, starting transfers between devices: 38 us -> 60.3 us  [send(): return lax.ppermute(array, ZERO, to)]
    ppermute x35, waiting for transfers between devices: 41.3 us -> 29.9 us  [send(): return lax.ppermute(array, ZERO, to)]
    ppermute x8 -> x5, starting transfers between devices: 20.6 us -> 10.3 us  [norm_of(): there = lax.ppermute(tile, axis, move)]
    ppermute x8 -> x5, waiting for transfers between devices: 8.24 us -> 4.78 us  [norm_of(): there = lax.ppermute(tile, axis, move)]
    pallas_call x15 -> x13, Pallas kernels: 13.7 us -> 14 us  [the longest x5 11.3 us: lay(): pl.pallas_call(lambda *refs: lay_kernel(work, keys, n_in, *refs), out_sha...]
  transfers between devices with their start and end apart: 43 -> 40, of which waited for: 19 -> 15; matrix products, arithmetic and copies ran while one was open for 0% -> 0% of each run, Pallas kernels for 10% -> 10%
where the time goes in v2:
time: 123 us
  starting transfers between devices  70.6 us (57%)
  waiting for transfers between devices  34.7 us (28%)
  Pallas kernels  16.5 us (13%)
    ppermute x35, starting transfers between devices, send(): return lax.ppermute(array, ZERO, to)  60.3 us
    ppermute x35, waiting for transfers between devices, send(): return lax.ppermute(array, ZERO, to)  29.9 us
    pallas_call x5, Pallas kernels, lay(): pl.pallas_call(lambda *refs: lay_kernel(work, keys, n_in, *refs), out_sha...  11.3 us
    ppermute x5, starting transfers between devices, norm_of(): there = lax.ppermute(tile, axis, move)  10.3 us
    ppermute x5, waiting for transfers between devices, norm_of(): there = lax.ppermute(tile, axis, move)  4.78 us
  transfers between devices with their start and end apart: 40, of which 15 were waited for; matrix products, arithmetic and copies ran while one was open for 0% of the time, Pallas kernels for 10%

profile of v2, /device:TPU:1, one launch (start us, length us, event | category | flops | bytes accessed | tf_op | source)
XLA Modules:
  0.0 122.8 jit_solution(12211480585256795402)
XLA Ops:
  6.8 2.8 %collective-permute-start.3 = (bf16[120,1536]{1,0:T(8,128)(2,1)S(1)}, bf16[120,1536]{1,0:T(8,128)(2,1)S(1)}, u32[]{:S(2)}, u32[]{:S(2)}) collective-permute-start(bf16[120,1536]{1,0:T(8,128)(2,1)S(1)} %get-tuple-element.25.keep.refs_6_), channel_id=1, source_target_pairs={{0,24},{4,100},{8,0},{12,108},{16,8},{20,116},{24,16},{28,124},{32... | collective-permute-start | bytes 1105928 | tf_op jit(solution)/shard_map/ppermute | solution.py:64
  11.3 3.6 %collective-permute-done.5.refs_3_ = bf16[120,1536]{1,0:T(8,128)(2,1)S(1)} collective-permute-done((bf16[120,1536]{1,0:T(8,128)(2,1)S(1)}, bf16[120,1536]{1,0:T(8,128)(2,1)S(1)}, u32[]{:S(2)}, u32[]{:S(2)}) %collective-permute-start.5) | collective-permute-done | bytes 368672 | tf_op jit(solution)/shard_map/ppermute | solution.py:64
  20.7 2.7 %collective-permute-start.9 = (bf16[224,1536]{1,0:T(8,128)(2,1)S(1)}, bf16[224,1536]{1,0:T(8,128)(2,1)S(1)}, u32[]{:S(2)}, u32[]{:S(2)}) collective-permute-start(bf16[224,1536]{1,0:T(8,128)(2,1)S(1)} %pair.1.refs_0_), channel_id=1, source_target_pairs={{0,96},{4,28},{8,104},{12,4},{16,112},{20,12},{24,120},{28,20},{32... | collective-permute-start | bytes 2064392 | tf_op jit(solution)/shard_map/ppermute | solution.py:64
  23.4 6.2 %collective-permute-done.6.refs_4_ = bf16[120,1536]{1,0:T(8,128)(2,1)S(1)} collective-permute-done((bf16[120,1536]{1,0:T(8,128)(2,1)S(1)}, bf16[120,1536]{1,0:T(8,128)(2,1)S(1)}, u32[]{:S(2)}, u32[]{:S(2)}) %collective-permute-start.6) | collective-permute-done | bytes 368672 | tf_op jit(solution)/shard_map/ppermute | solution.py:64
  34.9 2.3 %collective-permute-start.37 = (bf16[8,512]{1,0:T(8,128)(2,1)S(1)}, bf16[8,512]{1,0:T(8,128)(2,1)S(1)}, u32[]{:S(2)}, u32[]{:S(2)}) collective-permute-start(bf16[8,512]{1,0:T(8,128)(2,1)S(1)} %shard_map.181.here), channel_id=1, source_target_pairs={{0,24},{4,100},{8,16},{12,108},{16,8},{20,116},{24,0},{28,124},{32... | collective-permute-start | bytes 24584 | tf_op jit(solution)/shard_map/ppermute | solution.py:370
  41.3 3.6 %collective-permute-start.39 = (bf16[8,512]{1,0:T(8,128)(2,1)S(1)}, bf16[8,512]{1,0:T(8,128)(2,1)S(1)}, u32[]{:S(2)}, u32[]{:S(2)}) collective-permute-start(bf16[8,512]{1,0:T(8,128)(2,1)S(1)} %shard_map.183.here), channel_id=1, source_target_pairs={{0,3},{1,2},{2,1},{3,0},{4,7},{5,6},{6,5},{7,4},{8,11},{9,10},{10,... | collective-permute-start | bytes 24584 | tf_op jit(solution)/shard_map/ppermute | solution.py:370
  44.9 2.8 %collective-permute-start.23 = (bf16[448,512]{1,0:T(8,128)(2,1)S(1)}, bf16[448,512]{1,0:T(8,128)(2,1)S(1)}, u32[]{:S(2)}, u32[]{:S(2)}) collective-permute-start(bf16[448,512]{1,0:T(8,128)(2,1)S(1)} %shard_map.174.refs_1_), channel_id=1, source_target_pairs={{0,96},{4,28},{8,104},{12,4},{16,112},{20,12},{24,120},{28,20},{32... | collective-permute-start | bytes 1376264 | tf_op jit(solution)/shard_map/ppermute | solution.py:64
  47.7 3.5 %collective-permute-start.32 = (bf16[448,512]{1,0:T(8,128)(2,1)S(1)}, bf16[448,512]{1,0:T(8,128)(2,1)S(1)}, u32[]{:S(2)}, u32[]{:S(2)}) collective-permute-start(bf16[448,512]{1,0:T(8,128)(2,1)S(1)} %shard_map.174.refs_1_), channel_id=1, source_target_pairs={{0,4},{4,0},{8,12},{12,8},{16,20},{20,16},{24,28},{28,24},{32,36},... | collective-permute-start | bytes 1376264 | tf_op jit(solution)/shard_map/ppermute | solution.py:64
  53.3 5.5 %collective-permute-start.28 = (bf16[448,512]{1,0:T(8,128)(2,1)S(1)}, bf16[448,512]{1,0:T(8,128)(2,1)S(1)}, u32[]{:S(2)}, u32[]{:S(2)}) collective-permute-start(bf16[448,512]{1,0:T(8,128)(2,1)S(1)} %collective-permute-done.17.refs_1_.refs_4_), channel_id=1, source_target_pairs={{0,4},{4,0},{8,12},{12,8},{16,20},{20,16},{24,28},{28,24},{32,36},... | collective-permute-start | bytes 1376264 | tf_op jit(solution)/shard_map/ppermute | solution.py:64
  59.3 3.1 %collective-permute-done.18.refs_1_.refs_10_ = bf16[448,512]{1,0:T(8,128)(2,1)S(1)} collective-permute-done((bf16[448,512]{1,0:T(8,128)(2,1)S(1)}, bf16[448,512]{1,0:T(8,128)(2,1)S(1)}, u32[]{:S(2)}, u32[]{:S(2)}) %collective-permute-start.18) | collective-permute-done | bytes 458784 | tf_op jit(solution)/shard_map/ppermute | solution.py:64
  63.9 2.4 %collective-permute-start.24 = (bf16[896,512]{1,0:T(8,128)(2,1)S(1)}, bf16[896,512]{1,0:T(8,128)(2,1)S(1)}, u32[]{:S(2)}, u32[]{:S(2)}) collective-permute-start(bf16[896,512]{1,0:T(8,128)(2,1)S(1)} %get-tuple-element.28.refs_2_), channel_id=1, source_target_pairs={{0,96},{4,28},{8,104},{12,4},{16,112},{20,12},{24,120},{28,20},{32... | collective-permute-start | bytes 2752520 | tf_op jit(solution)/shard_map/ppermute | solution.py:64
  66.2 6.3 %collective-permute-start.33 = (bf16[896,512]{1,0:T(8,128)(2,1)S(1)}, bf16[896,512]{1,0:T(8,128)(2,1)S(1)}, u32[]{:S(2)}, u32[]{:S(2)}) collective-permute-start(bf16[896,512]{1,0:T(8,128)(2,1)S(1)} %get-tuple-element.28.refs_2_), channel_id=1, source_target_pairs={{0,4},{4,0},{8,12},{12,8},{16,20},{20,16},{24,28},{28,24},{32,36},... | collective-permute-start | bytes 2752520 | tf_op jit(solution)/shard_map/ppermute | solution.py:64
  72.6 3.0 %collective-permute-start.10 = (bf16[224,1536]{1,0:T(8,128)(2,1)S(1)}, bf16[224,1536]{1,0:T(8,128)(2,1)S(1)}, u32[]{:S(2)}, u32[]{:S(2)}) collective-permute-start(bf16[224,1536]{1,0:T(8,128)(2,1)S(1)} %collective-permute-done.9.refs_3_.refs_0_.refs_6_), channel_id=1, source_target_pairs={{0,96},{4,28},{8,104},{12,4},{16,112},{20,12},{24,120},{28,20},{32... | collective-permute-start | bytes 2064392 | tf_op jit(solution)/shard_map/ppermute | solution.py:64
  75.5 5.1 %collective-permute-done.8.refs_1_ = bf16[672,512]{1,0:T(8,128)(2,1)S(1)} collective-permute-done((bf16[672,512]{1,0:T(8,128)(2,1)S(1)}, bf16[672,512]{1,0:T(8,128)(2,1)S(1)}, u32[]{:S(2)}, u32[]{:S(2)}) %collective-permute-start.8) | collective-permute-done | bytes 688160 | tf_op jit(solution)/shard_map/ppermute | solution.py:64
  80.7 3.9 %collective-permute-start.25 = (bf16[224,1536]{1,0:T(8,128)(2,1)S(1)}, bf16[224,1536]{1,0:T(8,128)(2,1)S(1)}, u32[]{:S(2)}, u32[]{:S(2)}) collective-permute-start(bf16[224,1536]{1,0:T(8,128)(2,1)S(1)} %collective-permute-done.9.refs_3_.refs_0_.refs_6_), channel_id=1, source_target_pairs={{0,4},{4,0},{8,12},{12,8},{16,20},{20,16},{24,28},{28,24},{32,36},... | collective-permute-start | bytes 2064392 | tf_op jit(solution)/shard_map/ppermute | solution.py:64
  84.6 3.5 %collective-permute-start.29 = (bf16[896,512]{1,0:T(8,128)(2,1)S(1)}, bf16[896,512]{1,0:T(8,128)(2,1)S(1)}, u32[]{:S(2)}, u32[]{:S(2)}) collective-permute-start(bf16[896,512]{1,0:T(8,128)(2,1)S(1)} %collective-permute-done.19.refs_2_.refs_5_), channel_id=1, source_target_pairs={{0,4},{4,0},{8,12},{12,8},{16,20},{20,16},{24,28},{28,24},{32,36},... | collective-permute-start | bytes 2752520 | tf_op jit(solution)/shard_map/ppermute | solution.py:64
  89.7 5.8 %collective-permute-start.27 = (bf16[896,512]{1,0:T(8,128)(2,1)S(1)}, bf16[896,512]{1,0:T(8,128)(2,1)S(1)}, u32[]{:S(2)}, u32[]{:S(2)}) collective-permute-start(bf16[896,512]{1,0:T(8,128)(2,1)S(1)} %collective-permute-done.24.refs_2_.refs_8_), channel_id=1, source_target_pairs={{0,4},{4,0},{8,12},{12,8},{16,20},{20,16},{24,28},{28,24},{32,36},... | collective-permute-start | bytes 2752520 | tf_op jit(solution)/shard_map/ppermute | solution.py:64
  95.5 3.0 %collective-permute-start.12 = (bf16[672,512]{1,0:T(8,128)(2,1)S(1)}, bf16[672,512]{1,0:T(8,128)(2,1)S(1)}, u32[]{:S(2)}, u32[]{:S(2)}) collective-permute-start(bf16[672,512]{1,0:T(8,128)(2,1)S(1)} %collective-permute-done.11.refs_4_), channel_id=1, source_target_pairs={{0,96},{4,28},{8,104},{12,4},{16,112},{20,12},{24,120},{28,20},{32... | collective-permute-start | bytes 2064392 | tf_op jit(solution)/shard_map/ppermute | solution.py:64
  98.6 4.1 %collective-permute-start.22 = (bf16[896,512]{1,0:T(8,128)(2,1)S(1)}, bf16[896,512]{1,0:T(8,128)(2,1)S(1)}, u32[]{:S(2)}, u32[]{:S(2)}) collective-permute-start(bf16[896,512]{1,0:T(8,128)(2,1)S(1)} %collective-permute-done.20.refs_2_.refs_11_), channel_id=1, source_target_pairs={{0,4},{4,0},{8,12},{12,8},{16,20},{20,16},{24,28},{28,24},{32,36},... | collective-permute-start | bytes 2752520 | tf_op jit(solution)/shard_map/ppermute | solution.py:64
  102.7 3.7 %collective-permute-done.12.refs_3_ = bf16[672,512]{1,0:T(8,128)(2,1)S(1)} collective-permute-done((bf16[672,512]{1,0:T(8,128)(2,1)S(1)}, bf16[672,512]{1,0:T(8,128)(2,1)S(1)}, u32[]{:S(2)}, u32[]{:S(2)}) %collective-permute-start.12) | collective-permute-done | bytes 688160 | tf_op jit(solution)/shard_map/ppermute | solution.py:64
  108.8 2.6 %shard_map.175 = (bf16[1024,3584]{1,0:T(8,128)(2,1)}, bf16[512,3584]{1,0:T(8,128)(2,1)}, bf16[3584,1024]{1,0:T(8,128)(2,1)}) custom-call(bf16[224,1536]{1,0:T(8,128)(2,1)S(1)} %pair.1.refs_0_, bf16[448,512]{1,0:T(8,128)(2,1)S(1)} %shard_map.174.refs_1_, bf16[896,512]{1,0:T(8,128)(2,1)S(1)} %get-tuple-element.28.refs_2_, ...), custom_call_target="tpu_custom_call" | custom-call | tf_op jit(solution)/shard_map/pallas_call | solution.py:277
  111.4 2.6 %shard_map.176 = (bf16[1024,3584]{1,0:T(8,128)(2,1)}, bf16[512,3584]{1,0:T(8,128)(2,1)}, bf16[3584,1024]{1,0:T(8,128)(2,1)}) custom-call(bf16[224,1536]{1,0:T(8,128)(2,1)S(1)} %collective-permute-done.1.refs_0_.refs_3_, bf16[448,512]{1,0:T(8,128)(2,1)S(1)} %collective-permute-done.17.refs_1_.refs_4_, ...), custom_call_target="tpu_custom_call", output_to_operand_aliasing={{0}: (10, {}), {1}: (11, {}), {2}: (12, {})} | custom-call | tf_op jit(solution)/shard_map/pallas_call | solution.py:277
  116.0 2.4 %value.1 = bf16[512,3584]{1,0:T(8,128)(2,1)} custom-call(bf16[224,1536]{1,0:T(8,128)(2,1)S(1)} %pair.1.refs_0_, bf16[448,512]{1,0:T(8,128)(2,1)S(1)} %shard_map.174.refs_1_, bf16[896,512]{1,0:T(8,128)(2,1)S(1)} %get-tuple-element.28.refs_2_, bf16[224,1536]{1,0:T(8,128)(2,1)S(1)} %collective-permute-done.1.refs_0_.refs_3_, ...), custom_call_target="tpu_custom_call" | custom-call | tf_op jit(solution)/shard_map/value/pallas_call | solution.py:331
  120.4 2.3 %shard_map.179 = (bf16[1024,3584]{1,0:T(8,128)(2,1)}, bf16[512,3584]{1,0:T(8,128)(2,1)}, bf16[3584,1024]{1,0:T(8,128)(2,1)}) custom-call(bf16[224,1536]{1,0:T(8,128)(2,1)S(1)} %collective-permute-done.1.refs_0_.refs_3_, bf16[672,512]{1,0:T(8,128)(2,1)S(1)} %collective-permute-done.8.refs_1_, ...), custom_call_target="tpu_custom_call", output_to_operand_aliasing={{0}: (8, {}), {1}: (9, {}), {2}: (10, {})} | custom-call | tf_op jit(solution)/shard_map/pallas_call | solution.py:277
  (71 shorter events, 35.3 us)
Async XLA Ops:
  4.7 10.2 %collective-permute-start.5 = (bf16[120,1536]{1,0:T(8,128)(2,1)S(1)}, bf16[120,1536]{1,0:T(8,128)(2,1)S(1)}, u32[]{:S(2)}, u32[]{:S(2)}) collective-permute-start(bf16[120,1536]{1,0:T(8,128)(2,1)S(1)} %get-tuple-element.26), channel_id=1, source_target_pairs={{0,100},{4,24},{8,108},{12,0},{16,116},{20,8},{24,124},{28,16},{32... | collective-permute-start | bytes 1105928 | tf_op jit(solution)/shard_map/ppermute | solution.py:64
  9.6 11.0 %collective-permute-start = (bf16[120,1536]{1,0:T(8,128)(2,1)S(1)}, bf16[120,1536]{1,0:T(8,128)(2,1)S(1)}, u32[]{:S(2)}, u32[]{:S(2)}) collective-permute-start(bf16[120,1536]{1,0:T(8,128)(2,1)S(1)} %get-tuple-element.26), channel_id=1, source_target_pairs={{0,4},{4,0},{8,12},{12,8},{16,20},{20,16},{24,28},{28,24},{32,36},... | collective-permute-start | bytes 1105928 | tf_op jit(solution)/shard_map/ppermute | solution.py:64
  17.8 33.4 %collective-permute-start.17 = (bf16[448,512]{1,0:T(8,128)(2,1)S(1)}, bf16[448,512]{1,0:T(8,128)(2,1)S(1)}, u32[]{:S(2)}, u32[]{:S(2)}) collective-permute-start(bf16[448,512]{1,0:T(8,128)(2,1)S(1)} %shard_map.174.refs_1_), channel_id=1, source_target_pairs={{0,32},{4,12},{8,40},{12,20},{16,48},{20,28},{24,56},{28,4},{32,64... | collective-permute-start | bytes 1376264 | tf_op jit(solution)/shard_map/ppermute | solution.py:64
  17.9 11.7 %collective-permute-start.6 = (bf16[120,1536]{1,0:T(8,128)(2,1)S(1)}, bf16[120,1536]{1,0:T(8,128)(2,1)S(1)}, u32[]{:S(2)}, u32[]{:S(2)}) collective-permute-start(bf16[120,1536]{1,0:T(8,128)(2,1)S(1)} %collective-permute-done.2.refs_0_), channel_id=1, source_target_pairs={{0,8},{4,36},{8,16},{12,44},{16,24},{20,52},{24,0},{28,60},{32,40}... | collective-permute-start | bytes 1105928 | tf_op jit(solution)/shard_map/ppermute | solution.py:64
  18.6 11.0 %collective-permute-start.7 = (bf16[120,1536]{1,0:T(8,128)(2,1)S(1)}, bf16[120,1536]{1,0:T(8,128)(2,1)S(1)}, u32[]{:S(2)}, u32[]{:S(2)}) collective-permute-start(bf16[120,1536]{1,0:T(8,128)(2,1)S(1)} %collective-permute-done.5.refs_3_), channel_id=1, source_target_pairs={{0,24},{4,100},{8,0},{12,108},{16,8},{20,116},{24,16},{28,124},{32... | collective-permute-start | bytes 1105928 | tf_op jit(solution)/shard_map/ppermute | solution.py:64
  20.7 38.0 %collective-permute-start.9 = (bf16[224,1536]{1,0:T(8,128)(2,1)S(1)}, bf16[224,1536]{1,0:T(8,128)(2,1)S(1)}, u32[]{:S(2)}, u32[]{:S(2)}) collective-permute-start(bf16[224,1536]{1,0:T(8,128)(2,1)S(1)} %pair.1.refs_0_), channel_id=1, source_target_pairs={{0,96},{4,28},{8,104},{12,4},{16,112},{20,12},{24,120},{28,20},{32... | collective-permute-start | bytes 2064392 | tf_op jit(solution)/shard_map/ppermute | solution.py:64
  23.4 35.5 %collective-permute-start.1 = (bf16[224,1536]{1,0:T(8,128)(2,1)S(1)}, bf16[224,1536]{1,0:T(8,128)(2,1)S(1)}, u32[]{:S(2)}, u32[]{:S(2)}) collective-permute-start(bf16[224,1536]{1,0:T(8,128)(2,1)S(1)} %pair.1.refs_0_), channel_id=1, source_target_pairs={{0,32},{4,12},{8,40},{12,20},{16,48},{20,28},{24,56},{28,4},{32,64... | collective-permute-start | bytes 2064392 | tf_op jit(solution)/shard_map/ppermute | solution.py:64
  53.3 10.3 %collective-permute-start.28 = (bf16[448,512]{1,0:T(8,128)(2,1)S(1)}, bf16[448,512]{1,0:T(8,128)(2,1)S(1)}, u32[]{:S(2)}, u32[]{:S(2)}) collective-permute-start(bf16[448,512]{1,0:T(8,128)(2,1)S(1)} %collective-permute-done.17.refs_1_.refs_4_), channel_id=1, source_target_pairs={{0,4},{4,0},{8,12},{12,8},{16,20},{20,16},{24,28},{28,24},{32,36},... | collective-permute-start | bytes 1376264 | tf_op jit(solution)/shard_map/ppermute | solution.py:64
  59.2 25.3 %collective-permute-start.19 = (bf16[896,512]{1,0:T(8,128)(2,1)S(1)}, bf16[896,512]{1,0:T(8,128)(2,1)S(1)}, u32[]{:S(2)}, u32[]{:S(2)}) collective-permute-start(bf16[896,512]{1,0:T(8,128)(2,1)S(1)} %get-tuple-element.28.refs_2_), channel_id=1, source_target_pairs={{0,32},{4,12},{8,40},{12,20},{16,48},{20,28},{24,56},{28,4},{32,64... | collective-permute-start | bytes 2752520 | tf_op jit(solution)/shard_map/ppermute | solution.py:64
  62.4 10.2 %collective-permute-start.11 = (bf16[672,512]{1,0:T(8,128)(2,1)S(1)}, bf16[672,512]{1,0:T(8,128)(2,1)S(1)}, u32[]{:S(2)}, u32[]{:S(2)}) collective-permute-start(bf16[672,512]{1,0:T(8,128)(2,1)S(1)} %get-tuple-element.27.refs_3_), channel_id=1, source_target_pairs={{0,96},{4,28},{8,104},{12,4},{16,112},{20,12},{24,120},{28,20},{32... | collective-permute-start | bytes 2064392 | tf_op jit(solution)/shard_map/ppermute | solution.py:64
  63.6 17.1 %collective-permute-start.8 = (bf16[672,512]{1,0:T(8,128)(2,1)S(1)}, bf16[672,512]{1,0:T(8,128)(2,1)S(1)}, u32[]{:S(2)}, u32[]{:S(2)}) collective-permute-start(bf16[672,512]{1,0:T(8,128)(2,1)S(1)} %get-tuple-element.27.refs_3_), channel_id=1, source_target_pairs={{0,32},{4,12},{8,40},{12,20},{16,48},{20,28},{24,56},{28,4},{32,64... | collective-permute-start | bytes 2064392 | tf_op jit(solution)/shard_map/ppermute | solution.py:64
  63.9 20.7 %collective-permute-start.24 = (bf16[896,512]{1,0:T(8,128)(2,1)S(1)}, bf16[896,512]{1,0:T(8,128)(2,1)S(1)}, u32[]{:S(2)}, u32[]{:S(2)}) collective-permute-start(bf16[896,512]{1,0:T(8,128)(2,1)S(1)} %get-tuple-element.28.refs_2_), channel_id=1, source_target_pairs={{0,96},{4,28},{8,104},{12,4},{16,112},{20,12},{24,120},{28,20},{32... | collective-permute-start | bytes 2752520 | tf_op jit(solution)/shard_map/ppermute | solution.py:64
  66.2 18.4 %collective-permute-start.33 = (bf16[896,512]{1,0:T(8,128)(2,1)S(1)}, bf16[896,512]{1,0:T(8,128)(2,1)S(1)}, u32[]{:S(2)}, u32[]{:S(2)}) collective-permute-start(bf16[896,512]{1,0:T(8,128)(2,1)S(1)} %get-tuple-element.28.refs_2_), channel_id=1, source_target_pairs={{0,4},{4,0},{8,12},{12,8},{16,20},{20,16},{24,28},{28,24},{32,36},... | collective-permute-start | bytes 2752520 | tf_op jit(solution)/shard_map/ppermute | solution.py:64
  72.6 17.1 %collective-permute-start.10 = (bf16[224,1536]{1,0:T(8,128)(2,1)S(1)}, bf16[224,1536]{1,0:T(8,128)(2,1)S(1)}, u32[]{:S(2)}, u32[]{:S(2)}) collective-permute-start(bf16[224,1536]{1,0:T(8,128)(2,1)S(1)} %collective-permute-done.9.refs_3_.refs_0_.refs_6_), channel_id=1, source_target_pairs={{0,96},{4,28},{8,104},{12,4},{16,112},{20,12},{24,120},{28,20},{32... | collective-permute-start | bytes 2064392 | tf_op jit(solution)/shard_map/ppermute | solution.py:64
  80.7 14.8 %collective-permute-start.25 = (bf16[224,1536]{1,0:T(8,128)(2,1)S(1)}, bf16[224,1536]{1,0:T(8,128)(2,1)S(1)}, u32[]{:S(2)}, u32[]{:S(2)}) collective-permute-start(bf16[224,1536]{1,0:T(8,128)(2,1)S(1)} %collective-permute-done.9.refs_3_.refs_0_.refs_6_), channel_id=1, source_target_pairs={{0,4},{4,0},{8,12},{12,8},{16,20},{20,16},{24,28},{28,24},{32,36},... | collective-permute-start | bytes 2064392 | tf_op jit(solution)/shard_map/ppermute | solution.py:64
  84.5 10.9 %collective-permute-start.13 = (bf16[224,1536]{1,0:T(8,128)(2,1)S(1)}, bf16[224,1536]{1,0:T(8,128)(2,1)S(1)}, u32[]{:S(2)}, u32[]{:S(2)}) collective-permute-start(bf16[224,1536]{1,0:T(8,128)(2,1)S(1)} %collective-permute-done.1.refs_0_.refs_3_), channel_id=1, source_target_pairs={{0,4},{4,0},{8,12},{12,8},{16,20},{20,16},{24,28},{28,24},{32,36},... | collective-permute-start | bytes 2064392 | tf_op jit(solution)/shard_map/ppermute | solution.py:64
  84.5 14.1 %collective-permute-start.20 = (bf16[896,512]{1,0:T(8,128)(2,1)S(1)}, bf16[896,512]{1,0:T(8,128)(2,1)S(1)}, u32[]{:S(2)}, u32[]{:S(2)}) collective-permute-start(bf16[896,512]{1,0:T(8,128)(2,1)S(1)} %collective-permute-done.19.refs_2_.refs_5_), channel_id=1, source_target_pairs={{0,32},{4,12},{8,40},{12,20},{16,48},{20,28},{24,56},{28,4},{32,64... | collective-permute-start | bytes 2752520 | tf_op jit(solution)/shard_map/ppermute | solution.py:64
  84.6 23.0 %collective-permute-start.29 = (bf16[896,512]{1,0:T(8,128)(2,1)S(1)}, bf16[896,512]{1,0:T(8,128)(2,1)S(1)}, u32[]{:S(2)}, u32[]{:S(2)}) collective-permute-start(bf16[896,512]{1,0:T(8,128)(2,1)S(1)} %collective-permute-done.19.refs_2_.refs_5_), channel_id=1, source_target_pairs={{0,4},{4,0},{8,12},{12,8},{16,20},{20,16},{24,28},{28,24},{32,36},... | collective-permute-start | bytes 2752520 | tf_op jit(solution)/shard_map/ppermute | solution.py:64
  89.7 18.0 %collective-permute-start.27 = (bf16[896,512]{1,0:T(8,128)(2,1)S(1)}, bf16[896,512]{1,0:T(8,128)(2,1)S(1)}, u32[]{:S(2)}, u32[]{:S(2)}) collective-permute-start(bf16[896,512]{1,0:T(8,128)(2,1)S(1)} %collective-permute-done.24.refs_2_.refs_8_), channel_id=1, source_target_pairs={{0,4},{4,0},{8,12},{12,8},{16,20},{20,16},{24,28},{28,24},{32,36},... | collective-permute-start | bytes 2752520 | tf_op jit(solution)/shard_map/ppermute | solution.py:64
  95.5 10.9 %collective-permute-start.12 = (bf16[672,512]{1,0:T(8,128)(2,1)S(1)}, bf16[672,512]{1,0:T(8,128)(2,1)S(1)}, u32[]{:S(2)}, u32[]{:S(2)}) collective-permute-start(bf16[672,512]{1,0:T(8,128)(2,1)S(1)} %collective-permute-done.11.refs_4_), channel_id=1, source_target_pairs={{0,96},{4,28},{8,104},{12,4},{16,112},{20,12},{24,120},{28,20},{32... | collective-permute-start | bytes 2064392 | tf_op jit(solution)/shard_map/ppermute | solution.py:64
  98.6 17.3 %collective-permute-start.22 = (bf16[896,512]{1,0:T(8,128)(2,1)S(1)}, bf16[896,512]{1,0:T(8,128)(2,1)S(1)}, u32[]{:S(2)}, u32[]{:S(2)}) collective-permute-start(bf16[896,512]{1,0:T(8,128)(2,1)S(1)} %collective-permute-done.20.refs_2_.refs_11_), channel_id=1, source_target_pairs={{0,4},{4,0},{8,12},{12,8},{16,20},{20,16},{24,28},{28,24},{32,36},... | collective-permute-start | bytes 2752520 | tf_op jit(solution)/shard_map/ppermute | solution.py:64
  102.7 13.3 %collective-permute-start.15 = (bf16[224,1536]{1,0:T(8,128)(2,1)S(1)}, bf16[224,1536]{1,0:T(8,128)(2,1)S(1)}, u32[]{:S(2)}, u32[]{:S(2)}) collective-permute-start(bf16[224,1536]{1,0:T(8,128)(2,1)S(1)} %collective-permute-done.10.refs_0_.refs_2_.refs_9_), channel_id=1, source_target_pairs={{0,4},{4,0},{8,12},{12,8},{16,20},{20,16},{24,28},{28,24},{32,36},... | collective-permute-start | bytes 2064392 | tf_op jit(solution)/shard_map/ppermute | solution.py:64
  106.4 14.0 %collective-permute-start.14 = (bf16[672,512]{1,0:T(8,128)(2,1)S(1)}, bf16[672,512]{1,0:T(8,128)(2,1)S(1)}, u32[]{:S(2)}, u32[]{:S(2)}) collective-permute-start(bf16[672,512]{1,0:T(8,128)(2,1)S(1)} %collective-permute-done.8.refs_1_), channel_id=1, source_target_pairs={{0,4},{4,0},{8,12},{12,8},{16,20},{20,16},{24,28},{28,24},{32,36},... | collective-permute-start | bytes 2064392 | tf_op jit(solution)/shard_map/ppermute | solution.py:64
  107.7 12.7 %collective-permute-start.16 = (bf16[672,512]{1,0:T(8,128)(2,1)S(1)}, bf16[672,512]{1,0:T(8,128)(2,1)S(1)}, u32[]{:S(2)}, u32[]{:S(2)}) collective-permute-start(bf16[672,512]{1,0:T(8,128)(2,1)S(1)} %collective-permute-done.12.refs_3_), channel_id=1, source_target_pairs={{0,4},{4,0},{8,12},{12,8},{16,20},{20,16},{24,28},{28,24},{32,36},... | collective-permute-start | bytes 2064392 | tf_op jit(solution)/shard_map/ppermute | solution.py:64
  (16 other events, 103.5 us)

commit v3 on v2

--- a/solution.py
+++ b/solution.py
@@ -15,6 +15,7 @@
 ROWS = 112
 HALF = 1536
 CHUNK = 512
+PART = 128
 GROUP = 8 * ROWS
 STRIP = 2 * ROWS
 REST = 3 * STRIP
@@ -211,9 +212,10 @@
 SHAPES = {"query": (1024, 3584), "key": (512, 3584), "mixed": (3584, 1024)}
 
 
-def lay_kernel(work, keys, n_in, *refs):
+def lay_kernel(work, sides, keys, n_in, *refs):
     n = len(keys)
-    own, partner, refs = dict(zip(keys, refs)), dict(zip(keys, refs[n:])), refs[2 * n + n_in :]
+    units = {side: dict(zip(keys, refs[i * n :])) for i, side in enumerate(sides)}
+    own, partner, refs = units.get("own"), units.get("partner"), refs[len(sides) * n + n_in :]
     outs, (whole, turned, sems) = dict(zip(NAMES, refs[:3])), refs[3:]
     y, x, c = place()
 
@@ -225,7 +227,7 @@
             copy.start()
             started.append(copy)
 
-        for step, j in work:
+        for step, j in work if route1 else ():
             name, first = ROUTE1[j]
             if name == "mixed":
                 g = (x + step + 4) % 4
@@ -236,7 +238,7 @@
                         route1[step, unit].at[pl.ds(at, STRIP), pl.ds(column, CHUNK)],
                         outs[name].at[pl.ds(row, STRIP), pl.ds(first, CHUNK)],
                     )
-        for i, (step, j) in enumerate(work):
+        for i, (step, j) in enumerate(work if route0 else ()):
             name, first = ROUTE0[j]
             for k in range(4):
                 row = pl.multiple_of(((x + k) % 4) * STRIP, 16)
@@ -244,9 +246,13 @@
                 whole[i, pl.ds(row, STRIP), :] = route0[step, unit][
                     at : at + STRIP, column : column + CHUNK
                 ]
-            turned[i] = whole[i].T
             column = pl.multiple_of(((y + step + 4) % 4) * GROUP, 128)
-            start(turned.at[i], outs[name].at[pl.ds(first, CHUNK), pl.ds(column, GROUP)])
+            for at in range(0, CHUNK, PART):
+                turned[i, at : at + PART, :] = whole[i, :, at : at + PART].T
+                start(
+                    turned.at[i, pl.ds(at, PART), :],
+                    outs[name].at[pl.ds(first + at, PART), pl.ds(column, GROUP)],
+                )
         for copy in started:
             copy.wait()
 
@@ -259,30 +265,34 @@
         lay(partner, own)
 
 
+BOTH = ("own", "partner")
 LAID = (
-    ((0, 0), (0, 1), (0, 2)),
-    ((-1, 0), (-1, 2), (1, 1)),
-    ((1, 0), (1, 2)),
-    ((2, 0), (2, 2)),
-    ((-1, 1), (2, 1)),
+    (((0, 0), (0, 1), (0, 2)), BOTH),
+    (((-1, 0), (-1, 2), (1, 1)), BOTH),
+    (((1, 0), (1, 2)), BOTH),
+    (((2, 0), (2, 2)), BOTH),
+    (((-1, 1), (2, 1)), ("own",)),
+    (((-1, 1),), ("partner",)),
+    (((2, 1),), ("partner",)),
 )
 
 
-def lay(work, mine, theirs, before):
+def lay(work, sides, mine, theirs, before):
     n = len(work)
     n_in = 0 if before is None else 3
     shapes = tuple(jax.ShapeDtypeStruct(SHAPES[name], jnp.bfloat16) for name in NAMES)
     keys = tuple(dict.fromkeys((s, u) for s, j in work for u in UNITS_OF[j]))
-    units = [side[s][u] for side in (mine, theirs) for s, u in keys]
-    return pl.pallas_call(
-        lambda *refs: lay_kernel(work, keys, n_in, *refs),
+    by_side = {"own": mine, "partner": theirs}
+    units = [by_side[side][s][u] for side in sides for s, u in keys]
+    return pl.pallas_call(
+        lambda *refs: lay_kernel(work, sides, keys, n_in, *refs),
         out_shape=shapes,
         in_specs=vmem(len(units)) + anywhere(n_in),
         out_specs=tuple(anywhere(3)),
         scratch_shapes=[
             pltpu.VMEM((n, GROUP, CHUNK), jnp.bfloat16),
             pltpu.VMEM((n, CHUNK, GROUP), jnp.bfloat16),
-            pltpu.SemaphoreType.DMA((5 * n,)),
+            pltpu.SemaphoreType.DMA((8 * n,)),
         ],
         input_output_aliases={len(units) + i: i for i in range(n_in)},
         compiler_params=pltpu.CompilerParams(vmem_limit_bytes=10 * 2**20),
@@ -363,8 +373,8 @@
 
 def norm_of(tile):
     moves = (
+        ("width", list(enumerate(ACROSS))), ("width", list(enumerate(NEAR))),
         (ZERO, PARTNER), (ZERO, along_first(NEAR)), (ZERO, along_first(ACROSS)),
-        ("width", list(enumerate(NEAR))), ("width", list(enumerate(ACROSS))),
     )
     for k, (axis, move) in enumerate(moves):
         there = lax.ppermute(tile, axis, move)
@@ -439,8 +449,8 @@
     theirs = {s: [send(u, PARTNER) for u in mine[s]] for s in STEPS}
 
     outs = None
-    for work in LAID:
-        outs = lay(work, mine, theirs, outs)
+    for work, sides in LAID:
+        outs = lay(work, sides, mine, theirs, outs)
     ready_query, ready_key, ready_mixed = outs
     ready_value = value_of([side[s][u] for side in (mine, theirs) for s, u in VALUE_KEYS])
 

time: 123 us -> 121 us (0.984)
  starting transfers between devices: 70.6 us -> 49.8 us
  waiting for transfers between devices: 34.7 us -> 52.4 us
    ppermute x35, starting transfers between devices: 60.3 us -> 39.3 us  [send(): return lax.ppermute(array, ZERO, to)]
    ppermute x35, waiting for transfers between devices: 29.9 us -> 44.3 us  [send(): return lax.ppermute(array, ZERO, to)]
    ppermute x5, waiting for transfers between devices: 4.78 us -> 8.1 us  [norm_of(): there = lax.ppermute(tile, axis, move)]
    pallas_call x5 -> x7, Pallas kernels: 11.3 us -> 12.2 us  [lay(): pl.pallas_call(lambda *refs: lay_kernel(work, sides, keys, n_in, *refs),...]
  transfers between devices with their start and end apart: 40 -> 40, of which waited for: 15 -> 20; matrix products, arithmetic and copies ran while one was open for 0% -> 0% of each run, Pallas kernels for 10% -> 12%
where the time goes in v3:
time: 121 us; the launch traced here: 120 us
  waiting for transfers between devices  52.4 us (43%)
  starting transfers between devices  49.8 us (41%)
  Pallas kernels  17.3 us (14%)
    ppermute x35, waiting for transfers between devices, send(): return lax.ppermute(array, ZERO, to)  44.3 us
    ppermute x35, starting transfers between devices, send(): return lax.ppermute(array, ZERO, to)  39.3 us
    pallas_call x7, Pallas kernels, lay(): pl.pallas_call(lambda *refs: lay_kernel(work, sides, keys, n_in, *refs),...  12.2 us
    ppermute x5, starting transfers between devices, norm_of(): there = lax.ppermute(tile, axis, move)  10.5 us
    ppermute x5, waiting for transfers between devices, norm_of(): there = lax.ppermute(tile, axis, move)  8.1 us
    pallas_call x1, Pallas kernels, value_of(): pl.pallas_call(value_kernel, out_shape=jax.ShapeDtypeStruct((512, 3584),...  2.44 us
  transfers between devices with their start and end apart: 40, of which 20 were waited for; matrix products, arithmetic and copies ran while one was open for 0% of the time, Pallas kernels for 12%

profile of v3, /device:TPU:1, one launch (start us, length us, event | category | flops | bytes accessed | tf_op | source)
XLA Modules:
  0.0 120.4 jit_solution(1896820809269817083)
XLA Ops:
  2.5 2.2 %collective-permute-start.4 = (bf16[120,1536]{1,0:T(8,128)(2,1)S(1)}, bf16[120,1536]{1,0:T(8,128)(2,1)S(1)}, u32[]{:S(2)}, u32[]{:S(2)}) collective-permute-start(bf16[120,1536]{1,0:T(8,128)(2,1)S(1)} %get-tuple-element.31.keep.refs_6_), channel_id=1, source_target_pairs={{0,8},{4,36},{8,16},{12,44},{16,24},{20,52},{24,0},{28,60},{32,40}... | collective-permute-start | bytes 1105928 | tf_op jit(solution)/shard_map/ppermute | solution.py:65
  4.7 2.0 %collective-permute-start.7 = (bf16[120,1536]{1,0:T(8,128)(2,1)S(1)}, bf16[120,1536]{1,0:T(8,128)(2,1)S(1)}, u32[]{:S(2)}, u32[]{:S(2)}) collective-permute-start(bf16[120,1536]{1,0:T(8,128)(2,1)S(1)} %get-tuple-element.32), channel_id=1, source_target_pairs={{0,100},{4,24},{8,108},{12,0},{16,116},{20,8},{24,124},{28,16},{32... | collective-permute-start | bytes 1105928 | tf_op jit(solution)/shard_map/ppermute | solution.py:65
  6.8 2.8 %collective-permute-start.5 = (bf16[120,1536]{1,0:T(8,128)(2,1)S(1)}, bf16[120,1536]{1,0:T(8,128)(2,1)S(1)}, u32[]{:S(2)}, u32[]{:S(2)}) collective-permute-start(bf16[120,1536]{1,0:T(8,128)(2,1)S(1)} %get-tuple-element.31.keep.refs_6_), channel_id=1, source_target_pairs={{0,24},{4,100},{8,0},{12,108},{16,8},{20,116},{24,16},{28,124},{32... | collective-permute-start | bytes 1105928 | tf_op jit(solution)/shard_map/ppermute | solution.py:65
  11.3 3.6 %collective-permute-done.7.refs_3_ = bf16[120,1536]{1,0:T(8,128)(2,1)S(1)} collective-permute-done((bf16[120,1536]{1,0:T(8,128)(2,1)S(1)}, bf16[120,1536]{1,0:T(8,128)(2,1)S(1)}, u32[]{:S(2)}, u32[]{:S(2)}) %collective-permute-start.7) | collective-permute-done | bytes 368672 | tf_op jit(solution)/shard_map/ppermute | solution.py:65
  18.1 2.5 %collective-permute-start.9 = (bf16[120,1536]{1,0:T(8,128)(2,1)S(1)}, bf16[120,1536]{1,0:T(8,128)(2,1)S(1)}, u32[]{:S(2)}, u32[]{:S(2)}) collective-permute-start(bf16[120,1536]{1,0:T(8,128)(2,1)S(1)} %collective-permute-done.7.refs_3_), channel_id=1, source_target_pairs={{0,24},{4,100},{8,0},{12,108},{16,8},{20,116},{24,16},{28,124},{32... | collective-permute-start | bytes 1105928 | tf_op jit(solution)/shard_map/ppermute | solution.py:65
  22.2 3.6 %collective-permute-done.8.refs_4_ = bf16[120,1536]{1,0:T(8,128)(2,1)S(1)} collective-permute-done((bf16[120,1536]{1,0:T(8,128)(2,1)S(1)}, bf16[120,1536]{1,0:T(8,128)(2,1)S(1)}, u32[]{:S(2)}, u32[]{:S(2)}) %collective-permute-start.8) | collective-permute-done | bytes 368672 | tf_op jit(solution)/shard_map/ppermute | solution.py:65
  26.2 3.8 %collective-permute-start.35 = (bf16[8,512]{1,0:T(8,128)(2,1)S(1)}, bf16[8,512]{1,0:T(8,128)(2,1)S(1)}, u32[]{:S(2)}, u32[]{:S(2)}) collective-permute-start(bf16[8,512]{1,0:T(8,128)(2,1)S(1)} %get-tuple-element.56.here), channel_id=1, source_target_pairs={{0,3},{1,2},{2,1},{3,0},{4,7},{5,6},{6,5},{7,4},{8,11},{9,10},{10,... | collective-permute-start | bytes 24584 | tf_op jit(solution)/shard_map/ppermute | solution.py:380
  31.1 2.5 %collective-permute-done.36.there = bf16[8,512]{1,0:T(8,128)(2,1)S(1)} collective-permute-done((bf16[8,512]{1,0:T(8,128)(2,1)S(1)}, bf16[8,512]{1,0:T(8,128)(2,1)S(1)}, u32[]{:S(2)}, u32[]{:S(2)}) %collective-permute-start.36) | collective-permute-done | bytes 8224 | tf_op jit(solution)/shard_map/ppermute | solution.py:380
  33.6 6.1 %collective-permute-start.37 = (bf16[8,512]{1,0:T(8,128)(2,1)S(1)}, bf16[8,512]{1,0:T(8,128)(2,1)S(1)}, u32[]{:S(2)}, u32[]{:S(2)}) collective-permute-start(bf16[8,512]{1,0:T(8,128)(2,1)S(1)} %shard_map.183.here), channel_id=1, source_target_pairs={{0,4},{4,0},{8,12},{12,8},{16,20},{20,16},{24,28},{28,24},{32,36},... | collective-permute-start | bytes 24584 | tf_op jit(solution)/shard_map/ppermute | solution.py:380
  40.6 2.5 %collective-permute-done.38.there = bf16[8,512]{1,0:T(8,128)(2,1)S(1)} collective-permute-done((bf16[8,512]{1,0:T(8,128)(2,1)S(1)}, bf16[8,512]{1,0:T(8,128)(2,1)S(1)}, u32[]{:S(2)}, u32[]{:S(2)}) %collective-permute-start.38) | collective-permute-done | bytes 8224 | tf_op jit(solution)/shard_map/ppermute | solution.py:380
  43.6 2.0 %collective-permute-start.17 = (bf16[448,512]{1,0:T(8,128)(2,1)S(1)}, bf16[448,512]{1,0:T(8,128)(2,1)S(1)}, u32[]{:S(2)}, u32[]{:S(2)}) collective-permute-start(bf16[448,512]{1,0:T(8,128)(2,1)S(1)} %shard_map.174.refs_1_), channel_id=1, source_target_pairs={{0,32},{4,12},{8,40},{12,20},{16,48},{20,28},{24,56},{28,4},{32,64... | collective-permute-start | bytes 1376264 | tf_op jit(solution)/shard_map/ppermute | solution.py:65
  46.8 3.4 %collective-permute-start.23 = (bf16[448,512]{1,0:T(8,128)(2,1)S(1)}, bf16[448,512]{1,0:T(8,128)(2,1)S(1)}, u32[]{:S(2)}, u32[]{:S(2)}) collective-permute-start(bf16[448,512]{1,0:T(8,128)(2,1)S(1)} %shard_map.174.refs_1_), channel_id=1, source_target_pairs={{0,96},{4,28},{8,104},{12,4},{16,112},{20,12},{24,120},{28,20},{32... | collective-permute-start | bytes 1376264 | tf_op jit(solution)/shard_map/ppermute | solution.py:65
  50.2 3.0 %collective-permute-done.17.refs_1_.refs_4_ = bf16[448,512]{1,0:T(8,128)(2,1)S(1)} collective-permute-done((bf16[448,512]{1,0:T(8,128)(2,1)S(1)}, bf16[448,512]{1,0:T(8,128)(2,1)S(1)}, u32[]{:S(2)}, u32[]{:S(2)}) %collective-permute-start.17) | collective-permute-done | bytes 458784 | tf_op jit(solution)/shard_map/ppermute | solution.py:65
  53.3 4.7 %collective-permute-start.28 = (bf16[448,512]{1,0:T(8,128)(2,1)S(1)}, bf16[448,512]{1,0:T(8,128)(2,1)S(1)}, u32[]{:S(2)}, u32[]{:S(2)}) collective-permute-start(bf16[448,512]{1,0:T(8,128)(2,1)S(1)} %collective-permute-done.17.refs_1_.refs_4_), channel_id=1, source_target_pairs={{0,4},{4,0},{8,12},{12,8},{16,20},{20,16},{24,28},{28,24},{32,36},... | collective-permute-start | bytes 1376264 | tf_op jit(solution)/shard_map/ppermute | solution.py:65
  58.6 2.9 %collective-permute-done.13.refs_0_.refs_3_ = bf16[224,1536]{1,0:T(8,128)(2,1)S(1)} collective-permute-done((bf16[224,1536]{1,0:T(8,128)(2,1)S(1)}, bf16[224,1536]{1,0:T(8,128)(2,1)S(1)}, u32[]{:S(2)}, u32[]{:S(2)}) %collective-permute-start.13) | collective-permute-done | bytes 688160 | tf_op jit(solution)/shard_map/ppermute | solution.py:65
  61.5 3.8 %collective-permute-start.33 = (bf16[896,512]{1,0:T(8,128)(2,1)S(1)}, bf16[896,512]{1,0:T(8,128)(2,1)S(1)}, u32[]{:S(2)}, u32[]{:S(2)}) collective-permute-start(bf16[896,512]{1,0:T(8,128)(2,1)S(1)} %get-tuple-element.34.refs_2_), channel_id=1, source_target_pairs={{0,4},{4,0},{8,12},{12,8},{16,20},{20,16},{24,28},{28,24},{32,36},... | collective-permute-start | bytes 2752520 | tf_op jit(solution)/shard_map/ppermute | solution.py:65
  67.5 2.7 %collective-permute-start.24 = (bf16[896,512]{1,0:T(8,128)(2,1)S(1)}, bf16[896,512]{1,0:T(8,128)(2,1)S(1)}, u32[]{:S(2)}, u32[]{:S(2)}) collective-permute-start(bf16[896,512]{1,0:T(8,128)(2,1)S(1)} %get-tuple-element.34.refs_2_), channel_id=1, source_target_pairs={{0,96},{4,28},{8,104},{12,4},{16,112},{20,12},{24,120},{28,20},{32... | collective-permute-start | bytes 2752520 | tf_op jit(solution)/shard_map/ppermute | solution.py:65
  70.2 5.2 %collective-permute-done.10.refs_4_ = bf16[672,512]{1,0:T(8,128)(2,1)S(1)} collective-permute-done((bf16[672,512]{1,0:T(8,128)(2,1)S(1)}, bf16[672,512]{1,0:T(8,128)(2,1)S(1)}, u32[]{:S(2)}, u32[]{:S(2)}) %collective-permute-start.10) | collective-permute-done | bytes 688160 | tf_op jit(solution)/shard_map/ppermute | solution.py:65
  78.4 8.5 %collective-permute-done.19.refs_2_.refs_5_ = bf16[896,512]{1,0:T(8,128)(2,1)S(1)} collective-permute-done((bf16[896,512]{1,0:T(8,128)(2,1)S(1)}, bf16[896,512]{1,0:T(8,128)(2,1)S(1)}, u32[]{:S(2)}, u32[]{:S(2)}) %collective-permute-start.19) | collective-permute-done | bytes 917536 | tf_op jit(solution)/shard_map/ppermute | solution.py:65
  88.7 4.0 %collective-permute-done.2.refs_0_.refs_2_.refs_9_ = bf16[224,1536]{1,0:T(8,128)(2,1)S(1)} collective-permute-done((bf16[224,1536]{1,0:T(8,128)(2,1)S(1)}, bf16[224,1536]{1,0:T(8,128)(2,1)S(1)}, u32[]{:S(2)}, u32[]{:S(2)}) %collective-permute-start.2) | collective-permute-done | bytes 688160 | tf_op jit(solution)/shard_map/ppermute | solution.py:65
  94.3 6.4 %collective-permute-done.20.refs_2_.refs_11_ = bf16[896,512]{1,0:T(8,128)(2,1)S(1)} collective-permute-done((bf16[896,512]{1,0:T(8,128)(2,1)S(1)}, bf16[896,512]{1,0:T(8,128)(2,1)S(1)}, u32[]{:S(2)}, u32[]{:S(2)}) %collective-permute-start.20) | collective-permute-done | bytes 917536 | tf_op jit(solution)/shard_map/ppermute | solution.py:65
  105.6 2.4 %shard_map.175 = (bf16[1024,3584]{1,0:T(8,128)(2,1)}, bf16[512,3584]{1,0:T(8,128)(2,1)}, bf16[3584,1024]{1,0:T(8,128)(2,1)}) custom-call(bf16[224,1536]{1,0:T(8,128)(2,1)S(1)} %pair.1.refs_0_, bf16[448,512]{1,0:T(8,128)(2,1)S(1)} %shard_map.174.refs_1_, bf16[896,512]{1,0:T(8,128)(2,1)S(1)} %get-tuple-element.34.refs_2_, ...), custom_call_target="tpu_custom_call" | custom-call | tf_op jit(solution)/shard_map/pallas_call | solution.py:287
  108.0 2.4 %shard_map.176 = (bf16[1024,3584]{1,0:T(8,128)(2,1)}, bf16[512,3584]{1,0:T(8,128)(2,1)}, bf16[3584,1024]{1,0:T(8,128)(2,1)}) custom-call(bf16[224,1536]{1,0:T(8,128)(2,1)S(1)} %collective-permute-done.13.refs_0_.refs_3_, bf16[448,512]{1,0:T(8,128)(2,1)S(1)} %collective-permute-done.17.refs_1_.refs_4_, ...), custom_call_target="tpu_custom_call", output_to_operand_aliasing={{0}: (10, {}), {1}: (11, {}), {2}: (12, {})} | custom-call | tf_op jit(solution)/shard_map/pallas_call | solution.py:287
  112.2 2.4 %value.1 = bf16[512,3584]{1,0:T(8,128)(2,1)} custom-call(bf16[224,1536]{1,0:T(8,128)(2,1)S(1)} %pair.1.refs_0_, bf16[448,512]{1,0:T(8,128)(2,1)S(1)} %shard_map.174.refs_1_, bf16[896,512]{1,0:T(8,128)(2,1)S(1)} %get-tuple-element.34.refs_2_, bf16[224,1536]{1,0:T(8,128)(2,1)S(1)} %collective-permute-done.13.refs_0_.refs_3_, ...), custom_call_target="tpu_custom_call" | custom-call | tf_op jit(solution)/shard_map/value/pallas_call | solution.py:341
  (73 shorter events, 33.8 us)
Async XLA Ops:
  4.7 10.2 %collective-permute-start.7 = (bf16[120,1536]{1,0:T(8,128)(2,1)S(1)}, bf16[120,1536]{1,0:T(8,128)(2,1)S(1)}, u32[]{:S(2)}, u32[]{:S(2)}) collective-permute-start(bf16[120,1536]{1,0:T(8,128)(2,1)S(1)} %get-tuple-element.32), channel_id=1, source_target_pairs={{0,100},{4,24},{8,108},{12,0},{16,116},{20,8},{24,124},{28,16},{32... | collective-permute-start | bytes 1105928 | tf_op jit(solution)/shard_map/ppermute | solution.py:65
  9.6 11.0 %collective-permute-start = (bf16[120,1536]{1,0:T(8,128)(2,1)S(1)}, bf16[120,1536]{1,0:T(8,128)(2,1)S(1)}, u32[]{:S(2)}, u32[]{:S(2)}) collective-permute-start(bf16[120,1536]{1,0:T(8,128)(2,1)S(1)} %get-tuple-element.32), channel_id=1, source_target_pairs={{0,4},{4,0},{8,12},{12,8},{16,20},{20,16},{24,28},{28,24},{32,36},... | collective-permute-start | bytes 1105928 | tf_op jit(solution)/shard_map/ppermute | solution.py:65
  17.8 32.4 %collective-permute-start.32 = (bf16[448,512]{1,0:T(8,128)(2,1)S(1)}, bf16[448,512]{1,0:T(8,128)(2,1)S(1)}, u32[]{:S(2)}, u32[]{:S(2)}) collective-permute-start(bf16[448,512]{1,0:T(8,128)(2,1)S(1)} %shard_map.174.refs_1_), channel_id=1, source_target_pairs={{0,4},{4,0},{8,12},{12,8},{16,20},{20,16},{24,28},{28,24},{32,36},... | collective-permute-start | bytes 1376264 | tf_op jit(solution)/shard_map/ppermute | solution.py:65
  20.7 37.8 %collective-permute-start.31 = (bf16[224,1536]{1,0:T(8,128)(2,1)S(1)}, bf16[224,1536]{1,0:T(8,128)(2,1)S(1)}, u32[]{:S(2)}, u32[]{:S(2)}) collective-permute-start(bf16[224,1536]{1,0:T(8,128)(2,1)S(1)} %pair.1.refs_0_), channel_id=1, source_target_pairs={{0,4},{4,0},{8,12},{12,8},{16,20},{20,16},{24,28},{28,24},{32,36},... | collective-permute-start | bytes 2064392 | tf_op jit(solution)/shard_map/ppermute | solution.py:65
  21.8 36.7 %collective-permute-start.1 = (bf16[224,1536]{1,0:T(8,128)(2,1)S(1)}, bf16[224,1536]{1,0:T(8,128)(2,1)S(1)}, u32[]{:S(2)}, u32[]{:S(2)}) collective-permute-start(bf16[224,1536]{1,0:T(8,128)(2,1)S(1)} %pair.1.refs_0_), channel_id=1, source_target_pairs={{0,96},{4,28},{8,104},{12,4},{16,112},{20,12},{24,120},{28,20},{32... | collective-permute-start | bytes 2064392 | tf_op jit(solution)/shard_map/ppermute | solution.py:65
  46.8 11.2 %collective-permute-start.23 = (bf16[448,512]{1,0:T(8,128)(2,1)S(1)}, bf16[448,512]{1,0:T(8,128)(2,1)S(1)}, u32[]{:S(2)}, u32[]{:S(2)}) collective-permute-start(bf16[448,512]{1,0:T(8,128)(2,1)S(1)} %shard_map.174.refs_1_), channel_id=1, source_target_pairs={{0,96},{4,28},{8,104},{12,4},{16,112},{20,12},{24,120},{28,20},{32... | collective-permute-start | bytes 1376264 | tf_op jit(solution)/shard_map/ppermute | solution.py:65
  50.2 11.3 %collective-permute-start.13 = (bf16[224,1536]{1,0:T(8,128)(2,1)S(1)}, bf16[224,1536]{1,0:T(8,128)(2,1)S(1)}, u32[]{:S(2)}, u32[]{:S(2)}) collective-permute-start(bf16[224,1536]{1,0:T(8,128)(2,1)S(1)} %pair.1.refs_0_), channel_id=1, source_target_pairs={{0,32},{4,12},{8,40},{12,20},{16,48},{20,28},{24,56},{28,4},{32,64... | collective-permute-start | bytes 2064392 | tf_op jit(solution)/shard_map/ppermute | solution.py:65
  53.3 12.1 %collective-permute-start.28 = (bf16[448,512]{1,0:T(8,128)(2,1)S(1)}, bf16[448,512]{1,0:T(8,128)(2,1)S(1)}, u32[]{:S(2)}, u32[]{:S(2)}) collective-permute-start(bf16[448,512]{1,0:T(8,128)(2,1)S(1)} %collective-permute-done.17.refs_1_.refs_4_), channel_id=1, source_target_pairs={{0,4},{4,0},{8,12},{12,8},{16,20},{20,16},{24,28},{28,24},{32,36},... | collective-permute-start | bytes 1376264 | tf_op jit(solution)/shard_map/ppermute | solution.py:65
  61.5 16.1 %collective-permute-start.33 = (bf16[896,512]{1,0:T(8,128)(2,1)S(1)}, bf16[896,512]{1,0:T(8,128)(2,1)S(1)}, u32[]{:S(2)}, u32[]{:S(2)}) collective-permute-start(bf16[896,512]{1,0:T(8,128)(2,1)S(1)} %get-tuple-element.34.refs_2_), channel_id=1, source_target_pairs={{0,4},{4,0},{8,12},{12,8},{16,20},{20,16},{24,28},{28,24},{32,36},... | collective-permute-start | bytes 2752520 | tf_op jit(solution)/shard_map/ppermute | solution.py:65
  65.4 10.1 %collective-permute-start.10 = (bf16[672,512]{1,0:T(8,128)(2,1)S(1)}, bf16[672,512]{1,0:T(8,128)(2,1)S(1)}, u32[]{:S(2)}, u32[]{:S(2)}) collective-permute-start(bf16[672,512]{1,0:T(8,128)(2,1)S(1)} %get-tuple-element.33.refs_3_), channel_id=1, source_target_pairs={{0,96},{4,28},{8,104},{12,4},{16,112},{20,12},{24,120},{28,20},{32... | collective-permute-start | bytes 2064392 | tf_op jit(solution)/shard_map/ppermute | solution.py:65
  65.8 11.3 %collective-permute-start.15 = (bf16[672,512]{1,0:T(8,128)(2,1)S(1)}, bf16[672,512]{1,0:T(8,128)(2,1)S(1)}, u32[]{:S(2)}, u32[]{:S(2)}) collective-permute-start(bf16[672,512]{1,0:T(8,128)(2,1)S(1)} %get-tuple-element.33.refs_3_), channel_id=1, source_target_pairs={{0,32},{4,12},{8,40},{12,20},{16,48},{20,28},{24,56},{28,4},{32,64... | collective-permute-start | bytes 2064392 | tf_op jit(solution)/shard_map/ppermute | solution.py:65
  67.5 19.4 %collective-permute-start.19 = (bf16[896,512]{1,0:T(8,128)(2,1)S(1)}, bf16[896,512]{1,0:T(8,128)(2,1)S(1)}, u32[]{:S(2)}, u32[]{:S(2)}) collective-permute-start(bf16[896,512]{1,0:T(8,128)(2,1)S(1)} %get-tuple-element.34.refs_2_), channel_id=1, source_target_pairs={{0,32},{4,12},{8,40},{12,20},{16,48},{20,28},{24,56},{28,4},{32,64... | collective-permute-start | bytes 2752520 | tf_op jit(solution)/shard_map/ppermute | solution.py:65
  67.5 19.4 %collective-permute-start.24 = (bf16[896,512]{1,0:T(8,128)(2,1)S(1)}, bf16[896,512]{1,0:T(8,128)(2,1)S(1)}, u32[]{:S(2)}, u32[]{:S(2)}) collective-permute-start(bf16[896,512]{1,0:T(8,128)(2,1)S(1)} %get-tuple-element.34.refs_2_), channel_id=1, source_target_pairs={{0,96},{4,28},{8,104},{12,4},{16,112},{20,12},{24,120},{28,20},{32... | collective-permute-start | bytes 2752520 | tf_op jit(solution)/shard_map/ppermute | solution.py:65
  75.4 12.7 %collective-permute-start.25 = (bf16[224,1536]{1,0:T(8,128)(2,1)S(1)}, bf16[224,1536]{1,0:T(8,128)(2,1)S(1)}, u32[]{:S(2)}, u32[]{:S(2)}) collective-permute-start(bf16[224,1536]{1,0:T(8,128)(2,1)S(1)} %collective-permute-done.1.refs_3_.refs_0_.refs_6_), channel_id=1, source_target_pairs={{0,4},{4,0},{8,12},{12,8},{16,20},{20,16},{24,28},{28,24},{32,36},... | collective-permute-start | bytes 2064392 | tf_op jit(solution)/shard_map/ppermute | solution.py:65
  77.1 11.2 %collective-permute-start.14 = (bf16[224,1536]{1,0:T(8,128)(2,1)S(1)}, bf16[224,1536]{1,0:T(8,128)(2,1)S(1)}, u32[]{:S(2)}, u32[]{:S(2)}) collective-permute-start(bf16[224,1536]{1,0:T(8,128)(2,1)S(1)} %collective-permute-done.13.refs_0_.refs_3_), channel_id=1, source_target_pairs={{0,4},{4,0},{8,12},{12,8},{16,20},{20,16},{24,28},{28,24},{32,36},... | collective-permute-start | bytes 2064392 | tf_op jit(solution)/shard_map/ppermute | solution.py:65
  77.7 15.0 %collective-permute-start.2 = (bf16[224,1536]{1,0:T(8,128)(2,1)S(1)}, bf16[224,1536]{1,0:T(8,128)(2,1)S(1)}, u32[]{:S(2)}, u32[]{:S(2)}) collective-permute-start(bf16[224,1536]{1,0:T(8,128)(2,1)S(1)} %collective-permute-done.1.refs_3_.refs_0_.refs_6_), channel_id=1, source_target_pairs={{0,96},{4,28},{8,104},{12,4},{16,112},{20,12},{24,120},{28,20},{32... | collective-permute-start | bytes 2064392 | tf_op jit(solution)/shard_map/ppermute | solution.py:65
  86.9 13.8 %collective-permute-start.20 = (bf16[896,512]{1,0:T(8,128)(2,1)S(1)}, bf16[896,512]{1,0:T(8,128)(2,1)S(1)}, u32[]{:S(2)}, u32[]{:S(2)}) collective-permute-start(bf16[896,512]{1,0:T(8,128)(2,1)S(1)} %collective-permute-done.19.refs_2_.refs_5_), channel_id=1, source_target_pairs={{0,32},{4,12},{8,40},{12,20},{16,48},{20,28},{24,56},{28,4},{32,64... | collective-permute-start | bytes 2752520 | tf_op jit(solution)/shard_map/ppermute | solution.py:65
  86.9 17.5 %collective-permute-start.29 = (bf16[896,512]{1,0:T(8,128)(2,1)S(1)}, bf16[896,512]{1,0:T(8,128)(2,1)S(1)}, u32[]{:S(2)}, u32[]{:S(2)}) collective-permute-start(bf16[896,512]{1,0:T(8,128)(2,1)S(1)} %collective-permute-done.19.refs_2_.refs_5_), channel_id=1, source_target_pairs={{0,4},{4,0},{8,12},{12,8},{16,20},{20,16},{24,28},{28,24},{32,36},... | collective-permute-start | bytes 2752520 | tf_op jit(solution)/shard_map/ppermute | solution.py:65
  88.2 16.3 %collective-permute-start.27 = (bf16[896,512]{1,0:T(8,128)(2,1)S(1)}, bf16[896,512]{1,0:T(8,128)(2,1)S(1)}, u32[]{:S(2)}, u32[]{:S(2)}) collective-permute-start(bf16[896,512]{1,0:T(8,128)(2,1)S(1)} %collective-permute-done.24.refs_2_.refs_8_), channel_id=1, source_target_pairs={{0,4},{4,0},{8,12},{12,8},{16,20},{20,16},{24,28},{28,24},{32,36},... | collective-permute-start | bytes 2752520 | tf_op jit(solution)/shard_map/ppermute | solution.py:65
  88.3 13.8 %collective-permute-start.30 = (bf16[672,512]{1,0:T(8,128)(2,1)S(1)}, bf16[672,512]{1,0:T(8,128)(2,1)S(1)}, u32[]{:S(2)}, u32[]{:S(2)}) collective-permute-start(bf16[672,512]{1,0:T(8,128)(2,1)S(1)} %collective-permute-done.10.refs_4_), channel_id=1, source_target_pairs={{0,4},{4,0},{8,12},{12,8},{16,20},{20,16},{24,28},{28,24},{32,36},... | collective-permute-start | bytes 2064392 | tf_op jit(solution)/shard_map/ppermute | solution.py:65
  100.7 11.5 %collective-permute-start.22 = (bf16[896,512]{1,0:T(8,128)(2,1)S(1)}, bf16[896,512]{1,0:T(8,128)(2,1)S(1)}, u32[]{:S(2)}, u32[]{:S(2)}) collective-permute-start(bf16[896,512]{1,0:T(8,128)(2,1)S(1)} %collective-permute-done.20.refs_2_.refs_11_), channel_id=1, source_target_pairs={{0,4},{4,0},{8,12},{12,8},{16,20},{20,16},{24,28},{28,24},{32,36},... | collective-permute-start | bytes 2752520 | tf_op jit(solution)/shard_map/ppermute | solution.py:65
  102.1 10.1 %collective-permute-start.3 = (bf16[224,1536]{1,0:T(8,128)(2,1)S(1)}, bf16[224,1536]{1,0:T(8,128)(2,1)S(1)}, u32[]{:S(2)}, u32[]{:S(2)}) collective-permute-start(bf16[224,1536]{1,0:T(8,128)(2,1)S(1)} %collective-permute-done.2.refs_0_.refs_2_.refs_9_), channel_id=1, source_target_pairs={{0,4},{4,0},{8,12},{12,8},{16,20},{20,16},{24,28},{28,24},{32,36},... | collective-permute-start | bytes 2064392 | tf_op jit(solution)/shard_map/ppermute | solution.py:65
  102.7 15.1 %collective-permute-start.16 = (bf16[672,512]{1,0:T(8,128)(2,1)S(1)}, bf16[672,512]{1,0:T(8,128)(2,1)S(1)}, u32[]{:S(2)}, u32[]{:S(2)}) collective-permute-start(bf16[672,512]{1,0:T(8,128)(2,1)S(1)} %collective-permute-done.15.refs_1_), channel_id=1, source_target_pairs={{0,4},{4,0},{8,12},{12,8},{16,20},{20,16},{24,28},{28,24},{32,36},... | collective-permute-start | bytes 2064392 | tf_op jit(solution)/shard_map/ppermute | solution.py:65
  104.4 14.6 %collective-permute-start.12 = (bf16[672,512]{1,0:T(8,128)(2,1)S(1)}, bf16[672,512]{1,0:T(8,128)(2,1)S(1)}, u32[]{:S(2)}, u32[]{:S(2)}) collective-permute-start(bf16[672,512]{1,0:T(8,128)(2,1)S(1)} %collective-permute-done.11.refs_3_), channel_id=1, source_target_pairs={{0,4},{4,0},{8,12},{12,8},{16,20},{20,16},{24,28},{28,24},{32,36},... | collective-permute-start | bytes 2064392 | tf_op jit(solution)/shard_map/ppermute | solution.py:65
  (16 other events, 116.2 us)

commit v4 on v3

--- a/solution.py
+++ b/solution.py
@@ -94,10 +94,10 @@
     ins, (keep, give), here, (line, sems) = refs[:14], refs[14:16], refs[16:30], refs[30:]
     y, x, c = place()
     copies = [pltpu.make_async_copy(a, b, sems.at[i]) for i, (a, b) in enumerate(zip(ins, here))]
-    for copy in copies:
+    for copy in copies[12:] + copies[:12]:
         copy.start()
     line[...] = jnp.zeros(line.shape, jnp.float32)
-    for copy in copies:
+    for copy in copies[12:]:
         copy.wait()
     tq, lq, hq, tk, lk, hk, tv, lv, hv, tm, lm, hm, gain, step = here
 
@@ -117,6 +117,8 @@
     line[pl.ds(row + 1, 1), :] = jnp.where(lane < at, turned, line[pl.ds(row + 1, 1), :])
     for to in (keep, give):
         to[ROWS : ROWS + 8, 0:512] = line[...].astype(jnp.bfloat16)
+    for copy in copies[:12]:
+        copy.wait()
 
     rows = slice(0, ROWS)
 
@@ -272,8 +274,7 @@
     (((1, 0), (1, 2)), BOTH),
     (((2, 0), (2, 2)), BOTH),
     (((-1, 1), (2, 1)), ("own",)),
-    (((-1, 1),), ("partner",)),
-    (((2, 1),), ("partner",)),
+    (((-1, 1), (2, 1)), ("partner",)),
 )
 
 

time: 121 us -> 123 us (1.017)
  starting transfers between devices: 49.8 us -> 62.4 us
  waiting for transfers between devices: 52.4 us -> 42.9 us
    ppermute x35, starting transfers between devices: 39.3 us -> 52.3 us  [send(): return lax.ppermute(array, ZERO, to)]
    ppermute x35, waiting for transfers between devices: 44.3 us -> 36.8 us  [send(): return lax.ppermute(array, ZERO, to)]
    ppermute x5, waiting for transfers between devices: 8.1 us -> 6.16 us  [norm_of(): there = lax.ppermute(tile, axis, move)]
    pallas_call x7 -> x6, Pallas kernels: 12.2 us -> 11.3 us  [lay(): pl.pallas_call(lambda *refs: lay_kernel(work, sides, keys, n_in, *refs),...]
  transfers between devices with their start and end apart: 40 -> 40, of which waited for: 20 -> 16; matrix products, arithmetic and copies ran while one was open for 0% -> 0% of each run, Pallas kernels for 12% -> 11%
where the time goes in v4:
time: 123 us
  starting transfers between devices  62.4 us (51%)
  waiting for transfers between devices  42.9 us (35%)
  Pallas kernels  16.4 us (13%)
    ppermute x35, starting transfers between devices, send(): return lax.ppermute(array, ZERO, to)  52.3 us
    ppermute x35, waiting for transfers between devices, send(): return lax.ppermute(array, ZERO, to)  36.8 us
    pallas_call x6, Pallas kernels, lay(): pl.pallas_call(lambda *refs: lay_kernel(work, sides, keys, n_in, *refs),...  11.3 us
    ppermute x5, starting transfers between devices, norm_of(): there = lax.ppermute(tile, axis, move)  10.1 us
    ppermute x5, waiting for transfers between devices, norm_of(): there = lax.ppermute(tile, axis, move)  6.16 us
  transfers between devices with their start and end apart: 40, of which 16 were waited for; matrix products, arithmetic and copies ran while one was open for 0% of the time, Pallas kernels for 11%

profile of v4, /device:TPU:1, one launch (start us, length us, event | category | flops | bytes accessed | tf_op | source)
XLA Modules:
  0.0 122.7 jit_solution(3541228483150129265)
XLA Ops:
  6.7 2.8 %collective-permute-start.4 = (bf16[120,1536]{1,0:T(8,128)(2,1)S(1)}, bf16[120,1536]{1,0:T(8,128)(2,1)S(1)}, u32[]{:S(2)}, u32[]{:S(2)}) collective-permute-start(bf16[120,1536]{1,0:T(8,128)(2,1)S(1)} %get-tuple-element.28.keep.refs_6_), channel_id=1, source_target_pairs={{0,24},{4,100},{8,0},{12,108},{16,8},{20,116},{24,16},{28,124},{32... | collective-permute-start | bytes 1105928 | tf_op jit(solution)/shard_map/ppermute | solution.py:65
  11.3 3.6 %collective-permute-done.6.refs_3_ = bf16[120,1536]{1,0:T(8,128)(2,1)S(1)} collective-permute-done((bf16[120,1536]{1,0:T(8,128)(2,1)S(1)}, bf16[120,1536]{1,0:T(8,128)(2,1)S(1)}, u32[]{:S(2)}, u32[]{:S(2)}) %collective-permute-start.6) | collective-permute-done | bytes 368672 | tf_op jit(solution)/shard_map/ppermute | solution.py:65
  20.7 2.7 %collective-permute-start.11 = (bf16[224,1536]{1,0:T(8,128)(2,1)S(1)}, bf16[224,1536]{1,0:T(8,128)(2,1)S(1)}, u32[]{:S(2)}, u32[]{:S(2)}) collective-permute-start(bf16[224,1536]{1,0:T(8,128)(2,1)S(1)} %pair.1.refs_0_), channel_id=1, source_target_pairs={{0,96},{4,28},{8,104},{12,4},{16,112},{20,12},{24,120},{28,20},{32... | collective-permute-start | bytes 2064392 | tf_op jit(solution)/shard_map/ppermute | solution.py:65
  23.3 6.3 %collective-permute-done.7.refs_4_ = bf16[120,1536]{1,0:T(8,128)(2,1)S(1)} collective-permute-done((bf16[120,1536]{1,0:T(8,128)(2,1)S(1)}, bf16[120,1536]{1,0:T(8,128)(2,1)S(1)}, u32[]{:S(2)}, u32[]{:S(2)}) %collective-permute-start.7) | collective-permute-done | bytes 368672 | tf_op jit(solution)/shard_map/ppermute | solution.py:65
  29.8 3.8 %collective-permute-start.35 = (bf16[8,512]{1,0:T(8,128)(2,1)S(1)}, bf16[8,512]{1,0:T(8,128)(2,1)S(1)}, u32[]{:S(2)}, u32[]{:S(2)}) collective-permute-start(bf16[8,512]{1,0:T(8,128)(2,1)S(1)} %get-tuple-element.50.here), channel_id=1, source_target_pairs={{0,3},{1,2},{2,1},{3,0},{4,7},{5,6},{6,5},{7,4},{8,11},{9,10},{10,... | collective-permute-start | bytes 24584 | tf_op jit(solution)/shard_map/ppermute | solution.py:381
  35.0 2.8 %collective-permute-done.36.there = bf16[8,512]{1,0:T(8,128)(2,1)S(1)} collective-permute-done((bf16[8,512]{1,0:T(8,128)(2,1)S(1)}, bf16[8,512]{1,0:T(8,128)(2,1)S(1)}, u32[]{:S(2)}, u32[]{:S(2)}) %collective-permute-start.36) | collective-permute-done | bytes 8224 | tf_op jit(solution)/shard_map/ppermute | solution.py:381
  37.8 2.8 %collective-permute-start.37 = (bf16[8,512]{1,0:T(8,128)(2,1)S(1)}, bf16[8,512]{1,0:T(8,128)(2,1)S(1)}, u32[]{:S(2)}, u32[]{:S(2)}) collective-permute-start(bf16[8,512]{1,0:T(8,128)(2,1)S(1)} %shard_map.182.here), channel_id=1, source_target_pairs={{0,4},{4,0},{8,12},{12,8},{16,20},{20,16},{24,28},{28,24},{32,36},... | collective-permute-start | bytes 24584 | tf_op jit(solution)/shard_map/ppermute | solution.py:381
  46.1 2.9 %collective-permute-start.23 = (bf16[448,512]{1,0:T(8,128)(2,1)S(1)}, bf16[448,512]{1,0:T(8,128)(2,1)S(1)}, u32[]{:S(2)}, u32[]{:S(2)}) collective-permute-start(bf16[448,512]{1,0:T(8,128)(2,1)S(1)} %shard_map.174.refs_1_), channel_id=1, source_target_pairs={{0,96},{4,28},{8,104},{12,4},{16,112},{20,12},{24,120},{28,20},{32... | collective-permute-start | bytes 1376264 | tf_op jit(solution)/shard_map/ppermute | solution.py:65
  51.2 3.3 %collective-permute-done.23.refs_1_.refs_7_ = bf16[448,512]{1,0:T(8,128)(2,1)S(1)} collective-permute-done((bf16[448,512]{1,0:T(8,128)(2,1)S(1)}, bf16[448,512]{1,0:T(8,128)(2,1)S(1)}, u32[]{:S(2)}, u32[]{:S(2)}) %collective-permute-start.23) | collective-permute-done | bytes 458784 | tf_op jit(solution)/shard_map/ppermute | solution.py:65
  54.4 4.3 %collective-permute-start.28 = (bf16[448,512]{1,0:T(8,128)(2,1)S(1)}, bf16[448,512]{1,0:T(8,128)(2,1)S(1)}, u32[]{:S(2)}, u32[]{:S(2)}) collective-permute-start(bf16[448,512]{1,0:T(8,128)(2,1)S(1)} %collective-permute-done.17.refs_1_.refs_4_), channel_id=1, source_target_pairs={{0,4},{4,0},{8,12},{12,8},{16,20},{20,16},{24,28},{28,24},{32,36},... | collective-permute-start | bytes 1376264 | tf_op jit(solution)/shard_map/ppermute | solution.py:65
  59.2 4.5 %collective-permute-done.18.refs_1_.refs_10_ = bf16[448,512]{1,0:T(8,128)(2,1)S(1)} collective-permute-done((bf16[448,512]{1,0:T(8,128)(2,1)S(1)}, bf16[448,512]{1,0:T(8,128)(2,1)S(1)}, u32[]{:S(2)}, u32[]{:S(2)}) %collective-permute-start.18) | collective-permute-done | bytes 458784 | tf_op jit(solution)/shard_map/ppermute | solution.py:65
  65.2 2.7 %collective-permute-start.24 = (bf16[896,512]{1,0:T(8,128)(2,1)S(1)}, bf16[896,512]{1,0:T(8,128)(2,1)S(1)}, u32[]{:S(2)}, u32[]{:S(2)}) collective-permute-start(bf16[896,512]{1,0:T(8,128)(2,1)S(1)} %get-tuple-element.31.refs_2_), channel_id=1, source_target_pairs={{0,96},{4,28},{8,104},{12,4},{16,112},{20,12},{24,120},{28,20},{32... | collective-permute-start | bytes 2752520 | tf_op jit(solution)/shard_map/ppermute | solution.py:65
  67.9 4.6 %collective-permute-start.33 = (bf16[896,512]{1,0:T(8,128)(2,1)S(1)}, bf16[896,512]{1,0:T(8,128)(2,1)S(1)}, u32[]{:S(2)}, u32[]{:S(2)}) collective-permute-start(bf16[896,512]{1,0:T(8,128)(2,1)S(1)} %get-tuple-element.31.refs_2_), channel_id=1, source_target_pairs={{0,4},{4,0},{8,12},{12,8},{16,20},{20,16},{24,28},{28,24},{32,36},... | collective-permute-start | bytes 2752520 | tf_op jit(solution)/shard_map/ppermute | solution.py:65
  73.8 2.7 %collective-permute-start.12 = (bf16[224,1536]{1,0:T(8,128)(2,1)S(1)}, bf16[224,1536]{1,0:T(8,128)(2,1)S(1)}, u32[]{:S(2)}, u32[]{:S(2)}) collective-permute-start(bf16[224,1536]{1,0:T(8,128)(2,1)S(1)} %collective-permute-done.11.refs_3_.refs_0_.refs_6_), channel_id=1, source_target_pairs={{0,96},{4,28},{8,104},{12,4},{16,112},{20,12},{24,120},{28,20},{32... | collective-permute-start | bytes 2064392 | tf_op jit(solution)/shard_map/ppermute | solution.py:65
  76.5 4.4 %collective-permute-done.9.refs_1_ = bf16[672,512]{1,0:T(8,128)(2,1)S(1)} collective-permute-done((bf16[672,512]{1,0:T(8,128)(2,1)S(1)}, bf16[672,512]{1,0:T(8,128)(2,1)S(1)}, u32[]{:S(2)}, u32[]{:S(2)}) %collective-permute-start.9) | collective-permute-done | bytes 688160 | tf_op jit(solution)/shard_map/ppermute | solution.py:65
  80.9 3.5 %collective-permute-start.25 = (bf16[224,1536]{1,0:T(8,128)(2,1)S(1)}, bf16[224,1536]{1,0:T(8,128)(2,1)S(1)}, u32[]{:S(2)}, u32[]{:S(2)}) collective-permute-start(bf16[224,1536]{1,0:T(8,128)(2,1)S(1)} %collective-permute-done.11.refs_3_.refs_0_.refs_6_), channel_id=1, source_target_pairs={{0,4},{4,0},{8,12},{12,8},{16,20},{20,16},{24,28},{28,24},{32,36},... | collective-permute-start | bytes 2064392 | tf_op jit(solution)/shard_map/ppermute | solution.py:65
  84.5 3.5 %collective-permute-start.29 = (bf16[896,512]{1,0:T(8,128)(2,1)S(1)}, bf16[896,512]{1,0:T(8,128)(2,1)S(1)}, u32[]{:S(2)}, u32[]{:S(2)}) collective-permute-start(bf16[896,512]{1,0:T(8,128)(2,1)S(1)} %collective-permute-done.19.refs_2_.refs_5_), channel_id=1, source_target_pairs={{0,4},{4,0},{8,12},{12,8},{16,20},{20,16},{24,28},{28,24},{32,36},... | collective-permute-start | bytes 2752520 | tf_op jit(solution)/shard_map/ppermute | solution.py:65
  88.0 3.0 %collective-permute-done.12.refs_0_.refs_2_.refs_9_ = bf16[224,1536]{1,0:T(8,128)(2,1)S(1)} collective-permute-done((bf16[224,1536]{1,0:T(8,128)(2,1)S(1)}, bf16[224,1536]{1,0:T(8,128)(2,1)S(1)}, u32[]{:S(2)}, u32[]{:S(2)}) %collective-permute-start.12) | collective-permute-done | bytes 688160 | tf_op jit(solution)/shard_map/ppermute | solution.py:65
  91.0 4.4 %collective-permute-start.27 = (bf16[896,512]{1,0:T(8,128)(2,1)S(1)}, bf16[896,512]{1,0:T(8,128)(2,1)S(1)}, u32[]{:S(2)}, u32[]{:S(2)}) collective-permute-start(bf16[896,512]{1,0:T(8,128)(2,1)S(1)} %collective-permute-done.24.refs_2_.refs_8_), channel_id=1, source_target_pairs={{0,4},{4,0},{8,12},{12,8},{16,20},{20,16},{24,28},{28,24},{32,36},... | collective-permute-start | bytes 2752520 | tf_op jit(solution)/shard_map/ppermute | solution.py:65
  95.5 2.8 %collective-permute-done.20.refs_2_.refs_11_ = bf16[896,512]{1,0:T(8,128)(2,1)S(1)} collective-permute-done((bf16[896,512]{1,0:T(8,128)(2,1)S(1)}, bf16[896,512]{1,0:T(8,128)(2,1)S(1)}, u32[]{:S(2)}, u32[]{:S(2)}) %collective-permute-start.20) | collective-permute-done | bytes 917536 | tf_op jit(solution)/shard_map/ppermute | solution.py:65
  98.3 4.3 %collective-permute-start.22 = (bf16[896,512]{1,0:T(8,128)(2,1)S(1)}, bf16[896,512]{1,0:T(8,128)(2,1)S(1)}, u32[]{:S(2)}, u32[]{:S(2)}) collective-permute-start(bf16[896,512]{1,0:T(8,128)(2,1)S(1)} %collective-permute-done.20.refs_2_.refs_11_), channel_id=1, source_target_pairs={{0,4},{4,0},{8,12},{12,8},{16,20},{20,16},{24,28},{28,24},{32,36},... | collective-permute-start | bytes 2752520 | tf_op jit(solution)/shard_map/ppermute | solution.py:65
  102.6 2.9 %collective-permute-done.15.refs_3_ = bf16[672,512]{1,0:T(8,128)(2,1)S(1)} collective-permute-done((bf16[672,512]{1,0:T(8,128)(2,1)S(1)}, bf16[672,512]{1,0:T(8,128)(2,1)S(1)}, u32[]{:S(2)}, u32[]{:S(2)}) %collective-permute-start.15) | collective-permute-done | bytes 688160 | tf_op jit(solution)/shard_map/ppermute | solution.py:65
  111.1 2.4 %shard_map.176 = (bf16[1024,3584]{1,0:T(8,128)(2,1)}, bf16[512,3584]{1,0:T(8,128)(2,1)}, bf16[3584,1024]{1,0:T(8,128)(2,1)}) custom-call(bf16[224,1536]{1,0:T(8,128)(2,1)S(1)} %collective-permute-done.1.refs_0_.refs_3_, bf16[448,512]{1,0:T(8,128)(2,1)S(1)} %collective-permute-done.17.refs_1_.refs_4_, ...), custom_call_target="tpu_custom_call", output_to_operand_aliasing={{0}: (10, {}), {1}: (11, {}), {2}: (12, {})} | custom-call | tf_op jit(solution)/shard_map/pallas_call | solution.py:288
  115.3 2.4 %value.1 = bf16[512,3584]{1,0:T(8,128)(2,1)} custom-call(bf16[224,1536]{1,0:T(8,128)(2,1)S(1)} %pair.1.refs_0_, bf16[448,512]{1,0:T(8,128)(2,1)S(1)} %shard_map.174.refs_1_, bf16[896,512]{1,0:T(8,128)(2,1)S(1)} %get-tuple-element.31.refs_2_, bf16[224,1536]{1,0:T(8,128)(2,1)S(1)} %collective-permute-done.1.refs_0_.refs_3_, ...), custom_call_target="tpu_custom_call" | custom-call | tf_op jit(solution)/shard_map/value/pallas_call | solution.py:342
  (72 shorter events, 38.2 us)
Async XLA Ops:
  4.6 10.3 %collective-permute-start.6 = (bf16[120,1536]{1,0:T(8,128)(2,1)S(1)}, bf16[120,1536]{1,0:T(8,128)(2,1)S(1)}, u32[]{:S(2)}, u32[]{:S(2)}) collective-permute-start(bf16[120,1536]{1,0:T(8,128)(2,1)S(1)} %get-tuple-element.29), channel_id=1, source_target_pairs={{0,100},{4,24},{8,108},{12,0},{16,116},{20,8},{24,124},{28,16},{32... | collective-permute-start | bytes 1105928 | tf_op jit(solution)/shard_map/ppermute | solution.py:65
  9.6 11.0 %collective-permute-start = (bf16[120,1536]{1,0:T(8,128)(2,1)S(1)}, bf16[120,1536]{1,0:T(8,128)(2,1)S(1)}, u32[]{:S(2)}, u32[]{:S(2)}) collective-permute-start(bf16[120,1536]{1,0:T(8,128)(2,1)S(1)} %get-tuple-element.29), channel_id=1, source_target_pairs={{0,4},{4,0},{8,12},{12,8},{16,20},{20,16},{24,28},{28,24},{32,36},... | collective-permute-start | bytes 1105928 | tf_op jit(solution)/shard_map/ppermute | solution.py:65
  17.8 33.3 %collective-permute-start.17 = (bf16[448,512]{1,0:T(8,128)(2,1)S(1)}, bf16[448,512]{1,0:T(8,128)(2,1)S(1)}, u32[]{:S(2)}, u32[]{:S(2)}) collective-permute-start(bf16[448,512]{1,0:T(8,128)(2,1)S(1)} %shard_map.174.refs_1_), channel_id=1, source_target_pairs={{0,32},{4,12},{8,40},{12,20},{16,48},{20,28},{24,56},{28,4},{32,64... | collective-permute-start | bytes 1376264 | tf_op jit(solution)/shard_map/ppermute | solution.py:65
  17.9 11.8 %collective-permute-start.7 = (bf16[120,1536]{1,0:T(8,128)(2,1)S(1)}, bf16[120,1536]{1,0:T(8,128)(2,1)S(1)}, u32[]{:S(2)}, u32[]{:S(2)}) collective-permute-start(bf16[120,1536]{1,0:T(8,128)(2,1)S(1)} %collective-permute-done.3.refs_0_), channel_id=1, source_target_pairs={{0,8},{4,36},{8,16},{12,44},{16,24},{20,52},{24,0},{28,60},{32,40}... | collective-permute-start | bytes 1105928 | tf_op jit(solution)/shard_map/ppermute | solution.py:65
  18.6 11.0 %collective-permute-start.8 = (bf16[120,1536]{1,0:T(8,128)(2,1)S(1)}, bf16[120,1536]{1,0:T(8,128)(2,1)S(1)}, u32[]{:S(2)}, u32[]{:S(2)}) collective-permute-start(bf16[120,1536]{1,0:T(8,128)(2,1)S(1)} %collective-permute-done.6.refs_3_), channel_id=1, source_target_pairs={{0,24},{4,100},{8,0},{12,108},{16,8},{20,116},{24,16},{28,124},{32... | collective-permute-start | bytes 1105928 | tf_op jit(solution)/shard_map/ppermute | solution.py:65
  20.7 38.0 %collective-permute-start.11 = (bf16[224,1536]{1,0:T(8,128)(2,1)S(1)}, bf16[224,1536]{1,0:T(8,128)(2,1)S(1)}, u32[]{:S(2)}, u32[]{:S(2)}) collective-permute-start(bf16[224,1536]{1,0:T(8,128)(2,1)S(1)} %pair.1.refs_0_), channel_id=1, source_target_pairs={{0,96},{4,28},{8,104},{12,4},{16,112},{20,12},{24,120},{28,20},{32... | collective-permute-start | bytes 2064392 | tf_op jit(solution)/shard_map/ppermute | solution.py:65
  23.3 35.5 %collective-permute-start.1 = (bf16[224,1536]{1,0:T(8,128)(2,1)S(1)}, bf16[224,1536]{1,0:T(8,128)(2,1)S(1)}, u32[]{:S(2)}, u32[]{:S(2)}) collective-permute-start(bf16[224,1536]{1,0:T(8,128)(2,1)S(1)} %pair.1.refs_0_), channel_id=1, source_target_pairs={{0,32},{4,12},{8,40},{12,20},{16,48},{20,28},{24,56},{28,4},{32,64... | collective-permute-start | bytes 2064392 | tf_op jit(solution)/shard_map/ppermute | solution.py:65
  54.4 10.7 %collective-permute-start.28 = (bf16[448,512]{1,0:T(8,128)(2,1)S(1)}, bf16[448,512]{1,0:T(8,128)(2,1)S(1)}, u32[]{:S(2)}, u32[]{:S(2)}) collective-permute-start(bf16[448,512]{1,0:T(8,128)(2,1)S(1)} %collective-permute-done.17.refs_1_.refs_4_), channel_id=1, source_target_pairs={{0,4},{4,0},{8,12},{12,8},{16,20},{20,16},{24,28},{28,24},{32,36},... | collective-permute-start | bytes 1376264 | tf_op jit(solution)/shard_map/ppermute | solution.py:65
  59.2 25.2 %collective-permute-start.19 = (bf16[896,512]{1,0:T(8,128)(2,1)S(1)}, bf16[896,512]{1,0:T(8,128)(2,1)S(1)}, u32[]{:S(2)}, u32[]{:S(2)}) collective-permute-start(bf16[896,512]{1,0:T(8,128)(2,1)S(1)} %get-tuple-element.31.refs_2_), channel_id=1, source_target_pairs={{0,32},{4,12},{8,40},{12,20},{16,48},{20,28},{24,56},{28,4},{32,64... | collective-permute-start | bytes 2752520 | tf_op jit(solution)/shard_map/ppermute | solution.py:65
  63.7 10.1 %collective-permute-start.14 = (bf16[672,512]{1,0:T(8,128)(2,1)S(1)}, bf16[672,512]{1,0:T(8,128)(2,1)S(1)}, u32[]{:S(2)}, u32[]{:S(2)}) collective-permute-start(bf16[672,512]{1,0:T(8,128)(2,1)S(1)} %get-tuple-element.30.refs_3_), channel_id=1, source_target_pairs={{0,96},{4,28},{8,104},{12,4},{16,112},{20,12},{24,120},{28,20},{32... | collective-permute-start | bytes 2064392 | tf_op jit(solution)/shard_map/ppermute | solution.py:65
  65.2 15.7 %collective-permute-start.9 = (bf16[672,512]{1,0:T(8,128)(2,1)S(1)}, bf16[672,512]{1,0:T(8,128)(2,1)S(1)}, u32[]{:S(2)}, u32[]{:S(2)}) collective-permute-start(bf16[672,512]{1,0:T(8,128)(2,1)S(1)} %get-tuple-element.30.refs_3_), channel_id=1, source_target_pairs={{0,32},{4,12},{8,40},{12,20},{16,48},{20,28},{24,56},{28,4},{32,64... | collective-permute-start | bytes 2064392 | tf_op jit(solution)/shard_map/ppermute | solution.py:65
  65.2 19.2 %collective-permute-start.24 = (bf16[896,512]{1,0:T(8,128)(2,1)S(1)}, bf16[896,512]{1,0:T(8,128)(2,1)S(1)}, u32[]{:S(2)}, u32[]{:S(2)}) collective-permute-start(bf16[896,512]{1,0:T(8,128)(2,1)S(1)} %get-tuple-element.31.refs_2_), channel_id=1, source_target_pairs={{0,96},{4,28},{8,104},{12,4},{16,112},{20,12},{24,120},{28,20},{32... | collective-permute-start | bytes 2752520 | tf_op jit(solution)/shard_map/ppermute | solution.py:65
  67.9 16.6 %collective-permute-start.33 = (bf16[896,512]{1,0:T(8,128)(2,1)S(1)}, bf16[896,512]{1,0:T(8,128)(2,1)S(1)}, u32[]{:S(2)}, u32[]{:S(2)}) collective-permute-start(bf16[896,512]{1,0:T(8,128)(2,1)S(1)} %get-tuple-element.31.refs_2_), channel_id=1, source_target_pairs={{0,4},{4,0},{8,12},{12,8},{16,20},{20,16},{24,28},{28,24},{32,36},... | collective-permute-start | bytes 2752520 | tf_op jit(solution)/shard_map/ppermute | solution.py:65
  73.8 17.2 %collective-permute-start.12 = (bf16[224,1536]{1,0:T(8,128)(2,1)S(1)}, bf16[224,1536]{1,0:T(8,128)(2,1)S(1)}, u32[]{:S(2)}, u32[]{:S(2)}) collective-permute-start(bf16[224,1536]{1,0:T(8,128)(2,1)S(1)} %collective-permute-done.11.refs_3_.refs_0_.refs_6_), channel_id=1, source_target_pairs={{0,96},{4,28},{8,104},{12,4},{16,112},{20,12},{24,120},{28,20},{32... | collective-permute-start | bytes 2064392 | tf_op jit(solution)/shard_map/ppermute | solution.py:65
  80.9 14.4 %collective-permute-start.25 = (bf16[224,1536]{1,0:T(8,128)(2,1)S(1)}, bf16[224,1536]{1,0:T(8,128)(2,1)S(1)}, u32[]{:S(2)}, u32[]{:S(2)}) collective-permute-start(bf16[224,1536]{1,0:T(8,128)(2,1)S(1)} %collective-permute-done.11.refs_3_.refs_0_.refs_6_), channel_id=1, source_target_pairs={{0,4},{4,0},{8,12},{12,8},{16,20},{20,16},{24,28},{28,24},{32,36},... | collective-permute-start | bytes 2064392 | tf_op jit(solution)/shard_map/ppermute | solution.py:65
  84.4 10.9 %collective-permute-start.2 = (bf16[224,1536]{1,0:T(8,128)(2,1)S(1)}, bf16[224,1536]{1,0:T(8,128)(2,1)S(1)}, u32[]{:S(2)}, u32[]{:S(2)}) collective-permute-start(bf16[224,1536]{1,0:T(8,128)(2,1)S(1)} %collective-permute-done.1.refs_0_.refs_3_), channel_id=1, source_target_pairs={{0,4},{4,0},{8,12},{12,8},{16,20},{20,16},{24,28},{28,24},{32,36},... | collective-permute-start | bytes 2064392 | tf_op jit(solution)/shard_map/ppermute | solution.py:65
  84.4 13.8 %collective-permute-start.20 = (bf16[896,512]{1,0:T(8,128)(2,1)S(1)}, bf16[896,512]{1,0:T(8,128)(2,1)S(1)}, u32[]{:S(2)}, u32[]{:S(2)}) collective-permute-start(bf16[896,512]{1,0:T(8,128)(2,1)S(1)} %collective-permute-done.19.refs_2_.refs_5_), channel_id=1, source_target_pairs={{0,32},{4,12},{8,40},{12,20},{16,48},{20,28},{24,56},{28,4},{32,64... | collective-permute-start | bytes 2752520 | tf_op jit(solution)/shard_map/ppermute | solution.py:65
  84.5 23.0 %collective-permute-start.29 = (bf16[896,512]{1,0:T(8,128)(2,1)S(1)}, bf16[896,512]{1,0:T(8,128)(2,1)S(1)}, u32[]{:S(2)}, u32[]{:S(2)}) collective-permute-start(bf16[896,512]{1,0:T(8,128)(2,1)S(1)} %collective-permute-done.19.refs_2_.refs_5_), channel_id=1, source_target_pairs={{0,4},{4,0},{8,12},{12,8},{16,20},{20,16},{24,28},{28,24},{32,36},... | collective-permute-start | bytes 2752520 | tf_op jit(solution)/shard_map/ppermute | solution.py:65
  91.0 16.6 %collective-permute-start.27 = (bf16[896,512]{1,0:T(8,128)(2,1)S(1)}, bf16[896,512]{1,0:T(8,128)(2,1)S(1)}, u32[]{:S(2)}, u32[]{:S(2)}) collective-permute-start(bf16[896,512]{1,0:T(8,128)(2,1)S(1)} %collective-permute-done.24.refs_2_.refs_8_), channel_id=1, source_target_pairs={{0,4},{4,0},{8,12},{12,8},{16,20},{20,16},{24,28},{28,24},{32,36},... | collective-permute-start | bytes 2752520 | tf_op jit(solution)/shard_map/ppermute | solution.py:65
  95.4 10.2 %collective-permute-start.15 = (bf16[672,512]{1,0:T(8,128)(2,1)S(1)}, bf16[672,512]{1,0:T(8,128)(2,1)S(1)}, u32[]{:S(2)}, u32[]{:S(2)}) collective-permute-start(bf16[672,512]{1,0:T(8,128)(2,1)S(1)} %collective-permute-done.14.refs_4_), channel_id=1, source_target_pairs={{0,96},{4,28},{8,104},{12,4},{16,112},{20,12},{24,120},{28,20},{32... | collective-permute-start | bytes 2064392 | tf_op jit(solution)/shard_map/ppermute | solution.py:65
  98.3 17.1 %collective-permute-start.22 = (bf16[896,512]{1,0:T(8,128)(2,1)S(1)}, bf16[896,512]{1,0:T(8,128)(2,1)S(1)}, u32[]{:S(2)}, u32[]{:S(2)}) collective-permute-start(bf16[896,512]{1,0:T(8,128)(2,1)S(1)} %collective-permute-done.20.refs_2_.refs_11_), channel_id=1, source_target_pairs={{0,4},{4,0},{8,12},{12,8},{16,20},{20,16},{24,28},{28,24},{32,36},... | collective-permute-start | bytes 2752520 | tf_op jit(solution)/shard_map/ppermute | solution.py:65
  102.6 12.7 %collective-permute-start.13 = (bf16[224,1536]{1,0:T(8,128)(2,1)S(1)}, bf16[224,1536]{1,0:T(8,128)(2,1)S(1)}, u32[]{:S(2)}, u32[]{:S(2)}) collective-permute-start(bf16[224,1536]{1,0:T(8,128)(2,1)S(1)} %collective-permute-done.12.refs_0_.refs_2_.refs_9_), channel_id=1, source_target_pairs={{0,4},{4,0},{8,12},{12,8},{16,20},{20,16},{24,28},{28,24},{32,36},... | collective-permute-start | bytes 2064392 | tf_op jit(solution)/shard_map/ppermute | solution.py:65
  105.5 15.4 %collective-permute-start.10 = (bf16[672,512]{1,0:T(8,128)(2,1)S(1)}, bf16[672,512]{1,0:T(8,128)(2,1)S(1)}, u32[]{:S(2)}, u32[]{:S(2)}) collective-permute-start(bf16[672,512]{1,0:T(8,128)(2,1)S(1)} %collective-permute-done.9.refs_1_), channel_id=1, source_target_pairs={{0,4},{4,0},{8,12},{12,8},{16,20},{20,16},{24,28},{28,24},{32,36},... | collective-permute-start | bytes 2064392 | tf_op jit(solution)/shard_map/ppermute | solution.py:65
  107.6 13.4 %collective-permute-start.16 = (bf16[672,512]{1,0:T(8,128)(2,1)S(1)}, bf16[672,512]{1,0:T(8,128)(2,1)S(1)}, u32[]{:S(2)}, u32[]{:S(2)}) collective-permute-start(bf16[672,512]{1,0:T(8,128)(2,1)S(1)} %collective-permute-done.15.refs_3_), channel_id=1, source_target_pairs={{0,4},{4,0},{8,12},{12,8},{16,20},{20,16},{24,28},{28,24},{32,36},... | collective-permute-start | bytes 2064392 | tf_op jit(solution)/shard_map/ppermute | solution.py:65
  (16 other events, 107.3 us)
